TPU v7x, 32 devices: a whole 2x2x4 slice. The times are simulated.
32 devices in a mesh: ep: 4 (over z), dp: 8 (over y, x, core).
Axes of the slice: x: 2, y: 2, z: 4, core: 2. Of those that a mesh axis runs over, the one named last changes fastest.
Arguments:
- act_in: bfloat16 [65536, 640], P(('ep', 'dp'))
- grad_out: bfloat16 [65536, 640], P(('ep', 'dp'))
- slot_ids: int32 [2, 65536, 1], P(None, ('ep', 'dp'))
- gate_vals: float32 [2, 65536, 1], P(None, ('ep', 'dp'))
- w_dense: bfloat16 [2, 640, 640], replicated
- w_gate: bfloat16 [2, 16, 640, 1024], P(None, 'ep')
- w_up: bfloat16 [2, 16, 640, 1024], P(None, 'ep')
- w_down: bfloat16 [2, 16, 1024, 640], P(None, 'ep')
- ws_gate: bfloat16 [2, 640, 1024], replicated
- ws_up: bfloat16 [2, 640, 1024], replicated
- ws_down: bfloat16 [2, 1024, 640], replicated
Outputs:
- output 1: bfloat16 [65536, 640], P(('ep', 'dp'))
- output 2: bfloat16 [2, 640, 640], replicated
- output 3: bfloat16 [2, 16, 640, 1024], P(None, 'ep')
- output 4: bfloat16 [2, 16, 640, 1024], P(None, 'ep')
- output 5: bfloat16 [2, 16, 1024, 640], P(None, 'ep')
- output 6: bfloat16 [2, 640, 1024], replicated
- output 7: bfloat16 [2, 640, 1024], replicated
- output 8: bfloat16 [2, 1024, 640], replicated
All inputs are finite; a program needn't handle non-finite values.
Results may differ from a plain program's by a relative error of at most 0.02.
Values are sent between devices in bfloat16 or wider.
A program may use at most 1 GiB of HBM per device.

v0:
```python
import jax
import jax.numpy as jnp
from jax import lax
from jax.sharding import PartitionSpec as P

ALL_AXES = ("ep", "dp")


def silu_grad(pre_act):
    sigma = jax.nn.sigmoid(pre_act)
    return sigma * (1.0 + pre_act * (1.0 - sigma))


def contract_rows(left, right):
    return lax.dot_general(left, right, (((0,), (0,)), ((), ())), preferred_element_type=jnp.float32)


def contract_cols(left, right):
    return lax.dot_general(left, right, (((1,), (1,)), ((), ())), preferred_element_type=jnp.float32)


def layer_front(act, weights, slot_ids, ep_size):
    w_dense, w_gate, w_up, w_down, ws_gate, ws_up, ws_down = weights
    tokens, width = act.shape
    top = slot_ids.shape[1]
    local_exp = w_gate.shape[0]
    capacity = 2 * tokens * top // (local_exp * ep_size)
    dense_pre = jnp.dot(act, w_dense, preferred_element_type=jnp.float32)
    mixed = (act.astype(jnp.float32) + dense_pre).astype(jnp.bfloat16)
    slot_flat = slot_ids.reshape(tokens * top)
    copy_ids = jnp.arange(1, tokens * top + 1, dtype=jnp.int32)
    slot_owner = jnp.zeros((local_exp * ep_size * capacity,), jnp.int32).at[slot_flat].set(copy_ids)
    tok_owner = (slot_owner + top - 1) // top
    mixed_ext = jnp.concatenate([jnp.zeros((1, width), mixed.dtype), mixed], axis=0)
    send_buf = jnp.take(mixed_ext, tok_owner, axis=0).reshape(ep_size, local_exp, capacity, width)
    recv_rows = lax.all_to_all(send_buf, "ep", 0, 1).reshape(local_exp, ep_size * capacity, width)
    a_one = jnp.einsum("erd,edf->erf", recv_rows, w_gate, preferred_element_type=jnp.float32)
    a_three = jnp.einsum("erd,edf->erf", recv_rows, w_up, preferred_element_type=jnp.float32)
    hidden = (jax.nn.silu(a_one) * a_three).astype(jnp.bfloat16)
    s_one = jnp.dot(mixed, ws_gate, preferred_element_type=jnp.float32)
    s_three = jnp.dot(mixed, ws_up, preferred_element_type=jnp.float32)
    shared_hidden = (jax.nn.silu(s_one) * s_three).astype(jnp.bfloat16)
    return (act, mixed, slot_flat, slot_owner, recv_rows, a_one, a_three, hidden, s_one, s_three, shared_hidden)


def layer_finish(saved, weights, gate_vals, ep_size):
    act, mixed, slot_flat, slot_owner, recv_rows, a_one, a_three, hidden, s_one, s_three, shared_hidden = saved
    w_down = weights[3]
    ws_down = weights[6]
    tokens, width = mixed.shape
    top = gate_vals.shape[1]
    local_exp = hidden.shape[0]
    capacity = recv_rows.shape[1] // ep_size
    exp_out = jnp.einsum("erf,efd->erd", hidden, w_down, preferred_element_type=jnp.float32).astype(jnp.bfloat16)
    back_rows = lax.all_to_all(exp_out.reshape(local_exp, ep_size, capacity, width), "ep", 1, 0).reshape(local_exp * ep_size * capacity, width)
    picked = jnp.take(back_rows, slot_flat, axis=0).reshape(tokens, top, width)
    routed = jnp.sum(gate_vals[:, :, None] * picked.astype(jnp.float32), axis=1)
    shared_out = jnp.dot(shared_hidden, ws_down, preferred_element_type=jnp.float32)
    return (mixed.astype(jnp.float32) + routed + shared_out).astype(jnp.bfloat16)


def layer_backward(grad_y, saved, weights, gate_vals, ep_size):
    act, mixed, slot_flat, slot_owner, recv_rows, a_one, a_three, hidden, s_one, s_three, shared_hidden = saved
    w_dense, w_gate, w_up, w_down, ws_gate, ws_up, ws_down = weights
    tokens, width = grad_y.shape
    top = gate_vals.shape[1]
    local_exp = hidden.shape[0]
    capacity = recv_rows.shape[1] // ep_size
    grad_y32 = grad_y.astype(jnp.float32)
    grad_pick = (gate_vals[:, :, None] * grad_y32[:, None, :]).astype(jnp.bfloat16).reshape(tokens * top, width)
    grad_ext = jnp.concatenate([jnp.zeros((1, width), grad_pick.dtype), grad_pick], axis=0)
    send_grad = jnp.take(grad_ext, slot_owner, axis=0).reshape(ep_size, local_exp, capacity, width)
    grad_exp_out = lax.all_to_all(send_grad, "ep", 0, 1).reshape(local_exp, ep_size * capacity, width)
    g_w_down = jnp.einsum("erf,erd->efd", hidden, grad_exp_out, preferred_element_type=jnp.float32)
    grad_hidden = jnp.einsum("erd,efd->erf", grad_exp_out, w_down, preferred_element_type=jnp.float32)
    grad_a_one = (grad_hidden * a_three * silu_grad(a_one)).astype(jnp.bfloat16)
    grad_a_three = (grad_hidden * jax.nn.silu(a_one)).astype(jnp.bfloat16)
    g_w_gate = jnp.einsum("erd,erf->edf", recv_rows, grad_a_one, preferred_element_type=jnp.float32)
    g_w_up = jnp.einsum("erd,erf->edf", recv_rows, grad_a_three, preferred_element_type=jnp.float32)
    grad_rows = (jnp.einsum("erf,edf->erd", grad_a_one, w_gate, preferred_element_type=jnp.float32) + jnp.einsum("erf,edf->erd", grad_a_three, w_up, preferred_element_type=jnp.float32)).astype(jnp.bfloat16)
    grad_back = lax.all_to_all(grad_rows.reshape(local_exp, ep_size, capacity, width), "ep", 1, 0).reshape(local_exp * ep_size * capacity, width)
    grad_routed = jnp.sum(jnp.take(grad_back, slot_flat, axis=0).reshape(tokens, top, width).astype(jnp.float32), axis=1)
    g_ws_down = contract_rows(shared_hidden, grad_y)
    grad_shared = contract_cols(grad_y, ws_down)
    grad_s_one = (grad_shared * s_three * silu_grad(s_one)).astype(jnp.bfloat16)
    grad_s_three = (grad_shared * jax.nn.silu(s_one)).astype(jnp.bfloat16)
    g_ws_gate = contract_rows(mixed, grad_s_one)
    g_ws_up = contract_rows(mixed, grad_s_three)
    grad_mixed = (grad_y32 + grad_routed + contract_cols(grad_s_one, ws_gate) + contract_cols(grad_s_three, ws_up)).astype(jnp.bfloat16)
    g_w_dense = contract_rows(act, grad_mixed)
    grad_act = (grad_mixed.astype(jnp.float32) + contract_cols(grad_mixed, w_dense)).astype(jnp.bfloat16)
    dense_grads = (g_w_dense.astype(jnp.bfloat16), g_ws_gate.astype(jnp.bfloat16), g_ws_up.astype(jnp.bfloat16), g_ws_down.astype(jnp.bfloat16))
    expert_grads = (g_w_gate.astype(jnp.bfloat16), g_w_up.astype(jnp.bfloat16), g_w_down.astype(jnp.bfloat16))
    return grad_act, dense_grads, expert_grads


def solution(mesh):
    ep_size = mesh.shape["ep"]
    tok_spec = P(ALL_AXES, None)
    route_spec = P(None, ALL_AXES, None)
    exp_spec = P(None, "ep", None, None)
    repl_spec = P(None, None, None)

    def body(act_in, grad_out, slot_ids, gate_vals, w_dense, w_gate, w_up, w_down, ws_gate, ws_up, ws_down):
        layers = w_dense.shape[0]
        all_weights = [(w_dense[layer], w_gate[layer], w_up[layer], w_down[layer], ws_gate[layer], ws_up[layer], ws_down[layer]) for layer in range(layers)]
        saved_all = []
        act = act_in
        for layer in range(layers):
            saved = layer_front(act, all_weights[layer], slot_ids[layer], ep_size)
            saved_all.append(saved)
            if layer + 1 < layers:
                act = layer_finish(saved, all_weights[layer], gate_vals[layer], ep_size)
        grad_act = grad_out
        dense_sums = [None] * layers
        expert_sums = [None] * layers
        for layer in reversed(range(layers)):
            grad_act, dense_grads, expert_grads = layer_backward(grad_act, saved_all[layer], all_weights[layer], gate_vals[layer], ep_size)
            dense_sums[layer] = [lax.psum(part, ALL_AXES) for part in dense_grads]
            expert_sums[layer] = [lax.psum(part, "dp") for part in expert_grads]
        dense_out = [jnp.stack([dense_sums[layer][which] for layer in range(layers)]) for which in range(4)]
        expert_out = [jnp.stack([expert_sums[layer][which] for layer in range(layers)]) for which in range(3)]
        return (grad_act, dense_out[0], expert_out[0], expert_out[1], expert_out[2], dense_out[1], dense_out[2], dense_out[3])

    return jax.shard_map(body, mesh=mesh, in_specs=(tok_spec, tok_spec, route_spec, route_spec, repl_spec, exp_spec, exp_spec, exp_spec, repl_spec, repl_spec, repl_spec), out_specs=(tok_spec, repl_spec, exp_spec, exp_spec, exp_spec, repl_spec, repl_spec, repl_spec), check_vma=False)
```

profile of v0, /device:TPU:0, one launch (start us, length us, event | category | flops | bytes accessed | tf_op | source)
XLA Modules:
  0.0 1778.2 jit_solution(14945748476125738342)
XLA Ops:
  7.9 8.1 scatter_custom_fusion.1
  16.0 5.3 add_convert_fusion.6
  23.5 17.6 gather_fusion.1
  41.1 4.4 broadcast_select_fusion.1
  45.5 122.3 %all_to_all.105 = bf16[4,4,1,256,640]{4,3,1,2,0:T(8,128)(2,1)S(1)} all-to-all(bf16[4,4,1,256,640]{4,3,1,2,0:T(8,128)(2,1)S(1)} %bitcast.228), channel_id=1, replica_groups=mesh['ep'=4,'dp'=8] {'ep'}, dimensions={0} | all-to-all | bytes 10485760 | tf_op jit(solution)/shard_map/all_to_all | solution.py:36
  170.7 9.6 fusion.31
  180.4 18.7 %multiply_convert_fusion.5 = (bf16[4,1024,1024]{2,1,0:T(8,128)(2,1)}, f32[4,1024,1024]{2,1,0:T(8,128)}) fusion(f32[4,1024,1024]{2,1,0:T(8,128)} %fusion.31, bf16[4,1024,640]{2,1,0:T(8,128)(2,1)} %bitcast.233, bf16[2,4,640,1024]{3,2,1,0:T(8,128)(2,1)} %param.21), kind=kOutput, calls=%fused_computation.16 | convolution fusion | flops 5393874944 | bytes 52428800 | tf_op jit(solution)/shard_map/erd,edf->erf/dot_general | solution.py:38
  199.0 10.6 fusion.47
  212.5 5.3 all-to-all-start.2
  217.8 8.1 scatter_custom_fusion
  227.1 18.2 %gather_fusion = bf16[4096,640]{1,0:T(8,128)(2,1)} fusion(bf16[2049,640]{1,0:T(8,128)(2,1)S(1)} %concatenate.12, s32[4096]{0:T(1024)S(1)} %fusion.103), kind=kCustom, calls=%fused_computation.clone | custom fusion | bytes 10502144 | tf_op jit(solution)/shard_map/jit(_take)/gather | solution.py:72
  246.0 5.8 fusion.80
  255.2 7.5 multiply_convert_fusion.12
  262.7 69.5 %all-to-all-done.2 = bf16[1,4,4,256,640]{4,3,1,0,2:T(8,128)(2,1)} async-done(((bf16[1,4,4,256,640]{4,3,1,0,2:T(8,128)(2,1)}), bf16[1,4,4,256,640]{4,3,1,0,2:T(8,128)(2,1)}, u32[]{:S(2)}, u32[]{:S(2)}) %all-to-all-start.2) | async-done | bytes 5242912 | tf_op jit(solution)/shard_map/all_to_all | solution.py:55
  332.2 12.7 gather_fusion.2
  344.9 6.2 add_convert_fusion.5
  356.0 17.6 gather_fusion.3
  373.6 8.1 broadcast_select_fusion.3
  381.7 118.6 %all_to_all.106 = bf16[4,4,1,256,640]{4,3,1,2,0:T(8,128)(2,1)} all-to-all(bf16[4,4,1,256,640]{4,3,1,2,0:T(8,128)(2,1)S(1)} %bitcast.231), channel_id=1, replica_groups=mesh['ep'=4,'dp'=8] {'ep'}, dimensions={0} | all-to-all | bytes 10485760 | tf_op jit(solution)/shard_map/all_to_all | solution.py:36
  500.3 5.2 all-to-all-start
  508.7 14.0 fusion.15
  522.8 9.7 fusion.19
  532.4 87.6 %all-to-all-done = bf16[4,4,1,256,640]{4,3,1,2,0:T(8,128)(2,1)} async-done(((bf16[4,4,1,256,640]{4,3,1,2,0:T(8,128)(2,1)}), bf16[4,4,1,256,640]{4,3,1,2,0:T(8,128)(2,1)}, u32[]{:S(2)}, u32[]{:S(2)}) %all-to-all-start) | async-done | bytes 5242912 | tf_op jit(solution)/shard_map/all_to_all | solution.py:73
  620.0 5.5 copy.50
  625.5 24.8 %multiply_convert_fusion.3 = (bf16[4,1024,1024]{2,1,0:T(8,128)(2,1)}, bf16[4,1024,1024]{2,1,0:T(8,128)(2,1)}) fusion(f32[4,1024,1024]{2,1,0:T(8,128)} %fusion.15, f32[4,1024,1024]{2,1,0:T(8,128)} %fusion.19, bf16[4,1024,640]{2,1,0:T(8,128)(2,1)} %bitcast.244, bf16[2,4,1024,640]{3,2,1,0:T(8,128)(2,1)} %param.22), kind=kOutput, calls=%fused_computation.12 | convolution fusion | flops 5423235072 | bytes 60817408 | tf_op jit(solution)/shard_map/erd,efd->erf/dot_general | solution.py:75
  650.3 13.0 fusion.13
  663.3 12.2 add_convert_fusion.1
  678.4 5.5 all-to-all-start.4
  684.0 4.9 fusion.65
  688.9 6.2 fusion.68
  696.1 11.5 multiply_convert_fusion.10
  707.7 7.9 fusion.63
  715.6 83.2 %all-to-all-done.4 = bf16[1,4,4,256,640]{4,3,1,0,2:T(8,128)(2,1)} async-done(((bf16[1,4,4,256,640]{4,3,1,0,2:T(8,128)(2,1)}), bf16[1,4,4,256,640]{4,3,1,0,2:T(8,128)(2,1)}, u32[]{:S(2)}, u32[]{:S(2)}) %all-to-all-start.4) | async-done | bytes 5242912 | tf_op jit(solution)/shard_map/all_to_all | solution.py:81
  798.8 13.1 gather_fusion.4
  811.9 9.0 fusion.8
  825.4 17.6 gather_fusion.5
  843.1 6.9 broadcast_select_fusion
  849.9 5.5 all-to-all-start.5
  855.5 6.4 fusion.61
  866.5 5.3 fusion.57
  871.7 19.4 %convert_bitcast_fusion = bf16[1,4,1024,640]{3,2,1,0:T(8,128)(2,1)} fusion(bf16[4,1024,640]{2,1,0:T(8,128)(2,1)} %bitcast.245, f32[4,1024,1024]{2,1,0:T(8,128)} %fusion.19, f32[4,1024,1024]{2,1,0:T(8,128)} %fusion.15), kind=kOutput, calls=%fused_computation.69 | convolution fusion | flops 5396496384 | bytes 44040192 | tf_op jit(solution)/shard_map/erf,erd->efd/dot_general | solution.py:74
  891.1 79.2 %all-to-all-done.5 = bf16[4,4,1,256,640]{4,3,1,2,0:T(8,128)(2,1)} async-done(((bf16[4,4,1,256,640]{4,3,1,2,0:T(8,128)(2,1)}), bf16[4,4,1,256,640]{4,3,1,2,0:T(8,128)(2,1)}, u32[]{:S(2)}, u32[]{:S(2)}) %all-to-all-start.5) | async-done | bytes 5242912 | tf_op jit(solution)/shard_map/all_to_all | solution.py:73
  970.3 5.4 copy.58
  975.7 24.8 %multiply_convert_fusion.2 = (bf16[4,1024,1024]{2,1,0:T(8,128)(2,1)}, bf16[4,1024,1024]{2,1,0:T(8,128)(2,1)}) fusion(f32[4,1024,1024]{2,1,0:T(8,128)} %fusion.31, f32[4,1024,1024]{2,1,0:T(8,128)} %get-tuple-element.67, bf16[4,1024,640]{2,1,0:T(8,128)(2,1)} %bitcast.242, bf16[2,4,1024,640]{3,2,1,0:T(8,128)(2,1)} %param.22), kind=kOutput, calls=%fused_computation.11 | convolution fusion | flops 5423235072 | bytes 60817408 | tf_op jit(solution)/shard_map/erd,efd->erf/dot_general | solution.py:75
  1000.6 13.1 fusion.25
  1013.6 12.7 add_convert_fusion
  1029.1 5.1 all-to-all-start.6
  1034.2 11.3 convert_bitcast_fusion.2
  1045.5 11.4 convert_bitcast_fusion.4
  1056.9 5.1 fusion.84
  1062.1 10.7 multiply_convert_fusion.8
  1072.8 5.3 fusion.78
  1078.1 4.7 fusion.62
  1090.8 58.3 %all-to-all-done.6 = bf16[1,4,4,256,640]{4,3,1,0,2:T(8,128)(2,1)} async-done(((bf16[1,4,4,256,640]{4,3,1,0,2:T(8,128)(2,1)}), bf16[1,4,4,256,640]{4,3,1,0,2:T(8,128)(2,1)}, u32[]{:S(2)}, u32[]{:S(2)}) %all-to-all-start.6) | async-done | bytes 5242912 | tf_op jit(solution)/shard_map/all_to_all | solution.py:81
  1149.1 11.1 gather_fusion.6
  1160.3 9.0 fusion.12
  1174.0 12.6 convert_bitcast_fusion.1
  1186.6 11.2 convert_bitcast_fusion.5
  1197.9 7.6 convert_bitcast_fusion.3
  1206.9 6.5 add_convert_fusion.2
  1213.4 152.6 %all-reduce.9.cloned.1.call-done = (bf16[1,640,640]{1,2,0:T(8,128)(2,1)}, bf16[1,640,640]{1,2,0:T(8,128)(2,1)}, bf16[1,640,1024]{2,1,0:T(8,128)(2,1)}, bf16[1,64...) async-done(((bf16[1,640,640]{1,2,0:T(8,128)(2,1)}, ...) | async-done | bytes 9502736 | tf_op jit(solution)/shard_map/psum | solution.py:119
  1376.4 369.4 %all-reduce.11.cloned.1.call-done = (bf16[1,4,640,1024]{3,2,1,0:T(8,128)(2,1)}, bf16[1,4,640,1024]{3,2,1,0:T(8,128)(2,1)}, bf16[1,4,640,1024]{3,2,1,0:T(8,128)(2...) async-done(((bf16[1,4,640,1024]{3,2,1,0:T(8,128)(2,1)}, bf16[1,4,640,1024]{3,2,1,0:T(8,128)(2,1)}, ...) | async-done | bytes 31457296 | tf_op jit(solution)/shard_map/psum | solution.py:120
  1745.8 9.2 pad_maximum_fusion.2
  1755.0 15.8 pad_maximum_fusion
  (173 shorter events, 62.3 us)
Async XLA Ops:
  16.0 25.1 %copy-start.22 = (pred[4096]{0:T(1024)(128)(4,1)}, pred[4096]{0:T(1024)(128)(4,1)S(1)}, u32[]{:S(2)}) copy-start(pred[4096]{0:T(1024)(128)(4,1)S(1)} %compare_and_fusion) | copy-start | bytes 12292
  16.0 7.5 copy-start.16
  45.5 125.2 %slice-start.5 = ((s8[10485760]{0:T(1024)(128)(4,1)}), s8[4194304]{0:T(1024)(128)(4,1)S(1)}, s32[]{:S(2)}) async-start(s8[10485760]{0:T(1024)(128)(4,1)} %bitcast.260), calls=%async_computation.14 | async-start | bytes 8388608
  45.5 125.2 %slice-start.6 = ((s8[10485760]{0:T(1024)(128)(4,1)}), s8[4194304]{0:T(1024)(128)(4,1)S(1)}, s32[]{:S(2)}) async-start(s8[10485760]{0:T(1024)(128)(4,1)} %bitcast.260), calls=%async_computation.15 | async-start | bytes 8388608
  212.5 13.4 copy-start.24
  212.5 13.4 copy-start.2
  212.5 119.7 %all-to-all-start.2 = ((bf16[1,4,4,256,640]{4,3,1,0,2:T(8,128)(2,1)}), bf16[1,4,4,256,640]{4,3,1,0,2:T(8,128)(2,1)}, u32[]{:S(2)}, u32[]{:S(2)}) async-start(bf16[1,4,4,256,640]{4,3,1,0,2:T(8,128)(2,1)} %copy.53), calls=%async_computation.2 | async-start | bytes 10485760 | tf_op jit(solution)/shard_map/all_to_all | solution.py:55
  225.9 119.0 %copy-start.25 = (f32[1,2048,1]{1,2,0:T(1,128)}, f32[1,2048,1]{1,2,0:T(1,128)S(1)}, u32[]{:S(2)}) copy-start(f32[1,2048,1]{1,2,0:T(1,128)S(1)} %get-tuple-element.59) | copy-start | bytes 24580
  227.1 18.2 %copy-start.21 = (s32[2,2048,1]{1,2,0:T(1,128)S(1)}, s32[2,2048,1]{1,2,0:T(1,128)}, u32[]{:S(2)}) copy-start(s32[2,2048,1]{1,2,0:T(1,128)} %param.17) | copy-start | bytes 49156
  245.9 99.0 %copy-start.27 = (pred[2048]{0:T(1024)(128)(4,1)}, pred[2048]{0:T(1024)(128)(4,1)S(1)}, u32[]{:S(2)}) copy-start(pred[2048]{0:T(1024)(128)(4,1)S(1)} %compare_and_fusion.3) | copy-start | bytes 6148
  245.9 86.3 %copy-start.18 = (s32[2048]{0:T(1024)}, s32[2048]{0:T(1024)S(1)}, u32[]{:S(2)}) copy-start(s32[2048]{0:T(1024)S(1)} %fusion.109) | copy-start | bytes 24580
  246.0 9.2 copy-start.6
  246.0 9.2 copy-start.33
  251.8 3.4 copy-start.42
  344.9 6.3 copy-start.36
  500.3 119.6 %all-to-all-start = ((bf16[4,4,1,256,640]{4,3,1,2,0:T(8,128)(2,1)}), bf16[4,4,1,256,640]{4,3,1,2,0:T(8,128)(2,1)}, u32[]{:S(2)}, u32[]{:S(2)}) async-start(bf16[4,4,1,256,640]{4,3,1,2,0:T(8,128)(2,1)} %bitcast.230), calls=%async_computation | async-start | bytes 10485760 | tf_op jit(solution)/shard_map/all_to_all | solution.py:73
  505.6 17.2 slice-start.2
  508.7 14.1 copy-start.1
  508.7 14.0 slice-start.3
  508.7 14.0 slice-start.4
  678.4 5.5 copy-start.20
  678.4 5.6 copy-start.9
  678.4 120.4 %all-to-all-start.4 = ((bf16[1,4,4,256,640]{4,3,1,0,2:T(8,128)(2,1)}), bf16[1,4,4,256,640]{4,3,1,0,2:T(8,128)(2,1)}, u32[]{:S(2)}, u32[]{:S(2)}) async-start(bf16[1,4,4,256,640]{4,3,1,0,2:T(8,128)(2,1)} %copy.56), calls=%async_computation.4 | async-start | bytes 10485760 | tf_op jit(solution)/shard_map/all_to_all | solution.py:81
  683.9 5.0 copy-start.10
  683.9 5.0 copy-start.34
  688.9 7.2 copy-start.43
  688.9 7.2 copy-start.3
  688.9 7.2 copy-start.29
  696.1 11.5 copy-start.31
  811.9 9.0 copy-start.26
  811.9 9.0 copy-start.37
  820.9 3.8 copy-start.48
  825.4 17.6 copy-start.23
  849.9 5.5 copy-start.11
  849.9 120.4 %all-to-all-start.5 = ((bf16[4,4,1,256,640]{4,3,1,2,0:T(8,128)(2,1)}), bf16[4,4,1,256,640]{4,3,1,2,0:T(8,128)(2,1)}, u32[]{:S(2)}, u32[]{:S(2)}) async-start(bf16[4,4,1,256,640]{4,3,1,2,0:T(8,128)(2,1)} %bitcast.226), calls=%async_computation.5 | async-start | bytes 10485760 | tf_op jit(solution)/shard_map/all_to_all | solution.py:73
  855.4 6.4 copy-start.44
  855.4 10.4 slice-start.10
  855.4 10.4 slice-start.12
  861.8 4.0 copy-start.4
  861.8 4.0 slice-start.11
  861.8 4.6 slice-start.13
  1029.1 120.0 %all-to-all-start.6 = ((bf16[1,4,4,256,640]{4,3,1,0,2:T(8,128)(2,1)}), bf16[1,4,4,256,640]{4,3,1,0,2:T(8,128)(2,1)}, u32[]{:S(2)}, u32[]{:S(2)}) async-start(bf16[1,4,4,256,640]{4,3,1,0,2:T(8,128)(2,1)} %copy.59), calls=%async_computation.6 | async-start | bytes 10485760 | tf_op jit(solution)/shard_map/all_to_all | solution.py:81
  1034.2 331.8 %all-reduce.9.cloned.1.call-start = ((), (), s32[]{:S(2)}) async-start(), calls=%async_computation.7 | async-start | bytes 19005440 | tf_op jit(solution)/shard_map/psum | solution.py:119
  1034.2 27.8 %slice-start.8 = ((s8[8388608]{0:T(1024)(128)(4,1)}), s8[4194304]{0:T(1024)(128)(4,1)S(1)}, s32[]{:S(2)}) async-start(s8[8388608]{0:T(1024)(128)(4,1)} %bitcast.262), calls=%async_computation.17 | async-start | bytes 8388608
  1045.5 11.4 copy-start.47
  1045.5 16.5 slice-start.9
  1056.9 5.1 copy-start.30
  1056.9 5.1 copy-start.41
  1062.1 10.8 copy-start.32
  1072.8 5.3 copy-start.40
  1078.1 4.7 copy-start.7
  1082.8 4.0 copy-start.45
  1086.8 62.3 %copy-start.19 = (s32[2048]{0:T(1024)S(1)}, s32[2048]{0:T(1024)}, u32[]{:S(2)}) copy-start(s32[2048]{0:T(1024)} %copy-done.18) | copy-start | bytes 24580
  1149.1 11.1 copy-start.28
  1160.2 10.5 copy-start.35
  1173.9 571.9 %all-reduce.11.cloned.1.call-start = ((), (), s32[]{:S(2)}) async-start(), calls=%async_computation.8 | async-start | bytes 62914560 | tf_op jit(solution)/shard_map/psum | solution.py:120
  1174.0 23.9 %slice-start = ((s8[5242880]{0:T(1024)(128)(4,1)}), s8[4194304]{0:T(1024)(128)(4,1)S(1)}, s32[]{:S(2)}) async-start(s8[5242880]{0:T(1024)(128)(4,1)} %bitcast.235), calls=%async_computation.9 | async-start | bytes 8388608
  1174.0 23.9 %slice-start.14 = ((s8[8388608]{0:T(1024)(128)(4,1)}), s8[4194304]{0:T(1024)(128)(4,1)S(1)}, s32[]{:S(2)}) async-start(s8[8388608]{0:T(1024)(128)(4,1)} %bitcast.268), calls=%async_computation.23 | async-start | bytes 8388608
  1186.6 11.3 slice-start.1
  1186.6 11.3 slice-start.15
  1366.0 7.8 copy-start.12
  1370.1 3.6 copy-start.13
  1370.1 3.6 copy-start.14
  1370.1 3.6 copy-start.15
  (8 other events, 14.6 us)
Sparse Core Ops, SparseCore 0:
  1174.0 191.8 all-reduce.8
  1371.4 374.3 all-reduce.10
where the time goes:
time: 1780 us
  waiting for transfers between devices  900 us (51%)
  matrix products  376 us (21%)
  blocking collectives  241 us (14%)
  local copies, waits for them, and re-layouts  166 us (9%)
  other arithmetic  53.7 us (3%)
  starting transfers between devices  26.6 us (1%)
    psum x1, waiting for transfers between devices, body(): expert_sums[layer] = [lax.psum(part, 'dp') for part in expert_grads]  369 us
    all_to_all x2, blocking collectives, layer_front(): lax.all_to_all(send_buf, 'ep', 0, 1)  241 us
    all_to_all x2, waiting for transfers between devices, layer_backward(): lax.all_to_all(send_grad, 'ep', 0, 1)  167 us
    psum x1, waiting for transfers between devices, body(): dense_sums[layer] = [lax.psum(part, ALL_AXES) for part in dense_grads]  153 us
    all_to_all x2, waiting for transfers between devices, layer_backward(): lax.all_to_all(grad_rows.reshape(local_exp, ep_size, capacity, width), 'e...  141 us
    all_to_all x1, waiting for transfers between devices, layer_finish(): lax.all_to_all(exp_out.reshape(local_exp, ep_size, capacity, width), 'ep'...  69.5 us
    dot_general x8, matrix products, contract_cols(): lax.dot_general(left, right, (((1,), (1,)), ((), ())), preferred_element_...  63.8 us
    dot_general x2, matrix products, layer_backward(): jnp.einsum('erd,efd->erf', grad_exp_out, w_down, preferred_element_type=j...  49.6 us
  transfers between devices with their start and end apart: 7, of which 7 were waited for; matrix products, arithmetic and copies ran while one was open for 13% of the time, Pallas kernels for 0%

commit v1 on v0

v1 whole, which is shorter than its diff:
```python
import jax
import jax.numpy as jnp
from jax import lax
from jax.sharding import PartitionSpec as P

ALL_AXES = ("ep", "dp")


def silu_grad(pre_act):
    sigma = jax.nn.sigmoid(pre_act)
    return sigma * (1.0 + pre_act * (1.0 - sigma))


def contract_rows(left, right):
    return lax.dot_general(left, right, (((0,), (0,)), ((), ())), preferred_element_type=jnp.float32)


def contract_cols(left, right):
    return lax.dot_general(left, right, (((1,), (1,)), ((), ())), preferred_element_type=jnp.float32)


def dot32(left, right):
    return jnp.dot(left, right, preferred_element_type=jnp.float32)


class Place:
    def __init__(self, mesh):
        self.ep, self.dp = mesh.shape["ep"], mesh.shape["dp"]
        self.half_ep = self.ep // 2
        self.group = self.half_ep * self.dp
        self.z = lax.axis_index("ep")
        self.j = lax.axis_index("dp")
        self.core = self.j % 2
        self.chip = self.j // 2
        self.half = self.z // self.half_ep
        self.groups = [[g * self.group + m for m in range(self.group)] for g in range(2)]
        every = range(self.ep * self.dp)
        self.swap_z = [(d, (d + self.group) % (2 * self.group)) for d in every]
        self.swap_core = [(d, d ^ 1) for d in every]

    def exchange(self, rows):
        blocks = rows.reshape(self.group, rows.shape[0] // self.group, rows.shape[1])
        return lax.all_to_all(blocks, ALL_AXES, 0, 0, axis_index_groups=self.groups).reshape(rows.shape)

    def to_partner(self, value):
        return lax.ppermute(value, ALL_AXES, self.swap_z)

    def to_sibling(self, value):
        return lax.ppermute(value, ALL_AXES, self.swap_core)

    def my_half(self, value, core):
        size = value.shape[0] // 2
        return lax.dynamic_slice_in_dim(value, core * size, size, axis=0)


def foreign_weight(place, own):
    got = place.to_partner(place.my_half(own, place.core))
    other = place.to_sibling(got)
    low = jnp.where(place.core == 0, got, other)
    high = jnp.where(place.core == 0, other, got)
    return jnp.concatenate([low, high], axis=0)


def take_rows(source, index):
    return jnp.take(source, index, axis=0, mode="clip")


def with_zero_row(rows):
    return jnp.pad(rows, ((0, 8), (0, 0)))


def ffn_front(rows, w_one, w_three):
    a_one = dot32(rows, w_one)
    a_three = dot32(rows, w_three)
    hidden = (jax.nn.silu(a_one) * a_three).astype(jnp.bfloat16)
    return a_one, a_three, hidden


def ffn_back(grad_out, front, w_two):
    a_one, a_three, _ = front
    grad_hidden = contract_cols(grad_out, w_two)
    grad_one = (grad_hidden * a_three * silu_grad(a_one)).astype(jnp.bfloat16)
    grad_three = (grad_hidden * jax.nn.silu(a_one)).astype(jnp.bfloat16)
    return grad_one, grad_three


def ffn_weight_grads(rows, grad_out, hidden, grad_one, grad_three):
    return (contract_rows(rows, grad_one).astype(jnp.bfloat16), contract_rows(rows, grad_three).astype(jnp.bfloat16), contract_rows(hidden, grad_out).astype(jnp.bfloat16))


def ffn_rows_grad(grad_one, grad_three, w_one, w_three):
    return contract_cols(grad_one, w_one) + contract_cols(grad_three, w_three)


def reduce_expert(place, own, foreign):
    theirs = [place.to_sibling(place.my_half(part, 1 - place.core)) for part in (own, foreign)]
    mine = [place.my_half(part, place.core).astype(jnp.float32) + got.astype(jnp.float32) for part, got in zip((own, foreign), theirs)]
    home = place.to_partner(mine[1].astype(jnp.bfloat16))
    total = (mine[0] + home.astype(jnp.float32)).astype(jnp.bfloat16)
    return lax.all_gather(total, "dp", axis=0, tiled=True).reshape((place.dp // 2,) + own.shape)


def solution(mesh):
    tok_spec = P(ALL_AXES, None)
    route_spec = P(None, ALL_AXES, None)
    exp_spec = P(None, "ep", None, None)
    repl_spec = P(None, None, None)

    def body(act_in, grad_out, slot_ids, gate_vals, w_dense, w_gate, w_up, w_down, ws_gate, ws_up, ws_down):
        place = Place(mesh)
        layers = w_dense.shape[0]
        tokens = act_in.shape[0]
        slots = 2 * tokens
        half_slots = slots // 2

        own_w = [[lax.dynamic_index_in_dim(w[layer], place.chip, 0, keepdims=False) for w in (w_gate, w_up, w_down)] for layer in range(layers)]
        foreign_w = [[foreign_weight(place, w) for w in own_w[layer]] for layer in range(layers)]

        token_ids = jnp.arange(tokens, dtype=jnp.int32)
        slot_idx = slot_ids.reshape(layers, tokens)
        turned = (slot_idx + place.half * half_slots) % slots
        flat = (turned + jnp.arange(layers, dtype=jnp.int32)[:, None] * slots).reshape(-1)
        owner = jnp.full((layers * slots,), tokens, jnp.int32).at[flat].set(jnp.tile(token_ids, layers), unique_indices=True).reshape(layers, 2, half_slots)

        def dispatch(layer, rows):
            ext = with_zero_row(rows)
            return [place.exchange(take_rows(ext, owner[layer, part])) for part in range(2)]

        def collect(layer, parts):
            back = jnp.concatenate([place.exchange(part) for part in parts], axis=0)
            return take_rows(back, turned[layer]).astype(jnp.float32)

        saved = []
        act = act_in
        for layer in range(layers):
            mixed = (act.astype(jnp.float32) + dot32(act, w_dense[layer])).astype(jnp.bfloat16)
            recv = dispatch(layer, mixed)
            weights = (own_w[layer], foreign_w[layer])
            fronts = [ffn_front(rows, w[0], w[1]) for rows, w in zip(recv, weights)]
            shared = ffn_front(mixed, ws_gate[layer], ws_up[layer])
            saved.append((act, mixed, recv, weights, fronts, shared))
            if layer + 1 < layers:
                outs = [dot32(front[2], w[2]).astype(jnp.bfloat16) for front, w in zip(fronts, weights)]
                routed = gate_vals[layer] * collect(layer, outs)
                act = (mixed.astype(jnp.float32) + routed + dot32(shared[2], ws_down[layer])).astype(jnp.bfloat16)

        grad_y = grad_out
        dense_sums = [None] * layers
        expert_sums = [None] * layers
        for layer in reversed(range(layers)):
            act, mixed, recv, weights, fronts, shared = saved[layer]
            grad_y32 = grad_y.astype(jnp.float32)
            grad_recv = dispatch(layer, (gate_vals[layer] * grad_y32).astype(jnp.bfloat16))
            backs = [ffn_back(g, front, w[2]) for g, front, w in zip(grad_recv, fronts, weights)]
            grad_rows = [ffn_rows_grad(b[0], b[1], w[0], w[1]).astype(jnp.bfloat16) for b, w in zip(backs, weights)]
            grad_routed = collect(layer, grad_rows)
            parts = [ffn_weight_grads(rows, g, front[2], b[0], b[1]) for rows, g, front, b in zip(recv, grad_recv, fronts, backs)]
            expert_sums[layer] = [reduce_expert(place, own, foreign) for own, foreign in zip(*parts)]
            s_back = ffn_back(grad_y, shared, ws_down[layer])
            s_grads = ffn_weight_grads(mixed, grad_y, shared[2], s_back[0], s_back[1])
            grad_mixed = (grad_y32 + grad_routed + ffn_rows_grad(s_back[0], s_back[1], ws_gate[layer], ws_up[layer])).astype(jnp.bfloat16)
            g_dense = contract_rows(act, grad_mixed).astype(jnp.bfloat16)
            grad_y = (grad_mixed.astype(jnp.float32) + contract_cols(grad_mixed, w_dense[layer])).astype(jnp.bfloat16)
            dense_sums[layer] = [lax.psum(part, ALL_AXES) for part in (g_dense,) + s_grads]
        dense_out = [jnp.stack([dense_sums[layer][which] for layer in range(layers)]) for which in range(4)]
        expert_out = [jnp.stack([expert_sums[layer][which] for layer in range(layers)]) for which in range(3)]
        return (grad_y, dense_out[0], expert_out[0], expert_out[1], expert_out[2], dense_out[1], dense_out[2], dense_out[3])

    return jax.shard_map(body, mesh=mesh, in_specs=(tok_spec, tok_spec, route_spec, route_spec, repl_spec, exp_spec, exp_spec, exp_spec, repl_spec, repl_spec, repl_spec), out_specs=(tok_spec, repl_spec, exp_spec, exp_spec, exp_spec, repl_spec, repl_spec, repl_spec), check_vma=False)
```

time: 1780 us -> 1260 us (0.71)
  waiting for transfers between devices: 900 us -> 473 us
  blocking collectives: 241 us -> 0 us
  starting transfers between devices: 26.6 us -> 110 us
  local copies, waits for them, and re-layouts: 166 us -> 186 us
    psum x2 -> x1, waiting for transfers between devices: 522 us -> 0.01 us  [body(): lax.psum(part, ALL_AXES)]
    ppermute x0 -> x30, waiting for transfers between devices: none -> 351 us  [the longest x12 343 us: to_partner(): return lax.ppermute(value, ALL_AXES, self.swap_z)]
    all_to_all x5 -> x14, waiting for transfers between devices: 378 us -> 116 us  [exchange(): lax.all_to_all(blocks, ALL_AXES, 0, 0, axis_index_groups=self.groups)]
    all_to_all x2 -> x0, blocking collectives: 241 us -> none  [layer_front(): lax.all_to_all(send_buf, 'ep', 0, 1)]
    dot_general x24 -> x17, matrix products: 275 us -> 118 us  [dot32(): return jnp.dot(left, right, preferred_element_type=jnp.float32)]
    dot_general x8 -> x20, matrix products: 63.8 us -> 159 us  [contract_cols(): lax.dot_general(left, right, (((1,), (1,)), ((), ())), preferred_element_...]
    dot_general x8 -> x20, matrix products: 36.6 us -> 117 us  [contract_rows(): lax.dot_general(left, right, (((0,), (0,)), ((), ())), preferred_element_...]
    all_to_all x5 -> x14, starting transfers between devices: 26.6 us -> 93.4 us  [exchange(): lax.all_to_all(blocks, ALL_AXES, 0, 0, axis_index_groups=self.groups)]
  transfers between devices with their start and end apart: 7 -> 51, of which waited for: 7 -> 25; matrix products, arithmetic and copies ran while one was open for 13% -> 43% of each run, Pallas kernels for 0% -> 0%
where the time goes in v1:
time: 1260 us; the launch traced here: 1250 us
  waiting for transfers between devices  473 us (38%)
  matrix products  393 us (31%)
  local copies, waits for them, and re-layouts  186 us (15%)
  starting transfers between devices  110 us (9%)
  other arithmetic  70.3 us (6%)
  between operations  17.3 us (1%)
    ppermute x12, waiting for transfers between devices, to_partner(): return lax.ppermute(value, ALL_AXES, self.swap_z)  343 us
    dot_general x20, matrix products, contract_cols(): lax.dot_general(left, right, (((1,), (1,)), ((), ())), preferred_element_...  159 us
    dot_general x17, matrix products, dot32(): return jnp.dot(left, right, preferred_element_type=jnp.float32)  118 us
    dot_general x20, matrix products, contract_rows(): lax.dot_general(left, right, (((0,), (0,)), ((), ())), preferred_element_...  117 us
    gather x11, local copies, waits for them, and re-layouts, take_rows(): return jnp.take(source, index, axis=0, mode='clip')  117 us
    all_to_all x14, waiting for transfers between devices, exchange(): lax.all_to_all(blocks, ALL_AXES, 0, 0, axis_index_groups=self.groups)  116 us
    all_to_all x14, starting transfers between devices, exchange(): lax.all_to_all(blocks, ALL_AXES, 0, 0, axis_index_groups=self.groups)  93.4 us
    slice x3, local copies, waits for them, and re-layouts, body(): w[layer]  27.5 us
  transfers between devices with their start and end apart: 51, of which 25 were waited for; matrix products, arithmetic and copies ran while one was open for 43% of the time, Pallas kernels for 0%

profile of v1, /device:TPU:0, one launch (start us, length us, event | category | flops | bytes accessed | tf_op | source)
XLA Modules:
  0.0 1249.9 jit_solution(16236339365239090980)
XLA Ops:
  9.0 15.5 %scatter_custom_fusion = s32[8192]{0:T(1024)S(1)} fusion(s32[4096]{0:T(1024)S(1)} %bitcast.272, s32[4096]{0:T(1024)S(1)} %bitcast.273, s32[]{:T(128)} %constant.216.clone.1), kind=kCustom, calls=%fused_computation.229 | custom fusion | bytes 32772 | tf_op jit(solution)/shard_map/scatter | solution.py:123
  28.4 9.3 gather_fusion.5
  51.9 11.6 gather_fusion.2
  63.5 18.0 %all-to-all-done.7 = bf16[16,128,640]{2,1,0:T(8,128)(2,1)} async-done(((bf16[16,128,640]{2,1,0:T(8,128)(2,1)}), bf16[16,128,640]{2,1,0:T(8,128)(2,1)}, u32[]{:S(2)}, u32[]{:S(2)}) %all-to-all-start.7) | async-done | bytes 2621472 | tf_op jit(solution)/shard_map/all_to_all | solution.py:43
  81.5 6.6 all-to-all-start.3
  88.2 9.2 fusion.139
  101.3 9.2 fusion.138
  113.0 11.6 gather_fusion.1
  124.6 19.2 %all-to-all-done.3 = bf16[16,128,640]{2,1,0:T(8,128)(2,1)} async-done(((bf16[16,128,640]{2,1,0:T(8,128)(2,1)}), bf16[16,128,640]{2,1,0:T(8,128)(2,1)}, u32[]{:S(2)}, u32[]{:S(2)}) %all-to-all-start.3) | async-done | bytes 2621472 | tf_op jit(solution)/shard_map/all_to_all | solution.py:43
  143.8 6.7 all-to-all-start.1
  150.5 9.0 fusion.140
  164.4 31.5 %collective-permute-done.4 = bf16[512,640]{1,0:T(8,128)(2,1)} collective-permute-done((bf16[512,640]{1,0:T(8,128)(2,1)S(1)}, bf16[512,640]{1,0:T(8,128)(2,1)}, u32[]{:S(2)}, u32[]{:S(2)}) %collective-permute-start.4) | collective-permute-done | bytes 655392 | tf_op jit(solution)/shard_map/ppermute | solution.py:46
  206.6 10.6 multiply_convert_fusion.16
  223.9 13.9 %all-to-all-start.4 = ((bf16[16,128,640]{2,1,0:T(8,128)(2,1)}), bf16[16,128,640]{2,1,0:T(8,128)(2,1)}, u32[]{:S(2)}, u32[]{:S(2)}) async-start(bf16[16,128,640]{2,1,0:T(8,128)(2,1)} %bitcast.262), calls=%async_computation.4 | async-start | bytes 5242880 | tf_op jit(solution)/shard_map/all_to_all | solution.py:43
  243.5 12.9 %multiply_convert_fusion.17 = (bf16[2048,1024]{1,0:T(8,128)(2,1)S(1)}, f32[2048,1024]{1,0:T(8,128)}) fusion(f32[2048,1024]{1,0:T(8,128)S(1)} %fusion.65, bf16[2048,640]{1,0:T(8,128)(2,1)} %bitcast.11, bf16[1,4,640,1024]{3,2,1,0:T(8,128)(2,1)} %get-tuple-element.37, s32[]{:T(128)S(6)} %select_n.154), kind=kOutput, calls=%fused_computation.42 | convolution fusion | flops 2696937472 | bytes 24903684 | tf_op jit(solution)/shard_map/dot_general | solution.py:23
  264.3 11.0 all-to-all-done.4
  275.3 6.6 all-to-all-start.2
  281.9 9.4 gather_fusion
  291.3 28.0 %all-to-all-done.2 = bf16[16,128,640]{2,1,0:T(8,128)(2,1)} async-done(((bf16[16,128,640]{2,1,0:T(8,128)(2,1)}), bf16[16,128,640]{2,1,0:T(8,128)(2,1)}, u32[]{:S(2)}, u32[]{:S(2)}) %all-to-all-start.2) | async-done | bytes 2621472 | tf_op jit(solution)/shard_map/all_to_all | solution.py:43
  319.2 7.0 all-to-all-start
  331.9 7.5 multiply_convert_fusion.15
  344.8 12.7 %gather_fusion.3 = bf16[2048,640]{1,0:T(8,128)(2,1)} fusion(bf16[4096,640]{1,0:T(8,128)(2,1)} %pad_maximum_fusion.3, s32[2048]{0:T(1024)S(1)} %broadcast_clamp_fusion.1), kind=kCustom, calls=%fused_computation.3 | custom fusion | bytes 5251072 | tf_op jit(solution)/shard_map/jit(_take)/gather | solution.py:65
  357.5 7.2 add_convert_fusion.7
  369.2 9.7 gather_fusion.4
  391.1 45.9 %collective-permute-done.10 = bf16[320,1024]{1,0:T(8,128)(2,1)S(1)} collective-permute-done((bf16[320,1024]{1,0:T(8,128)(2,1)S(1)}, bf16[320,1024]{1,0:T(8,128)(2,1)S(1)}, u32[]{:S(2)}, u32[]{:S(2)}) %collective-permute-start.10) | collective-permute-done | bytes 655392 | tf_op jit(solution)/shard_map/ppermute | solution.py:46
  437.0 23.3 %collective-permute-done.8 = bf16[320,1024]{1,0:T(8,128)(2,1)} collective-permute-done((bf16[320,1024]{1,0:T(8,128)(2,1)S(1)}, bf16[320,1024]{1,0:T(8,128)(2,1)}, u32[]{:S(2)}, u32[]{:S(2)}) %collective-permute-start.8) | collective-permute-done | bytes 655392 | tf_op jit(solution)/shard_map/ppermute | solution.py:46
  460.3 13.6 %collective-permute-done.6 = bf16[512,640]{1,0:T(8,128)(2,1)S(1)} collective-permute-done((bf16[512,640]{1,0:T(8,128)(2,1)S(1)}, bf16[512,640]{1,0:T(8,128)(2,1)S(1)}, u32[]{:S(2)}, u32[]{:S(2)}) %collective-permute-start.6) | collective-permute-done | bytes 655392 | tf_op jit(solution)/shard_map/ppermute | solution.py:46
  475.1 9.3 gather_fusion.6
  497.2 9.4 fusion.45
  506.6 10.6 multiply_convert_fusion.13
  517.2 7.1 fusion.40
  541.2 9.4 fusion.95
  550.6 13.1 %multiply_convert_fusion.12 = (bf16[2048,1024]{1,0:T(8,128)(2,1)}, bf16[2048,1024]{1,0:T(8,128)(2,1)}) fusion(f32[2048,1024]{1,0:T(8,128)S(1)} %fusion.93, f32[2048,1024]{1,0:T(8,128)} %fusion.95, bf16[2048,640]{1,0:T(8,128)(2,1)} %bitcast.38, bf16[512,640]{1,0:T(8,128)(2,1)S(1)} %get-tuple-element.47, bf16[512,640]{1,0:T(8,128)(2,1)S(1)} %get-tuple-element.46), kind=kOutput, calls=%fused_computation.29 | convolution fusion | flops 2714238976 | bytes 29097984 | tf_op jit(solution)/shard_map/dot_general | solution.py:19
  579.8 8.9 fusion.33
  594.4 11.9 multiply_convert_fusion.9
  621.8 12.8 %gather_fusion.7 = bf16[2048,640]{1,0:T(8,128)(2,1)} fusion(bf16[4096,640]{1,0:T(8,128)(2,1)} %pad_maximum_fusion.4, s32[2048]{0:T(1024)S(1)} %broadcast_clamp_fusion), kind=kCustom, calls=%fused_computation.7 | custom fusion | bytes 5251072 | tf_op jit(solution)/shard_map/jit(_take)/gather | solution.py:65
  634.7 8.7 fusion.8
  648.0 9.3 gather_fusion.8
  657.3 6.6 all-to-all-start.10
  664.0 9.3 gather_fusion.9
  673.3 28.0 %all-to-all-done.10 = bf16[16,128,640]{2,1,0:T(8,128)(2,1)} async-done(((bf16[16,128,640]{2,1,0:T(8,128)(2,1)}), bf16[16,128,640]{2,1,0:T(8,128)(2,1)}, u32[]{:S(2)}, u32[]{:S(2)}) %all-to-all-start.10) | async-done | bytes 2621472 | tf_op jit(solution)/shard_map/all_to_all | solution.py:43
  701.3 7.0 all-to-all-start.12
  708.4 10.9 fusion.21
  723.3 11.6 multiply_convert_fusion.7
  752.6 7.1 fusion.23
  763.0 12.2 multiply_convert_fusion.6
  790.0 6.6 all-to-all-start.13
  796.7 13.9 %multiply_convert_fusion.3 = (bf16[2048,1024]{1,0:T(8,128)(2,1)S(1)}, bf16[2048,1024]{1,0:T(8,128)(2,1)}) fusion(f32[2048,1024]{1,0:T(8,128)} %copy-done.56, f32[2048,1024]{1,0:T(8,128)} %get-tuple-element.67, bf16[2048,640]{1,0:T(8,128)(2,1)} %get-tuple-element.69, bf16[2,1024,640]{2,1,0:T(8,128)(2,1)} %param.21), kind=kOutput, calls=%fused_computation.18 | convolution fusion | flops 2711617536 | bytes 29097984 | tf_op jit(solution)/shard_map/dot_general | solution.py:19
  810.6 9.6 fusion.53
  838.6 11.3 gather_fusion.10
  849.9 8.8 fusion.11
  863.8 10.4 fusion.16
  874.4 10.4 fusion.17
  887.3 44.5 %collective-permute-done.29 = bf16[512,640]{1,0:T(8,128)(2,1)S(1)} collective-permute-done((bf16[512,640]{1,0:T(8,128)(2,1)S(1)}, bf16[512,640]{1,0:T(8,128)(2,1)S(1)}, u32[]{:S(2)}, u32[]{:S(2)}) %collective-permute-start.29) | collective-permute-done | bytes 655392 | tf_op jit(solution)/shard_map/ppermute | solution.py:46
  933.2 6.6 convolution_convert_fusion.7
  947.7 38.5 %collective-permute-done.26 = bf16[512,640]{1,0:T(8,128)(2,1)S(1)} collective-permute-done((bf16[512,640]{1,0:T(8,128)(2,1)S(1)}, bf16[512,640]{1,0:T(8,128)(2,1)S(1)}, u32[]{:S(2)}, u32[]{:S(2)}) %collective-permute-start.26) | collective-permute-done | bytes 655392 | tf_op jit(solution)/shard_map/ppermute | solution.py:46
  1000.9 36.1 %collective-permute-done.17 = bf16[320,1024]{1,0:T(8,128)(2,1)S(1)} collective-permute-done((bf16[320,1024]{1,0:T(8,128)(2,1)S(1)}, bf16[320,1024]{1,0:T(8,128)(2,1)S(1)}, u32[]{:S(2)}, u32[]{:S(2)}) %collective-permute-start.17) | collective-permute-done | bytes 655392 | tf_op jit(solution)/shard_map/ppermute | solution.py:46
  1051.5 37.5 %collective-permute-done.14 = bf16[320,1024]{1,0:T(8,128)(2,1)S(1)} collective-permute-done((bf16[320,1024]{1,0:T(8,128)(2,1)S(1)}, bf16[320,1024]{1,0:T(8,128)(2,1)S(1)}, u32[]{:S(2)}, u32[]{:S(2)}) %collective-permute-start.14) | collective-permute-done | bytes 655392 | tf_op jit(solution)/shard_map/ppermute | solution.py:46
  1104.0 43.2 %collective-permute-done.23 = bf16[320,1024]{1,0:T(8,128)(2,1)S(1)} collective-permute-done((bf16[320,1024]{1,0:T(8,128)(2,1)S(1)}, bf16[320,1024]{1,0:T(8,128)(2,1)S(1)}, u32[]{:S(2)}, u32[]{:S(2)}) %collective-permute-start.23) | collective-permute-done | bytes 655392 | tf_op jit(solution)/shard_map/ppermute | solution.py:46
  1161.7 29.0 %collective-permute-done.20 = bf16[320,1024]{1,0:T(8,128)(2,1)S(1)} collective-permute-done((bf16[320,1024]{1,0:T(8,128)(2,1)S(1)}, bf16[320,1024]{1,0:T(8,128)(2,1)S(1)}, u32[]{:S(2)}, u32[]{:S(2)}) %collective-permute-start.20) | collective-permute-done | bytes 655392 | tf_op jit(solution)/shard_map/ppermute | solution.py:46
  1191.9 6.5 add_convert_fusion
  1208.5 9.2 pad_maximum_fusion.2
  1217.7 9.1 pad_maximum_fusion
  1233.2 9.1 pad_maximum_fusion.1
  (349 shorter events, 311.7 us)
Async XLA Ops:
  37.8 43.8 %all-to-all-start.7 = ((bf16[16,128,640]{2,1,0:T(8,128)(2,1)}), bf16[16,128,640]{2,1,0:T(8,128)(2,1)}, u32[]{:S(2)}, u32[]{:S(2)}) async-start(bf16[16,128,640]{2,1,0:T(8,128)(2,1)} %bitcast.248), calls=%async_computation.7 | async-start | bytes 5242880 | tf_op jit(solution)/shard_map/all_to_all | solution.py:43
  81.5 62.3 %all-to-all-start.3 = ((bf16[16,128,640]{2,1,0:T(8,128)(2,1)}), bf16[16,128,640]{2,1,0:T(8,128)(2,1)}, u32[]{:S(2)}, u32[]{:S(2)}) async-start(bf16[16,128,640]{2,1,0:T(8,128)(2,1)} %bitcast.241), calls=%async_computation.3 | async-start | bytes 5242880 | tf_op jit(solution)/shard_map/all_to_all | solution.py:43
  98.6 65.2 %collective-permute-start = (bf16[320,1024]{1,0:T(8,128)(2,1)S(1)}, bf16[320,1024]{1,0:T(8,128)(2,1)}, u32[]{:S(2)}, u32[]{:S(2)}) collective-permute-start(bf16[320,1024]{1,0:T(8,128)(2,1)S(1)} %dynamic-slice_bitcast_fusion.5), channel_id=1, source_target_pairs={{0,16},{1,17},{2,18},{3,19},{4,20},{5,21},{6,22},{7,23},{8,24},{9,... | collective-permute-start | bytes 1966088 | tf_op jit(solution)/shard_map/ppermute | solution.py:46
  112.6 51.5 %collective-permute-start.2 = (bf16[320,1024]{1,0:T(8,128)(2,1)}, bf16[320,1024]{1,0:T(8,128)(2,1)}, u32[]{:S(2)}, u32[]{:S(2)}) collective-permute-start(bf16[320,1024]{1,0:T(8,128)(2,1)} %dynamic-slice_bitcast_fusion.4), channel_id=1, source_target_pairs={{0,16},{1,17},{2,18},{3,19},{4,20},{5,21},{6,22},{7,23},{8,24},{9,... | collective-permute-start | bytes 1966088 | tf_op jit(solution)/shard_map/ppermute | solution.py:46
  143.8 80.1 %all-to-all-start.1 = ((bf16[16,128,640]{2,1,0:T(8,128)(2,1)}), bf16[16,128,640]{2,1,0:T(8,128)(2,1)}, u32[]{:S(2)}, u32[]{:S(2)}) async-start(bf16[16,128,640]{2,1,0:T(8,128)(2,1)} %bitcast.242), calls=%async_computation.1 | async-start | bytes 5242880 | tf_op jit(solution)/shard_map/all_to_all | solution.py:43
  160.8 35.1 %collective-permute-start.4 = (bf16[512,640]{1,0:T(8,128)(2,1)S(1)}, bf16[512,640]{1,0:T(8,128)(2,1)}, u32[]{:S(2)}, u32[]{:S(2)}) collective-permute-start(bf16[512,640]{1,0:T(8,128)(2,1)S(1)} %dynamic-slice_bitcast_fusion.3), channel_id=1, source_target_pairs={{0,16},{1,17},{2,18},{3,19},{4,20},{5,21},{6,22},{7,23},{8,24},{9,... | collective-permute-start | bytes 1966088 | tf_op jit(solution)/shard_map/ppermute | solution.py:46
  163.9 32.0 %collective-permute-start.1 = (bf16[320,1024]{1,0:T(8,128)(2,1)}, bf16[320,1024]{1,0:T(8,128)(2,1)S(1)}, u32[]{:S(2)}, u32[]{:S(2)}) collective-permute-start(bf16[320,1024]{1,0:T(8,128)(2,1)} %collective-permute-done), channel_id=1, source_target_pairs={{0,1},{1,0},{2,3},{3,2},{4,5},{5,4},{6,7},{7,6},{8,9},{9,8},{10,11... | collective-permute-start | bytes 1966088 | tf_op jit(solution)/shard_map/ppermute | solution.py:49
  164.1 33.0 %collective-permute-start.3 = (bf16[320,1024]{1,0:T(8,128)(2,1)}, bf16[320,1024]{1,0:T(8,128)(2,1)}, u32[]{:S(2)}, u32[]{:S(2)}) collective-permute-start(bf16[320,1024]{1,0:T(8,128)(2,1)} %collective-permute-done.2), channel_id=1, source_target_pairs={{0,1},{1,0},{2,3},{3,2},{4,5},{5,4},{6,7},{7,6},{8,9},{9,8},{10,11... | collective-permute-start | bytes 1966088 | tf_op jit(solution)/shard_map/ppermute | solution.py:49
  195.9 3.1 collective-permute-start.5
  200.8 16.4 %copy-start.22 = (bf16[512,640]{1,0:T(8,128)(2,1)}, bf16[512,640]{1,0:T(8,128)(2,1)S(1)}, u32[]{:S(2)}) copy-start(bf16[512,640]{1,0:T(8,128)(2,1)S(1)} %get-tuple-element.48) | copy-start | bytes 1966084
  200.9 16.4 %copy-start.24 = (bf16[512,640]{1,0:T(8,128)(2,1)}, bf16[512,640]{1,0:T(8,128)(2,1)S(1)}, u32[]{:S(2)}) copy-start(bf16[512,640]{1,0:T(8,128)(2,1)S(1)} %get-tuple-element.49) | copy-start | bytes 1966084
  223.9 51.4 %all-to-all-start.4 = ((bf16[16,128,640]{2,1,0:T(8,128)(2,1)}), bf16[16,128,640]{2,1,0:T(8,128)(2,1)}, u32[]{:S(2)}, u32[]{:S(2)}) async-start(bf16[16,128,640]{2,1,0:T(8,128)(2,1)} %bitcast.262), calls=%async_computation.4 | async-start | bytes 5242880 | tf_op jit(solution)/shard_map/all_to_all | solution.py:43
  243.5 13.0 %copy-start.57 = (f32[2048,1024]{1,0:T(8,128)}, f32[2048,1024]{1,0:T(8,128)S(1)}, u32[]{:S(2)}) copy-start(f32[2048,1024]{1,0:T(8,128)S(1)} %fusion.65) | copy-start | bytes 25165828
  275.3 43.9 %all-to-all-start.2 = ((bf16[16,128,640]{2,1,0:T(8,128)(2,1)}), bf16[16,128,640]{2,1,0:T(8,128)(2,1)}, u32[]{:S(2)}, u32[]{:S(2)}) async-start(bf16[16,128,640]{2,1,0:T(8,128)(2,1)} %bitcast.261), calls=%async_computation.2 | async-start | bytes 5242880 | tf_op jit(solution)/shard_map/all_to_all | solution.py:43
  319.2 59.7 %all-to-all-start = ((bf16[16,128,640]{2,1,0:T(8,128)(2,1)}), bf16[16,128,640]{2,1,0:T(8,128)(2,1)}, u32[]{:S(2)}, u32[]{:S(2)}) async-start(bf16[16,128,640]{2,1,0:T(8,128)(2,1)} %bitcast.244), calls=%async_computation | async-start | bytes 5242880 | tf_op jit(solution)/shard_map/all_to_all | solution.py:43
  326.9 17.9 %copy-start.36 = (s32[2048]{0:T(1024)}, s32[2048]{0:T(1024)S(1)}, u32[]{:S(2)}) copy-start(s32[2048]{0:T(1024)S(1)} %broadcast_clamp_fusion.1) | copy-start | bytes 24580
  344.8 12.7 %copy-start.39 = (f32[1,2048,1]{1,2,0:T(1,128)S(1)}, f32[1,2048,1]{1,2,0:T(1,128)}, u32[]{:S(2)}) copy-start(f32[1,2048,1]{1,2,0:T(1,128)} %get-tuple-element.61) | copy-start | bytes 24580
  378.9 105.5 %all-to-all-start.5 = ((bf16[16,128,640]{2,1,0:T(8,128)(2,1)}), bf16[16,128,640]{2,1,0:T(8,128)(2,1)}, u32[]{:S(2)}, u32[]{:S(2)}) async-start(bf16[16,128,640]{2,1,0:T(8,128)(2,1)} %bitcast.243), calls=%async_computation.5 | async-start | bytes 5242880 | tf_op jit(solution)/shard_map/all_to_all | solution.py:43
  385.5 51.5 %collective-permute-start.10 = (bf16[320,1024]{1,0:T(8,128)(2,1)S(1)}, bf16[320,1024]{1,0:T(8,128)(2,1)S(1)}, u32[]{:S(2)}, u32[]{:S(2)}) collective-permute-start(bf16[320,1024]{1,0:T(8,128)(2,1)S(1)} %dynamic-slice_bitcast_fusion), channel_id=1, source_target_pairs={{0,16},{1,17},{2,18},{3,19},{4,20},{5,21},{6,22},{7,23},{8,24},{9,... | collective-permute-start | bytes 1966088 | tf_op jit(solution)/shard_map/ppermute | solution.py:46
  385.5 89.6 %copy-start.35 = (s32[2048]{0:T(1024)S(1)}, s32[2048]{0:T(1024)}, u32[]{:S(2)}) copy-start(s32[2048]{0:T(1024)} %copy-done.34) | copy-start | bytes 24580
  386.8 73.5 %collective-permute-start.8 = (bf16[320,1024]{1,0:T(8,128)(2,1)S(1)}, bf16[320,1024]{1,0:T(8,128)(2,1)}, u32[]{:S(2)}, u32[]{:S(2)}) collective-permute-start(bf16[320,1024]{1,0:T(8,128)(2,1)S(1)} %dynamic-slice_bitcast_fusion.1), channel_id=1, source_target_pairs={{0,16},{1,17},{2,18},{3,19},{4,20},{5,21},{6,22},{7,23},{8,24},{9,... | collective-permute-start | bytes 1966088 | tf_op jit(solution)/shard_map/ppermute | solution.py:46
  391.0 82.9 %collective-permute-start.6 = (bf16[512,640]{1,0:T(8,128)(2,1)S(1)}, bf16[512,640]{1,0:T(8,128)(2,1)S(1)}, u32[]{:S(2)}, u32[]{:S(2)}) collective-permute-start(bf16[512,640]{1,0:T(8,128)(2,1)S(1)} %dynamic-slice_bitcast_fusion.2), channel_id=1, source_target_pairs={{0,16},{1,17},{2,18},{3,19},{4,20},{5,21},{6,22},{7,23},{8,24},{9,... | collective-permute-start | bytes 1966088 | tf_op jit(solution)/shard_map/ppermute | solution.py:46
  437.0 37.0 %collective-permute-start.11 = (bf16[320,1024]{1,0:T(8,128)(2,1)S(1)}, bf16[320,1024]{1,0:T(8,128)(2,1)S(1)}, u32[]{:S(2)}, u32[]{:S(2)}) collective-permute-start(bf16[320,1024]{1,0:T(8,128)(2,1)S(1)} %collective-permute-done.10), channel_id=1, source_target_pairs={{0,1},{1,0},{2,3},{3,2},{4,5},{5,4},{6,7},{7,6},{8,9},{9,8},{10,11... | collective-permute-start | bytes 1966088 | tf_op jit(solution)/shard_map/ppermute | solution.py:49
  460.3 28.7 %collective-permute-start.9 = (bf16[320,1024]{1,0:T(8,128)(2,1)}, bf16[320,1024]{1,0:T(8,128)(2,1)}, u32[]{:S(2)}, u32[]{:S(2)}) collective-permute-start(bf16[320,1024]{1,0:T(8,128)(2,1)} %collective-permute-done.8), channel_id=1, source_target_pairs={{0,1},{1,0},{2,3},{3,2},{4,5},{5,4},{6,7},{7,6},{8,9},{9,8},{10,11... | collective-permute-start | bytes 1966088 | tf_op jit(solution)/shard_map/ppermute | solution.py:49
  474.0 60.4 %collective-permute-start.7 = (bf16[512,640]{1,0:T(8,128)(2,1)S(1)}, bf16[512,640]{1,0:T(8,128)(2,1)}, u32[]{:S(2)}, u32[]{:S(2)}) collective-permute-start(bf16[512,640]{1,0:T(8,128)(2,1)S(1)} %collective-permute-done.6), channel_id=1, source_target_pairs={{0,1},{1,0},{2,3},{3,2},{4,5},{5,4},{6,7},{7,6},{8,9},{9,8},{10,11... | collective-permute-start | bytes 1966088 | tf_op jit(solution)/shard_map/ppermute | solution.py:49
  484.4 12.8 %slice-start = ((s8[5242880]{0:T(1024)(128)(4,1)}), s8[1048576]{0:T(1024)(128)(4,1)S(1)}, s32[]{:S(2)}) async-start(s8[5242880]{0:T(1024)(128)(4,1)} %bitcast.249), calls=%async_computation.21 | async-start | bytes 2097152
  484.4 44.7 %all-to-all-start.8 = ((bf16[16,128,640]{2,1,0:T(8,128)(2,1)}), bf16[16,128,640]{2,1,0:T(8,128)(2,1)}, u32[]{:S(2)}, u32[]{:S(2)}) async-start(bf16[16,128,640]{2,1,0:T(8,128)(2,1)} %bitcast.245), calls=%async_computation.8 | async-start | bytes 5242880 | tf_op jit(solution)/shard_map/all_to_all | solution.py:43
  529.2 44.7 %all-to-all-start.6 = ((bf16[16,128,640]{2,1,0:T(8,128)(2,1)}), bf16[16,128,640]{2,1,0:T(8,128)(2,1)S(1)}, u32[]{:S(2)}, u32[]{:S(2)}) async-start(bf16[16,128,640]{2,1,0:T(8,128)(2,1)} %bitcast.257), calls=%async_computation.6 | async-start | bytes 5242880 | tf_op jit(solution)/shard_map/all_to_all | solution.py:43
  573.9 43.5 %all-to-all-start.9 = ((bf16[16,128,640]{2,1,0:T(8,128)(2,1)}), bf16[16,128,640]{2,1,0:T(8,128)(2,1)}, u32[]{:S(2)}, u32[]{:S(2)}) async-start(bf16[16,128,640]{2,1,0:T(8,128)(2,1)} %bitcast.260), calls=%async_computation.9 | async-start | bytes 5242880 | tf_op jit(solution)/shard_map/all_to_all | solution.py:43
  594.4 13.8 %copy-start.42 = (bf16[2,640,1024]{2,1,0:T(8,128)(2,1)S(1)}, bf16[2,640,1024]{2,1,0:T(8,128)(2,1)}, u32[]{:S(2)}) copy-start(bf16[2,640,1024]{2,1,0:T(8,128)(2,1)} %param.19) | copy-start | bytes 7864324
  621.8 12.8 %copy-start.1 = (bf16[2048,640]{1,0:T(8,128)(2,1)S(1)}, bf16[2048,640]{1,0:T(8,128)(2,1)}, u32[]{:S(2)}) copy-start(bf16[2048,640]{1,0:T(8,128)(2,1)} %param.12) | copy-start | bytes 7864324
  657.3 44.0 %all-to-all-start.10 = ((bf16[16,128,640]{2,1,0:T(8,128)(2,1)}), bf16[16,128,640]{2,1,0:T(8,128)(2,1)}, u32[]{:S(2)}, u32[]{:S(2)}) async-start(bf16[16,128,640]{2,1,0:T(8,128)(2,1)} %bitcast.247), calls=%async_computation.10 | async-start | bytes 5242880 | tf_op jit(solution)/shard_map/all_to_all | solution.py:43
  701.3 46.1 %all-to-all-start.12 = ((bf16[16,128,640]{2,1,0:T(8,128)(2,1)}), bf16[16,128,640]{2,1,0:T(8,128)(2,1)}, u32[]{:S(2)}, u32[]{:S(2)}) async-start(bf16[16,128,640]{2,1,0:T(8,128)(2,1)} %bitcast.246), calls=%async_computation.12 | async-start | bytes 5242880 | tf_op jit(solution)/shard_map/all_to_all | solution.py:43
  747.4 42.6 %all-to-all-start.11 = ((bf16[16,128,640]{2,1,0:T(8,128)(2,1)}), bf16[16,128,640]{2,1,0:T(8,128)(2,1)S(1)}, u32[]{:S(2)}, u32[]{:S(2)}) async-start(bf16[16,128,640]{2,1,0:T(8,128)(2,1)} %bitcast.258), calls=%async_computation.11 | async-start | bytes 5242880 | tf_op jit(solution)/shard_map/all_to_all | solution.py:43
  763.0 12.2 copy-start.21
  790.0 44.0 %all-to-all-start.13 = ((bf16[16,128,640]{2,1,0:T(8,128)(2,1)}), bf16[16,128,640]{2,1,0:T(8,128)(2,1)}, u32[]{:S(2)}, u32[]{:S(2)}) async-start(bf16[16,128,640]{2,1,0:T(8,128)(2,1)} %bitcast.259), calls=%async_computation.13 | async-start | bytes 5242880 | tf_op jit(solution)/shard_map/all_to_all | solution.py:43
  796.6 401.9 %all-reduce.7.cloned.1.call-start = ((), (), s32[]{:S(2)}) async-start(), calls=%async_computation.20 | async-start | bytes 19005440 | tf_op jit(solution)/shard_map/psum | solution.py:164
  796.7 13.9 %copy-start.43 = (bf16[2,640,1024]{2,1,0:T(8,128)(2,1)S(1)}, bf16[2,640,1024]{2,1,0:T(8,128)(2,1)}, u32[]{:S(2)}) copy-start(bf16[2,640,1024]{2,1,0:T(8,128)(2,1)} %param.19) | copy-start | bytes 7864324
  810.6 18.3 %copy-start.73 = (bf16[2048,1024]{1,0:T(8,128)(2,1)}, bf16[2048,1024]{1,0:T(8,128)(2,1)S(1)}, u32[]{:S(2)}) copy-start(bf16[2048,1024]{1,0:T(8,128)(2,1)S(1)} %get-tuple-element.24) | copy-start | bytes 12582916
  863.4 345.1 %all-gather.17.cloned.1.call-start = ((), (), s32[]{:S(2)}) async-start(), calls=%async_computation.19 | async-start | bytes 5898240 | tf_op jit(solution)/shard_map/all_gather | solution.py:100
  874.3 11.2 collective-permute-start.28
  884.9 2.4 collective-permute-start.27
  885.7 46.2 %collective-permute-start.29 = (bf16[512,640]{1,0:T(8,128)(2,1)S(1)}, bf16[512,640]{1,0:T(8,128)(2,1)S(1)}, u32[]{:S(2)}, u32[]{:S(2)}) collective-permute-start(bf16[512,640]{1,0:T(8,128)(2,1)S(1)} %add_convert_fusion.10), channel_id=1, source_target_pairs={{0,16},{1,17},{2,18},{3,19},{4,20},{5,21},{6,22},{7,23},{8,24},{9,... | collective-permute-start | bytes 1966088 | tf_op jit(solution)/shard_map/ppermute | solution.py:46
  933.0 275.5 %all-gather.15.cloned.1.call-start = ((), (), s32[]{:S(2)}) async-start(), calls=%async_computation.18 | async-start | bytes 5898240 | tf_op jit(solution)/shard_map/all_gather | solution.py:100
  939.9 6.1 collective-permute-start.25
  945.4 2.3 collective-permute-start.24
  946.2 40.1 %collective-permute-start.26 = (bf16[512,640]{1,0:T(8,128)(2,1)S(1)}, bf16[512,640]{1,0:T(8,128)(2,1)S(1)}, u32[]{:S(2)}, u32[]{:S(2)}) collective-permute-start(bf16[512,640]{1,0:T(8,128)(2,1)S(1)} %add_convert_fusion.12), channel_id=1, source_target_pairs={{0,16},{1,17},{2,18},{3,19},{4,20},{5,21},{6,22},{7,23},{8,24},{9,... | collective-permute-start | bytes 1966088 | tf_op jit(solution)/shard_map/ppermute | solution.py:46
  987.4 230.3 %all-gather.9.cloned.1.call-start = ((), (), s32[]{:S(2)}) async-start(), calls=%async_computation.15 | async-start | bytes 5898240 | tf_op jit(solution)/shard_map/all_gather | solution.py:100
  993.8 5.4 collective-permute-start.16
  998.7 2.2 collective-permute-start.15
  999.4 37.5 %collective-permute-start.17 = (bf16[320,1024]{1,0:T(8,128)(2,1)S(1)}, bf16[320,1024]{1,0:T(8,128)(2,1)S(1)}, u32[]{:S(2)}, u32[]{:S(2)}) collective-permute-start(bf16[320,1024]{1,0:T(8,128)(2,1)S(1)} %add_convert_fusion.18), channel_id=1, source_target_pairs={{0,16},{1,17},{2,18},{3,19},{4,20},{5,21},{6,22},{7,23},{8,24},{9,... | collective-permute-start | bytes 1966088 | tf_op jit(solution)/shard_map/ppermute | solution.py:46
  1038.2 179.5 %all-gather.7.cloned.1.call-start = ((), (), s32[]{:S(2)}) async-start(), calls=%async_computation.14 | async-start | bytes 5898240 | tf_op jit(solution)/shard_map/all_gather | solution.py:100
  1044.3 5.4 collective-permute-start.13
  1049.2 2.3 collective-permute-start.12
  1050.0 39.0 %collective-permute-start.14 = (bf16[320,1024]{1,0:T(8,128)(2,1)S(1)}, bf16[320,1024]{1,0:T(8,128)(2,1)S(1)}, u32[]{:S(2)}, u32[]{:S(2)}) collective-permute-start(bf16[320,1024]{1,0:T(8,128)(2,1)S(1)} %add_convert_fusion.20), channel_id=1, source_target_pairs={{0,16},{1,17},{2,18},{3,19},{4,20},{5,21},{6,22},{7,23},{8,24},{9,... | collective-permute-start | bytes 1966088 | tf_op jit(solution)/shard_map/ppermute | solution.py:46
  1090.2 136.6 %all-gather.13.cloned.1.call-start = ((), (), s32[]{:S(2)}) async-start(), calls=%async_computation.17 | async-start | bytes 5898240 | tf_op jit(solution)/shard_map/all_gather | solution.py:100
  1096.7 5.4 collective-permute-start.22
  1101.6 2.4 collective-permute-start.21
  1102.4 44.8 %collective-permute-start.23 = (bf16[320,1024]{1,0:T(8,128)(2,1)S(1)}, bf16[320,1024]{1,0:T(8,128)(2,1)S(1)}, u32[]{:S(2)}, u32[]{:S(2)}) collective-permute-start(bf16[320,1024]{1,0:T(8,128)(2,1)S(1)} %add_convert_fusion.14), channel_id=1, source_target_pairs={{0,16},{1,17},{2,18},{3,19},{4,20},{5,21},{6,22},{7,23},{8,24},{9,... | collective-permute-start | bytes 1966088 | tf_op jit(solution)/shard_map/ppermute | solution.py:46
  1148.4 84.8 %all-gather.11.cloned.1.call-start = ((), (), s32[]{:S(2)}) async-start(), calls=%async_computation.16 | async-start | bytes 5898240 | tf_op jit(solution)/shard_map/all_gather | solution.py:100
  1154.6 5.4 collective-permute-start.19
  1159.4 32.5 %copy-start.49 = (bf16[2,640,640]{2,1,0:T(8,128)(2,1)S(1)}, bf16[2,640,640]{2,1,0:T(8,128)(2,1)}, u32[]{:S(2)}) copy-start(bf16[2,640,640]{2,1,0:T(8,128)(2,1)} %param.15) | copy-start | bytes 4915204
  1159.4 2.3 collective-permute-start.18
  1160.2 30.5 %collective-permute-start.20 = (bf16[320,1024]{1,0:T(8,128)(2,1)S(1)}, bf16[320,1024]{1,0:T(8,128)(2,1)S(1)}, u32[]{:S(2)}, u32[]{:S(2)}) collective-permute-start(bf16[320,1024]{1,0:T(8,128)(2,1)S(1)} %add_convert_fusion.16), channel_id=1, source_target_pairs={{0,16},{1,17},{2,18},{3,19},{4,20},{5,21},{6,22},{7,23},{8,24},{9,... | collective-permute-start | bytes 1966088 | tf_op jit(solution)/shard_map/ppermute | solution.py:46
  (68 other events, 396.5 us)
Sparse Core Ops, SparseCore 0:
  863.5 295.5 all-reduce.6
Sparse Core Ops, SparseCore 1:
  933.1 42.2 all-gather.16
  987.5 41.5 all-gather.14
  1038.3 40.4 all-gather.8
  1090.3 39.8 all-gather.6
  1148.5 40.4 all-gather.12
  1192.0 41.1 all-gather.10

commit v2 on v0

v2 whole, which is shorter than its diff:
```python
import functools

import jax
import jax.numpy as jnp
from jax import lax
from jax.experimental import pallas as pl
from jax.experimental.pallas import tpu as pltpu
from jax.sharding import PartitionSpec as P


ALL_AXES = ("ep", "dp")
MESH = pl.DeviceIdType.MESH
STEPS = 2


def contract_rows(left, right):
    return lax.dot_general(left, right, (((0,), (0,)), ((), ())), preferred_element_type=jnp.float32)


def contract_cols(left, right):
    return lax.dot_general(left, right, (((1,), (1,)), ((), ())), preferred_element_type=jnp.float32)


def dot32(left, right):
    return jnp.dot(left, right, preferred_element_type=jnp.float32)


class Geometry:
    def __init__(self, ep, dp):
        self.ep, self.dp = ep, dp
        self.chips = (ep // 2) * (dp // 2)
        z, j = lax.axis_index("ep"), lax.axis_index("dp")
        self.core = j % 2
        self.local = j // 2
        self.base = (z // (ep // 2)) * (ep // 2)
        self.chip = (z % (ep // 2)) * (dp // 2) + j // 2
        self.me = 2 * self.chip + self.core
        self.sibling = (z, (j // 2) * 2 + 1 - self.core)
        self.partner = ((z + ep // 2) % ep, j)

    def member(self, index):
        return (self.base + index // self.dp, index % self.dp)

    def out_chip(self, step):
        return (self.chip + step) % self.chips

    def in_chip(self, step):
        return (self.chip - step + self.chips) % self.chips

    def entry_barrier(self):
        barrier = pltpu.get_barrier_semaphore()

        @pl.loop(1, self.chips)
        def _(step):
            for core in range(2):
                pl.semaphore_signal(barrier, inc=1, device_id=self.member(2 * self.out_chip(step) + core), device_id_type=MESH)

        for device in (self.sibling, self.partner):
            pl.semaphore_signal(barrier, inc=1, device_id=device, device_id_type=MESH)
        pl.semaphore_wait(barrier, 2 * self.chips)


class Outbound:
    def __init__(self, geo, send, recv, send_sem, recv_sem):
        self.geo, self.send, self.recv, self.send_sem, self.recv_sem = geo, send, recv, send_sem, recv_sem

    def copy(self, step, core):
        geo = self.geo
        index = 2 * geo.out_chip(step) + core
        return pltpu.make_async_remote_copy(src_ref=self.send.at[index], dst_ref=self.recv.at[step, geo.core], send_sem=self.send_sem.at[step, core], recv_sem=self.recv_sem.at[step, geo.core], device_id=geo.member(index), device_id_type=MESH)

    def own(self):
        geo = self.geo
        return pltpu.make_async_copy(self.send.at[geo.me], self.recv.at[0, geo.core], self.recv_sem.at[0, geo.core])

    def start(self):
        self.own().start()
        self.copy(0, 1 - self.geo.core).start()

        @pl.loop(1, self.geo.chips)
        def _(step):
            for core in range(2):
                self.copy(step, core).start()

    def wait_recv(self, step):
        for core in range(2):
            pltpu.make_async_copy(self.send.at[0], self.recv.at[step, core], self.recv_sem.at[step, core]).wait()

    def wait_sends(self):
        self.copy(0, 1 - self.geo.core).wait_send()

        @pl.loop(1, self.geo.chips)
        def _(step):
            for core in range(2):
                self.copy(step, core).wait_send()


class Return:
    def __init__(self, geo, rows, back, send_sem, recv_sem):
        self.geo, self.rows, self.back, self.send_sem, self.recv_sem = geo, rows, back, send_sem, recv_sem

    def copy(self, step, core):
        geo = self.geo
        return pltpu.make_async_remote_copy(src_ref=self.rows.at[step, core], dst_ref=self.back.at[geo.me], send_sem=self.send_sem.at[step, core], recv_sem=self.recv_sem.at[geo.me], device_id=geo.member(2 * geo.in_chip(step) + core), device_id_type=MESH)

    def start(self, step):
        geo = self.geo

        @pl.when(step == 0)
        def _():
            pltpu.make_async_copy(self.rows.at[0, geo.core], self.back.at[geo.me], self.recv_sem.at[geo.me]).start()
            self.copy(0, 1 - geo.core).start()

        @pl.when(step > 0)
        def _():
            for core in range(2):
                self.copy(step, core).start()

    def wait_all(self):
        geo = self.geo
        self.copy(0, 1 - geo.core).wait_send()

        @pl.loop(1, geo.chips)
        def _(step):
            for core in range(2):
                self.copy(step, core).wait_send()

        @pl.loop(0, 2 * geo.chips)
        def _(index):
            pltpu.make_async_copy(self.rows.at[0, 0], self.back.at[index], self.recv_sem.at[index]).wait()


def half_rows(rows, core):
    return pl.ds(pl.multiple_of(core * (rows // 2), 8), rows // 2)


class WeightSwap:
    def __init__(self, geo, layer, own, foreign, sems):
        self.geo, self.layer, self.own, self.foreign, self.sems = geo, layer, own, foreign, sems

    def over(self, which):
        geo = self.geo
        rows = half_rows(self.foreign[which].shape[0], geo.core)
        return pltpu.make_async_remote_copy(src_ref=self.own[which].at[self.layer, geo.local, rows], dst_ref=self.foreign[which].at[rows], send_sem=self.sems.at[0, which], recv_sem=self.sems.at[1, which], device_id=geo.partner, device_id_type=MESH)

    def across(self, which):
        geo = self.geo
        rows = self.foreign[which].at[half_rows(self.foreign[which].shape[0], geo.core)]
        return pltpu.make_async_remote_copy(src_ref=rows, dst_ref=rows, send_sem=self.sems.at[2, which], recv_sem=self.sems.at[3, which], device_id=geo.sibling, device_id_type=MESH)

    def start(self):
        for which in range(3):
            self.over(which).start()

    def pass_on(self):
        for which in range(3):
            self.over(which).wait()
            self.across(which).start()

    def finish(self):
        for which in range(3):
            self.across(which).wait()


def silu(value):
    return value * jax.nn.sigmoid(value)


def forward_kernel(ep, dp, send, mixed, *refs):
    refs = list(refs)

    def take(count):
        got = refs[:count]
        del refs[:count]
        return got

    experts, ws, got = take(3), take(3), take(3)
    recv_out, back, shared = take(3)
    keep_out, next_out = take(3), take(3)
    recv, outs = take(2)
    shared_w, own_w, foreign_w = take(3), take(3), take(3)
    go_sem, get_sem, ret_sem, res_sem, swap_sem, pass_sem, load_sem, save_sem = refs
    geo = Geometry(ep, dp)
    geo.entry_barrier()
    outbound = [Outbound(geo, send.at[part], recv.at[part], go_sem.at[part], get_sem.at[part]) for part in range(2)]
    returns = [Return(geo, outs.at[part], back.at[part], ret_sem.at[part], res_sem.at[part]) for part in range(2)]
    swap = WeightSwap(geo, 1, experts, next_out, swap_sem)
    outbound[0].start()
    loads = []
    passes = []
    for which in range(3):
        mine = half_rows(foreign_w[which].shape[0], geo.core)
        loads.append(pltpu.make_async_copy(ws[which].at[0], shared_w[which], load_sem.at[0, which]))
        loads.append(pltpu.make_async_copy(experts[which].at[0, geo.local], own_w[which], load_sem.at[1, which]))
        loads.append(pltpu.make_async_copy(got[which], foreign_w[which].at[mine], load_sem.at[2, which]))
        passes.append(pltpu.make_async_remote_copy(src_ref=got[which], dst_ref=foreign_w[which].at[mine], send_sem=pass_sem.at[0, which], recv_sem=pass_sem.at[1, which], device_id=geo.sibling, device_id_type=MESH))
    for copy in loads + passes:
        copy.start()
    outbound[1].start()
    swap.start()

    tile = 2 * STEPS * recv.shape[3]

    def ffn(rows, w_one, w_three, w_two):
        a_one = dot32(rows, w_one[...])
        a_three = dot32(rows, w_three[...])
        hidden = (silu(a_one) * a_three).astype(jnp.bfloat16)
        return dot32(hidden, w_two[...])

    for copy in loads + passes:
        copy.wait()

    @pl.loop(0, mixed.shape[0] // tile)
    def _(t):
        at = pl.ds(pl.multiple_of(t * tile, tile), tile)
        shared[at, :] = ffn(mixed[at, :], *shared_w)

    keeps = [pltpu.make_async_copy(src, dst, load_sem.at[0, which]) for which, (src, dst) in enumerate(zip(foreign_w, keep_out))]
    for keep in keeps:
        keep.start()
    width = mixed.shape[1]
    for part, weights in enumerate((own_w, foreign_w)):

        @pl.loop(0, geo.chips // STEPS)
        def _(t):
            steps = pl.ds(t * STEPS, STEPS)
            for step in range(STEPS):
                outbound[part].wait_recv(t * STEPS + step)
            pltpu.make_async_copy(recv.at[part, steps], recv_out.at[part, steps], save_sem.at[part, t]).start()
            rows = recv[part, steps].reshape(tile, width)
            outs[part, steps] = ffn(rows, *weights).astype(jnp.bfloat16).reshape(STEPS, 2, tile // (2 * STEPS), width)

            @pl.when(t > 0)
            def _():
                for step in range(STEPS):
                    returns[part].start((t - 1) * STEPS + step)

        for step in range(STEPS):
            returns[part].start(geo.chips - STEPS + step)
    swap.pass_on()
    for part in range(2):
        outbound[part].wait_sends()
        returns[part].wait_all()

        @pl.loop(0, geo.chips // STEPS)
        def _(t):
            steps = pl.ds(t * STEPS, STEPS)
            pltpu.make_async_copy(recv.at[part, steps], recv_out.at[part, steps], save_sem.at[part, t]).wait()

    for keep in keeps:
        keep.wait()
    swap.finish()


def forward_exchange(mesh, send, mixed, experts, shared, got):
    ep, dp = mesh.shape["ep"], mesh.shape["dp"]
    members, block, width = send.shape[1:]
    tokens = mixed.shape[0]
    bf16, f32 = jnp.bfloat16, jnp.float32
    shapes = [w.shape[2:] for w in experts]
    hidden = shapes[0][1]
    chips = members // 2
    anywhere = pl.BlockSpec(memory_space=pl.ANY)
    inside = pl.BlockSpec(memory_space=pltpu.VMEM)
    flops = 2 * 3 * width * hidden * (2 * members * block + tokens)
    expert = [jax.ShapeDtypeStruct(s, bf16) for s in shapes]
    dma = pltpu.SemaphoreType.DMA
    return pl.pallas_call(
        functools.partial(forward_kernel, ep, dp),
        name="forward_exchange",
        out_shape=[jax.ShapeDtypeStruct((2, chips, 2, block, width), bf16), jax.ShapeDtypeStruct((2, members, block, width), bf16), jax.ShapeDtypeStruct((tokens, width), f32)] + expert + expert,
        in_specs=[anywhere, inside] + [anywhere] * 9,
        out_specs=[anywhere, anywhere, inside] + [anywhere] * 6,
        scratch_shapes=[pltpu.VMEM((2, chips, 2, block, width), bf16) for _ in range(2)]
        + [pltpu.VMEM(s, bf16) for _ in range(3) for s in shapes]
        + [dma((2, chips, 2)), dma((2, chips, 2)), dma((2, chips, 2)), dma((2, members)), dma((4, 3)), dma((2, 3)), dma((3, 3)), dma((2, chips // STEPS))],
        compiler_params=pltpu.CompilerParams(collective_id=0, has_side_effects=True, vmem_limit_bytes=60 * 2**20),
        cost_estimate=pl.CostEstimate(flops=flops, bytes_accessed=40 * 2**20, transcendentals=0),
    )(send, mixed, *experts, *shared, *got)


class PairSum:
    def __init__(self, geo, stages, theirs, sems, expert):
        self.geo, self.stages, self.theirs, self.sems, self.expert = geo, stages, theirs, sems, expert

    def mine(self, which):
        return self.stages[which].at[self.expert, half_rows(self.stages[which].shape[1], self.geo.core)]

    def copy(self, which):
        geo = self.geo
        return pltpu.make_async_remote_copy(src_ref=self.stages[which].at[self.expert, half_rows(self.stages[which].shape[1], 1 - geo.core)], dst_ref=self.theirs[which].at[self.expert], send_sem=self.sems.at[0, self.expert, which], recv_sem=self.sems.at[1, self.expert, which], device_id=geo.sibling, device_id_type=MESH)

    def start(self):
        for which in range(3):
            self.copy(which).start()

    def finish(self):
        for which in range(3):
            self.copy(which).wait()
            mine = self.mine(which)
            mine[...] = (mine[...].astype(jnp.float32) + self.theirs[which][self.expert].astype(jnp.float32)).astype(jnp.bfloat16)


def backward_kernel(ep, dp, layer, *refs):
    refs = list(refs)

    def take(count):
        got = refs[:count]
        del refs[:count]
        return got

    held, send, mixed, grad_y = take(4)
    own_w, foreign_w, shared_w = take(3), take(3), take(3)
    back, shared_dx, recv = take(3)
    shared_out, own_out = take(3), take(3)
    x_buf, g_buf, dx_rows, dx_buf = take(4)
    weights, acc, stages, theirs, partner_in = take(3), take(3), take(3), take(3), take(3)
    go_sem, get_sem, ret_sem, res_sem, partner_sem, load_sem, x_sem, g_sem, dx_sem, pair_sem = refs

    geo = Geometry(ep, dp)
    geo.entry_barrier()
    tile = 2 * send.shape[2]
    width = mixed.shape[1]
    per_set = mixed.shape[0] // tile
    total = 3 * per_set
    outbound = [Outbound(geo, send.at[part], recv.at[part], go_sem.at[part], get_sem.at[part]) for part in range(2)]
    returns = [Return(geo, dx_rows.at[part], back.at[part], ret_sem.at[part], res_sem.at[part]) for part in range(2)]
    pairs = [PairSum(geo, stages, theirs, pair_sem, expert) for expert in range(2)]
    outbound[1].start()
    loads = []
    for which in range(3):
        loads.append(pltpu.make_async_copy(shared_w[which].at[layer], weights[which].at[2], load_sem.at[2, which]))
        loads.append(pltpu.make_async_copy(own_w[which].at[layer, geo.local], weights[which].at[0], load_sem.at[0, which]))
        loads.append(pltpu.make_async_copy(foreign_w[which], weights[which].at[1], load_sem.at[1, which]))
    for load in loads:
        load.start()
    outbound[0].start()
    moved, moved_sem, kept, kept_sem = (x_buf, x_sem, g_buf, g_sem) if layer else (g_buf, g_sem, x_buf, x_sem)

    def held_block(part, step, core):
        if layer:
            return held.at[2 * geo.in_chip(step) + core, part]
        return held.at[part, step, core]

    def fetch(i, slot):
        @pl.when(i < per_set)
        def _():
            at = pl.ds(pl.multiple_of(i * tile, tile), tile)
            pltpu.make_async_copy(mixed.at[at], x_buf.at[slot], x_sem.at[slot]).start()
            pltpu.make_async_copy(grad_y.at[at], g_buf.at[slot], g_sem.at[slot]).start()

        for part in range(2):
            begin = (2 - part) * per_set

            @pl.when((i >= begin) & (i < begin + per_set))
            def _(part=part, begin=begin):
                step = i - begin
                outbound[part].wait_recv(step)
                for core in range(2):
                    at = pl.ds(core * (tile // 2), tile // 2)
                    pltpu.make_async_copy(recv.at[part, step, core], moved.at[slot, at], moved_sem.at[slot]).start()
                    pltpu.make_async_copy(held_block(part, step, core), kept.at[slot, at], kept_sem.at[slot]).start()

    def store_shared(i):
        return pltpu.make_async_copy(dx_buf.at[i % 2], shared_dx.at[pl.ds(pl.multiple_of(i * tile, tile), tile)], dx_sem.at[i % 2])

    def partner_copies():
        return [pltpu.make_async_remote_copy(src_ref=pairs[1].mine(which), dst_ref=partner_in[which], send_sem=partner_sem.at[0, which], recv_sem=partner_sem.at[1, which], device_id=geo.partner, device_id_type=MESH) for which in range(3)]

    fetch(0, 0)
    for load in loads:
        load.wait()

    @pl.loop(0, total)
    def _(i):
        slot = i % 2
        which_set = 2 - i // per_set
        fetch(i + 1, (i + 1) % 2)
        pltpu.make_async_copy(mixed.at[pl.ds(0, tile)], x_buf.at[slot], x_sem.at[slot]).wait()
        pltpu.make_async_copy(mixed.at[pl.ds(0, tile)], g_buf.at[slot], g_sem.at[slot]).wait()

        @pl.when(i % per_set == 0)
        def _():
            for a in acc:
                a[...] = jnp.zeros(a.shape, jnp.float32)

        x = x_buf[slot]
        g = g_buf[slot]
        w_one, w_three, w_two = [w.at[which_set] for w in weights]
        a_one = dot32(x, w_one[...])
        a_three = dot32(x, w_three[...])
        grad_hidden = contract_cols(g, w_two[...])
        sigma = jax.nn.sigmoid(a_one)
        gated = a_one * sigma
        hidden = (gated * a_three).astype(jnp.bfloat16)
        grad_one = (grad_hidden * a_three * (sigma * (1.0 + a_one * (1.0 - sigma)))).astype(jnp.bfloat16)
        grad_three = (grad_hidden * gated).astype(jnp.bfloat16)
        acc[0][...] += contract_rows(x, grad_one)
        acc[1][...] += contract_rows(x, grad_three)
        acc[2][...] += contract_rows(hidden, g)
        dx = contract_cols(grad_one, w_one[...]) + contract_cols(grad_three, w_three[...])

        @pl.when(i < per_set)
        def _():
            pl.when(i >= 2)(lambda: store_shared(i - 2).wait())
            dx_buf[slot] = dx
            store_shared(i).start()

        @pl.when(i == per_set - 1)
        def _():
            for a, out in zip(acc, shared_out):
                out[...] = a[...].astype(jnp.bfloat16)

        for part in range(2):
            begin = (2 - part) * per_set

            @pl.when((i >= begin) & (i < begin + per_set))
            def _(part=part, begin=begin):
                dx_rows[part, i - begin] = dx.astype(jnp.bfloat16).reshape(2, tile // 2, width)

            @pl.when((i > begin) & (i <= begin + per_set))
            def _(part=part, begin=begin):
                returns[part].start(i - 1 - begin)

            @pl.when(i == begin + per_set - 1)
            def _(part=part):
                for a, stage in zip(acc, stages):
                    stage[part] = a[...].astype(jnp.bfloat16)

        pl.when(i == 2 * per_set)(pairs[1].start)
        pl.when(i == 2 * per_set + 1)(pairs[1].finish)

        @pl.when(i == 2 * per_set + 2)
        def _():
            for copy in partner_copies():
                copy.start()

    returns[0].start(per_set - 1)
    pairs[0].start()
    pairs[0].finish()
    for which, copy in enumerate(partner_copies()):
        copy.wait()
        own_out[which][...] = (pairs[0].mine(which)[...].astype(jnp.float32) + partner_in[which][...].astype(jnp.float32)).astype(jnp.bfloat16)
    store_shared(per_set - 2).wait()
    store_shared(per_set - 1).wait()
    for part in range(2):
        outbound[part].wait_sends()
        returns[part].wait_all()


def backward_exchange(mesh, layer, held, send, mixed, grad_y, own, foreign, shared):
    ep, dp = mesh.shape["ep"], mesh.shape["dp"]
    members, block, width = send.shape[1:]
    chips = members // 2
    tokens = mixed.shape[0]
    tile = 2 * block
    bf16, f32 = jnp.bfloat16, jnp.float32
    anywhere = pl.BlockSpec(memory_space=pl.ANY)
    inside = pl.BlockSpec(memory_space=pltpu.VMEM)
    shapes = [w.shape for w in foreign]
    halves = [(s[0] // 2, s[1]) for s in shapes]
    like = jax.ShapeDtypeStruct
    by_step = like((2, chips, 2, block, width), bf16)
    outs = [like((2, members, block, width), bf16), like((tokens, width), f32), by_step] + [like(s, bf16) for s in shapes + halves]
    vmem = pltpu.VMEM
    scratch = [vmem((2, tile, width), bf16), vmem((2, tile, width), bf16), vmem(by_step.shape, bf16), vmem((2, tile, width), f32)]
    scratch += [vmem((3,) + s, bf16) for s in shapes] + [vmem(s, f32) for s in shapes] + [vmem((2,) + s, bf16) for s in shapes]
    scratch += [vmem((2,) + s, bf16) for s in halves] + [vmem(s, bf16) for s in halves]
    dma = pltpu.SemaphoreType.DMA
    scratch += [dma((2, chips, 2)), dma((2, chips, 2)), dma((2, chips, 2)), dma((2, members)), dma((2, 3)), dma((3, 3)), dma((2,)), dma((2,)), dma((2,)), dma((2, 2, 3))]
    operands = [held, send, mixed, grad_y, *own, *foreign, *shared]
    flops = 2 * 8 * width * shapes[0][1] * (2 * members * block + tokens)
    return pl.pallas_call(
        functools.partial(backward_kernel, ep, dp, layer),
        name="backward_second" if layer else "backward_first",
        out_shape=outs,
        in_specs=[anywhere] * len(operands),
        out_specs=[anywhere] * 3 + [inside] * 6,
        scratch_shapes=scratch,
        compiler_params=pltpu.CompilerParams(collective_id=1 + layer, has_side_effects=True, vmem_limit_bytes=63 * 2**20),
        cost_estimate=pl.CostEstimate(flops=flops, bytes_accessed=60 * 2**20, transcendentals=0),
    )(*operands)


def final_kernel(ep, dp, *refs):
    refs = list(refs)

    def take(count):
        got = refs[:count]
        del refs[:count]
        return got

    halves, parts = take(3), take(4)
    full, sums = take(3), take(4)
    first, mine, wide, piece, other, last = [take(4) for _ in range(6)]
    load_sem, pair_sem, wide_send, wide_recv, partner_sem, spread_send, spread_recv, cross_sem, gather_send, gather_recv, local_sem, fold_sem = refs
    geo = Geometry(ep, dp)
    geo.entry_barrier()
    plane = dp // 2
    z, core = lax.axis_index("ep"), geo.core
    four, three = range(4), range(3)
    f32, bf16 = jnp.float32, jnp.bfloat16

    to_sibling = [pltpu.make_async_remote_copy(src_ref=parts[n].at[1 - core], dst_ref=first[n], send_sem=pair_sem.at[0, n], recv_sem=pair_sem.at[1, n], device_id=geo.sibling, device_id_type=MESH) for n in four]
    keep = [pltpu.make_async_copy(parts[n].at[core], mine[n], load_sem.at[n]) for n in four]
    for copy in to_sibling + keep:
        copy.start()

    def gather(n, step):
        to = (geo.local + step) % plane
        return pltpu.make_async_remote_copy(src_ref=halves[n], dst_ref=full[n].at[geo.local, core], send_sem=gather_send.at[n, step], recv_sem=gather_recv.at[n, step], device_id=(z, 2 * to + core), device_id_type=MESH)

    def gathered(n, step):
        return full[n].at[(geo.local - step + plane) % plane, core]

    def fold(n, step):
        return pltpu.make_async_remote_copy(src_ref=gathered(n, step), dst_ref=gathered(n, step), send_sem=fold_sem.at[0, n, step], recv_sem=fold_sem.at[1, n, step], device_id=geo.sibling, device_id_type=MESH)

    def fold_own(n):
        return pltpu.make_async_remote_copy(src_ref=halves[n], dst_ref=full[n].at[geo.local, core], send_sem=fold_sem.at[0, n, 0], recv_sem=fold_sem.at[1, n, 0], device_id=geo.sibling, device_id_type=MESH)

    local = [pltpu.make_async_copy(halves[n], full[n].at[geo.local, core], local_sem.at[n]) for n in three]

    for n in four:
        to_sibling[n].wait()
        keep[n].wait()
        mine[n][...] = (mine[n][...].astype(f32) + first[n][...].astype(f32)).astype(bf16)

    def widen(n, step):
        to = geo.out_chip(step)
        return pltpu.make_async_remote_copy(src_ref=mine[n].at[to], dst_ref=wide[n].at[step], send_sem=wide_send.at[n, step], recv_sem=wide_recv.at[n, step], device_id=geo.member(2 * to + core), device_id_type=MESH)

    for n in four:
        for step in range(1, geo.chips):
            widen(n, step).start()
    for n in three:
        local[n].start()
        fold_own(n).start()
        for step in range(1, plane):
            gather(n, step).start()
    for n in four:
        total = mine[n][geo.chip].astype(f32)
        for step in range(1, geo.chips):
            widen(n, step).wait()
            total += wide[n][step].astype(f32)
        piece[n][...] = total.astype(bf16)

    def swap(n):
        return pltpu.make_async_remote_copy(src_ref=piece[n], dst_ref=other[n], send_sem=partner_sem.at[0, n], recv_sem=partner_sem.at[1, n], device_id=geo.partner, device_id_type=MESH)

    for n in four:
        swap(n).start()
    for n in four:
        swap(n).wait()
        last[n][...] = (piece[n][...].astype(f32) + other[n][...].astype(f32)).astype(bf16)

    def spread(n, step):
        return pltpu.make_async_remote_copy(src_ref=last[n], dst_ref=sums[n].at[core, geo.chip], send_sem=spread_send.at[n, step], recv_sem=spread_recv.at[n, step], device_id=geo.member(2 * geo.out_chip(step) + core), device_id_type=MESH)

    own = [pltpu.make_async_copy(last[n], sums[n].at[core, geo.chip], load_sem.at[n]) for n in four]
    for n in four:
        own[n].start()
        for step in range(1, geo.chips):
            spread(n, step).start()
    for n in three:
        local[n].wait()
        fold_own(n).wait()
        for step in range(1, plane):
            gather(n, step).wait()
            fold(n, step).start()

    def cross(n):
        return pltpu.make_async_remote_copy(src_ref=sums[n].at[core], dst_ref=sums[n].at[core], send_sem=cross_sem.at[0, n], recv_sem=cross_sem.at[1, n], device_id=geo.sibling, device_id_type=MESH)

    for n in four:
        own[n].wait()
        for step in range(1, geo.chips):
            spread(n, step).wait()
        cross(n).start()
    for n in four:
        cross(n).wait()
    for n in three:
        for step in range(1, plane):
            fold(n, step).wait()


def final_exchange(mesh, halves, parts):
    ep, dp = mesh.shape["ep"], mesh.shape["dp"]
    chips, plane = ep * dp // 4, dp // 2
    bf16 = jnp.bfloat16
    anywhere = pl.BlockSpec(memory_space=pl.ANY)
    like = jax.ShapeDtypeStruct
    cut = [part.reshape(2, chips, part.shape[0] // (2 * chips), part.shape[1]) for part in parts]
    piece = [c.shape[2:] for c in cut]
    vmem, dma = pltpu.VMEM, pltpu.SemaphoreType.DMA
    scratch = [vmem((chips,) + s, bf16) for _ in range(3) for s in piece] + [vmem(s, bf16) for _ in range(3) for s in piece]
    scratch += [dma((4,)), dma((2, 4)), dma((4, chips)), dma((4, chips)), dma((2, 4)), dma((4, chips)), dma((4, chips)), dma((2, 4)), dma((3, plane)), dma((3, plane)), dma((3,)), dma((2, 3, plane))]
    outs = pl.pallas_call(
        functools.partial(final_kernel, ep, dp),
        name="final_exchange",
        out_shape=[like((plane, 2) + h.shape, bf16) for h in halves] + [like(c.shape, bf16) for c in cut],
        in_specs=[anywhere] * 7,
        out_specs=[anywhere] * 7,
        scratch_shapes=scratch,
        compiler_params=pltpu.CompilerParams(collective_id=3, has_side_effects=True, vmem_limit_bytes=40 * 2**20),
        cost_estimate=pl.CostEstimate(flops=10**10, bytes_accessed=30 * 2**20, transcendentals=0),
    )(*halves, *cut)
    full = [out.reshape(plane, 2 * out.shape[2], out.shape[3]) for out in outs[:3]]
    return full, [out.reshape(part.shape) for out, part in zip(outs[3:], parts)]


def take_rows(source, index):
    return jnp.take(source, index, axis=0, mode="clip")


def solution(mesh):
    tok_spec = P(ALL_AXES, None)
    route_spec = P(None, ALL_AXES, None)
    exp_spec = P(None, "ep", None, None)
    repl_spec = P(None, None, None)
    ep, dp = mesh.shape["ep"], mesh.shape["dp"]
    members = ep * dp // 2
    to_partner = [(d, (d + members) % (2 * members)) for d in range(2 * members)]
    groups = [[side * members + m for m in range(members)] for side in range(2)]

    def body(act_in, grad_out, slot_ids, gate_vals, w_dense, w_gate, w_up, w_down, ws_gate, ws_up, ws_down):
        tokens, width = act_in.shape
        slots = 2 * tokens
        block = tokens // members
        experts = (w_gate, w_up, w_down)
        shared = (ws_gate, ws_up, ws_down)
        core, local = lax.axis_index("dp") % 2, lax.axis_index("dp") // 2

        got = []
        for w in experts:
            rows, columns = w.shape[2] // 2, w.shape[3]
            mine = lax.dynamic_slice(w, (0, local, core * rows, 0), (1, 1, rows, columns)).reshape(rows, columns)
            got.append(lax.ppermute(mine, ALL_AXES, to_partner))

        side = lax.axis_index("ep") // (ep // 2)
        turned = (slot_ids.reshape(2, tokens) + side * tokens) % slots
        flat = (turned + jnp.arange(2, dtype=jnp.int32)[:, None] * slots).reshape(-1)
        token_ids = jnp.tile(jnp.arange(tokens, dtype=jnp.int32), 2)
        owner = jnp.full((2 * slots,), tokens, jnp.int32).at[flat].set(token_ids, unique_indices=True).reshape(2, 2, members, block)

        def extended(rows):
            return jnp.pad(rows, ((0, 8), (0, 0)))

        def to_slots(layer, rows):
            return take_rows(extended(rows), owner[layer].reshape(-1)).reshape(2, members, block, width)

        def from_slots(layer, back):
            return take_rows(back.reshape(slots, width), turned[layer]).astype(jnp.float32)

        def mix(act, layer):
            return (act.astype(jnp.float32) + dot32(act, w_dense[layer])).astype(jnp.bfloat16)

        def gated(grad, layer):
            return (gate_vals[layer] * grad.astype(jnp.float32)).astype(jnp.bfloat16)

        by_member = owner[1].transpose(1, 0, 2).reshape(-1)
        grads_two = take_rows(extended(gated(grad_out, 1)), by_member).reshape(members, 2, block, width)
        mixed_one = mix(act_in, 0)
        sent_one = to_slots(0, mixed_one)
        sent_one, grads_two = lax.optimization_barrier((sent_one, grads_two))
        recv, back, shared_y, *foreign = forward_exchange(mesh, sent_one, mixed_one, experts, shared, got)
        back, grads_two = lax.optimization_barrier((back, grads_two))
        grads_two = lax.all_to_all(grads_two, ALL_AXES, 0, 0, axis_index_groups=groups)
        routed = from_slots(0, back)
        act_two = (mixed_one.astype(jnp.float32) + gate_vals[0] * routed + shared_y).astype(jnp.bfloat16)
        mixed_two = mix(act_two, 1)

        def finish(layer, act, grad_y, back, shared_dx):
            routed = from_slots(layer, back)
            grad_mixed = (grad_y.astype(jnp.float32) + routed + shared_dx).astype(jnp.bfloat16)
            g_dense = contract_rows(act, grad_mixed).astype(jnp.bfloat16)
            return (grad_mixed.astype(jnp.float32) + contract_cols(grad_mixed, w_dense[layer])).astype(jnp.bfloat16), g_dense

        def gather(half):
            return lax.all_gather(half, "dp", axis=0, tiled=True).reshape((dp // 2, 2 * half.shape[0], half.shape[1]))

        out = backward_exchange(mesh, 1, grads_two, to_slots(1, mixed_two), mixed_two, grad_out, experts, foreign[3:], shared)
        shared_two, own_two = out[3:6], out[6:9]
        experts_two = [gather(half) for half in own_two]
        grad_one, dense_two = finish(1, act_two, grad_out, out[0], out[1])
        sums_two = [lax.psum(part, ALL_AXES) for part in (dense_two, *shared_two)]

        out = backward_exchange(mesh, 0, recv, to_slots(0, gated(grad_one, 0)), mixed_one, grad_one, experts, foreign[:3], shared)
        shared_one, own_one = out[3:6], out[6:9]
        grad_act, dense_one = finish(0, act_in, grad_one, out[0], out[1])
        experts_one, sums_one = final_exchange(mesh, own_one, [dense_one, *shared_one])

        expert_out = [jnp.stack(pair) for pair in zip(experts_one, experts_two)]
        sums_out = [jnp.stack(pair) for pair in zip(sums_one, sums_two)]
        return (grad_act, sums_out[0], *expert_out, *sums_out[1:])

    return jax.shard_map(body, mesh=mesh, in_specs=(tok_spec, tok_spec, route_spec, route_spec, repl_spec, exp_spec, exp_spec, exp_spec, repl_spec, repl_spec, repl_spec), out_specs=(tok_spec, repl_spec, exp_spec, exp_spec, exp_spec, repl_spec, repl_spec, repl_spec), check_vma=False)
```

time: 1780 us -> 1070 us (0.60)
  waiting for transfers between devices: 900 us -> 48.2 us
  Pallas kernels: 0 us -> 779 us
  matrix products: 376 us -> 21.9 us
  blocking collectives: 241 us -> 0 us
  local copies, waits for them, and re-layouts: 166 us -> 140 us
    pallas_call x0 -> x4, Pallas kernels: none -> 779 us  [the longest x2 400 us: backward_exchange(): pl.pallas_call(functools.partial(backward_kernel, ep, dp, layer), name='b...]
    psum x2 -> x1, waiting for transfers between devices: 522 us -> 0.01 us  [body(): sums_two = [lax.psum(part, ALL_AXES) for part in (dense_two, *shared_two)]]
    all_to_all x5 -> x1, waiting for transfers between devices: 378 us -> 32.1 us  [body(): lax.all_to_all(grads_two, ALL_AXES, 0, 0, axis_index_groups=groups)]
    dot_general x24 -> x2, matrix products: 275 us -> 7.74 us  [dot32(): return jnp.dot(left, right, preferred_element_type=jnp.float32)]
    all_to_all x2 -> x0, blocking collectives: 241 us -> none  [layer_front(): lax.all_to_all(send_buf, 'ep', 0, 1)]
    dot_general x8 -> x2, matrix products: 63.8 us -> 8.79 us  [contract_cols(): lax.dot_general(left, right, (((1,), (1,)), ((), ())), preferred_element_...]
    dot_general x8 -> x2, matrix products: 36.6 us -> 5.38 us  [contract_rows(): lax.dot_general(left, right, (((0,), (0,)), ((), ())), preferred_element_...]
    all_to_all x5 -> x1, starting transfers between devices: 26.6 us -> 4.59 us  [body(): lax.all_to_all(grads_two, ALL_AXES, 0, 0, axis_index_groups=groups)]
  transfers between devices with their start and end apart: 7 -> 8, of which waited for: 7 -> 3; matrix products, arithmetic and copies ran while one was open for 13% -> 16% of each run, Pallas kernels for 0% -> 36%
where the time goes in v2:
time: 1070 us
  Pallas kernels  779 us (73%)
  local copies, waits for them, and re-layouts  140 us (13%)
  other arithmetic  48.3 us (5%)
  waiting for transfers between devices  48.2 us (5%)
  matrix products  21.9 us (2%)
  between operations  16.4 us (2%)
  starting transfers between devices  11.8 us (1%)
    pallas_call x2, Pallas kernels, backward_exchange(): pl.pallas_call(functools.partial(backward_kernel, ep, dp, layer), name='b...  400 us
    pallas_call x1, Pallas kernels, forward_exchange(): pl.pallas_call(functools.partial(forward_kernel, ep, dp), name='forward_e...  200 us
    pallas_call x1, Pallas kernels, final_exchange(): pl.pallas_call(functools.partial(final_kernel, ep, dp), name='final_excha...  180 us
    gather x7, local copies, waits for them, and re-layouts, take_rows(): return jnp.take(source, index, axis=0, mode='clip')  110 us
    all_to_all x1, waiting for transfers between devices, body(): lax.all_to_all(grads_two, ALL_AXES, 0, 0, axis_index_groups=groups)  32.1 us
    another operation x3, other arithmetic, body(): expert_out = [jnp.stack(pair) for pair in zip(experts_one, experts_two)]  27.4 us
  transfers between devices with their start and end apart: 8, of which 3 were waited for; matrix products, arithmetic and copies ran while one was open for 16% of the time, Pallas kernels for 36%

profile of v2, /device:TPU:0, one launch (start us, length us, event | category | flops | bytes accessed | tf_op | source)
XLA Modules:
  0.0 1066.4 jit_solution(5591961137765066307)
XLA Ops:
  8.1 1.3 dynamic-slice_bitcast_fusion.2
  9.3 4.1 collective-permute-start
  13.4 2.0 dynamic-slice_bitcast_fusion.1
  15.4 0.0 collective-permute-start.1
  15.4 2.0 dynamic-slice_bitcast_fusion
  17.4 2.9 collective-permute-start.2
  20.3 0.1 broadcast_bitcast_fusion
  20.5 0.1 compare_select_fusion
  20.6 15.5 %scatter_custom_fusion = s32[8192]{0:T(1024)S(1)} fusion(s32[4096]{0:T(1024)S(1)} %bitcast.109, s32[4096]{0:T(1024)S(1)} %bitcast.110, s32[]{:T(128)} %constant.60.clone.1), kind=kCustom, calls=%fused_computation.57 | custom fusion | bytes 32772 | tf_op jit(solution)/shard_map/scatter | solution.py:644
  36.2 5.0 add_convert_fusion.4.mixed.refs_2_
  41.3 0.0 copy-start.10
  41.3 1.7 pad.13
  43.0 0.9 copy-done.10
  43.9 1.0 copy-done.8
  44.9 0.5 fusion
  45.4 0.2 pad.14
  45.7 20.2 %gather_fusion = bf16[4096,640]{1,0:T(8,128)(2,1)} fusion(bf16[2056,640]{1,0:T(8,128)(2,1)} %pad.13, s32[4096]{0:T(1024)S(1)} %get-tuple-element.86), kind=kCustom, calls=%fused_computation | custom fusion | bytes 10502144 | tf_op jit(solution)/shard_map/jit(_take)/gather | solution.py:613
  65.9 17.6 %gather_fusion.1 = bf16[4096,640]{1,0:T(8,128)(2,1)} fusion(bf16[2056,640]{1,0:T(8,128)(2,1)S(1)} %pad.14, s32[4096]{0:T(1024)S(1)} %broadcast_clamp_fusion.1), kind=kCustom, calls=%fused_computation.1 | custom fusion | bytes 10502144 | tf_op jit(solution)/shard_map/jit(_take)/gather | solution.py:613
  83.5 1.8 collective-permute-done.1.refs_7_
  85.3 13.2 %collective-permute-done.2.refs_8_ = bf16[512,640]{1,0:T(8,128)(2,1)} collective-permute-done((bf16[512,640]{1,0:T(8,128)(2,1)}, bf16[512,640]{1,0:T(8,128)(2,1)}, u32[]{:S(2)}, u32[]{:S(2)}) %collective-permute-start.2) | collective-permute-done | bytes 655392 | tf_op jit(solution)/shard_map/ppermute | solution.py:638
  98.5 200.2 %forward_exchange.1 = (bf16[2,8,2,128,640]{4,3,2,1,0:T(8,128)(2,1)}, bf16[2,16,128,640]{3,2,1,0:T(8,128)(2,1)}, f32[2048,640]{1,0:T(8,128)}, bf16[640,1024]{1,0:...) custom-call(bf16[2,16,128,640]{3,2,1,0:T(8,128)(2,1)} %bitcast.94, ...), custom_call_target="tpu_custom_call" | custom-call | flops 24159191040 | bytes 41943040 | tf_op jit(solution)/shard_map/forward_exchange/pallas_call | solution.py:268
  298.7 4.6 all-to-all-start
  303.3 0.0 all-reduce.7.cloned.1.call-start
  303.4 0.0 copy-start.22
  303.4 0.0 copy-start.11
  303.5 13.0 %gather_fusion.2 = bf16[2048,640]{1,0:T(8,128)(2,1)} fusion(bf16[4096,640]{1,0:T(8,128)(2,1)} %bitcast.84, s32[2048]{0:T(1024)S(1)} %broadcast_clamp_fusion.3), kind=kCustom, calls=%fused_computation.2 | custom fusion | bytes 5251072 | tf_op jit(solution)/shard_map/jit(_take)/gather | solution.py:613
  316.5 3.9 add_convert_fusion.3
  320.5 2.7 add_convert_fusion.2.refs_2_
  323.2 0.2 pad.15
  323.4 1.2 copy-done.12
  324.7 17.6 %gather_fusion.3 = bf16[4096,640]{1,0:T(8,128)(2,1)} fusion(bf16[2056,640]{1,0:T(8,128)(2,1)S(1)} %pad.15, s32[4096]{0:T(1024)S(1)} %get-tuple-element.84), kind=kCustom, calls=%fused_computation.3 | custom fusion | bytes 10502144 | tf_op jit(solution)/shard_map/jit(_take)/gather | solution.py:613
  342.3 32.1 %all-to-all-done.refs_0_ = bf16[16,2,128,640]{3,2,1,0:T(8,128)(2,1)} async-done(((bf16[16,2,128,640]{3,2,1,0:T(8,128)(2,1)}), bf16[16,2,128,640]{3,2,1,0:T(8,128)(2,1)}, u32[]{:S(2)}, u32[]{:S(2)}) %all-to-all-start) | async-done | bytes 5242912 | tf_op jit(solution)/shard_map/all_to_all | solution.py:668
  374.4 195.5 %backward_second.1 = (bf16[2,16,128,640]{3,2,1,0:T(8,128)(2,1)}, f32[2048,640]{1,0:T(8,128)}, bf16[2,8,2,128,640]{4,3,2,1,0:T(8,128)(2,1)}, bf16[640,1024]{1,0:T...) custom-call(bf16[16,2,128,640]{3,2,1,0:T(8,128)(2,1)} %all-to-all-do, ...), custom_call_target="tpu_custom_call" | custom-call | flops 64424509440 | bytes 62914560 | tf_op jit(solution)/shard_map/backward_second/pallas_call | solution.py:473
  569.9 13.2 %gather_fusion.4 = bf16[2048,640]{1,0:T(8,128)(2,1)} fusion(bf16[4096,640]{1,0:T(8,128)(2,1)} %bitcast.85, s32[2048]{0:T(1024)S(1)} %broadcast_clamp_fusion.2), kind=kCustom, calls=%fused_computation.4 | custom fusion | bytes 5251072 | tf_op jit(solution)/shard_map/jit(_take)/gather | solution.py:613
  583.1 4.3 fusion.2
  587.4 3.1 fusion.6
  590.6 0.0 all-reduce.7.cloned.1.call-update
  590.6 0.0 all-gather.8.cloned.1.call-start
  590.6 0.5 all-gather.8.cloned.1.call-update
  591.2 0.0 all-gather.6.cloned.1.call-start
  591.2 0.5 all-gather.6.cloned.1.call-update
  591.7 0.0 all-gather.4.cloned.1.call-start
  591.8 0.5 copy-done.14
  592.3 4.9 fusion.3
  597.2 0.2 pad.16
  597.4 0.5 copy-done.21
  597.9 17.6 %gather_fusion.5 = bf16[4096,640]{1,0:T(8,128)(2,1)} fusion(bf16[2056,640]{1,0:T(8,128)(2,1)S(1)} %pad.16, s32[4096]{0:T(1024)S(1)} %copy-done.21), kind=kCustom, calls=%fused_computation.5 | custom fusion | bytes 10502144 | tf_op jit(solution)/shard_map/jit(_take)/gather | solution.py:613
  615.5 0.0 all-gather.4.cloned.1.call-update
  615.5 204.2 %backward_first.1 = (bf16[2,16,128,640]{3,2,1,0:T(8,128)(2,1)}, f32[2048,640]{1,0:T(8,128)}, bf16[2,8,2,128,640]{4,3,2,1,0:T(8,128)(2,1)}, bf16[640,1024]{1,0:T(...) custom-call(bf16[2,8,2,128,640]{4,3,2,1,0:T(8,128)(2,1)} %get-tuple-, ...), custom_call_target="tpu_custom_call" | custom-call | flops 64424509440 | bytes 62914560 | tf_op jit(solution)/shard_map/backward_first/pallas_call | solution.py:473
  819.7 11.1 %gather_fusion.6 = bf16[2048,640]{1,0:T(8,128)(2,1)S(1)} fusion(bf16[4096,640]{1,0:T(8,128)(2,1)} %bitcast.86, s32[2048]{0:T(1024)S(1)} %copy-done.23), kind=kCustom, calls=%fused_computation.6 | custom fusion | bytes 5251072 | tf_op jit(solution)/shard_map/jit(_take)/gather | solution.py:613
  830.8 5.1 fusion.5
  835.9 3.9 add_convert_fusion
  839.9 2.2 convolution_convert_fusion.1
  842.2 0.1 copy-done.6
  842.3 0.3 copy-done.7
  842.6 179.6 %final_exchange.1 = (bf16[4,2,320,1024]{3,2,1,0:T(8,128)(2,1)}, bf16[4,2,320,1024]{3,2,1,0:T(8,128)(2,1)}, bf16[4,2,512,640]{3,2,1,0:T(8,128)(2,1)}, bf16[2,8,40...) custom-call(bf16[320,1024]{1,0:T(8,128)(2,1)S(1)} %copy-done.5, ...), custom_call_target="tpu_custom_call" | custom-call | flops 10000000000 | bytes 31457280 | tf_op jit(solution)/shard_map/final_exchange/pallas_call | solution.py:598
  1022.3 1.0 copy-done
  1023.3 2.6 pad_maximum_fusion.6
  1026.0 1.8 pad_maximum_fusion.5
  1027.7 0.9 copy-done.18
  1028.6 2.6 pad_maximum_fusion.3
  1031.2 9.2 pad_maximum_fusion.2
  1040.4 9.1 pad_maximum_fusion.1
  1049.5 9.1 pad_maximum_fusion
  (66 shorter events, 0.3 us)
Async XLA Ops:
  8.0 12.5 %copy-start.24 = (s32[2,2048,1]{1,2,0:T(1,128)S(1)}, s32[2,2048,1]{1,2,0:T(1,128)}, u32[]{:S(2)}) copy-start(s32[2,2048,1]{1,2,0:T(1,128)} %param.13) | copy-start | bytes 49156
  8.0 28.2 %copy-start.25 = (f32[2,2048,1]{1,2,0:T(1,128)S(1)}, f32[2,2048,1]{1,2,0:T(1,128)}, u32[]{:S(2)}) copy-start(f32[2,2048,1]{1,2,0:T(1,128)} %param.14) | copy-start | bytes 49156
  8.0 28.2 %copy-start.27 = (bf16[2,640,640]{2,1,0:T(8,128)(2,1)S(1)}, bf16[2,640,640]{2,1,0:T(8,128)(2,1)}, u32[]{:S(2)}) copy-start(bf16[2,640,640]{2,1,0:T(8,128)(2,1)} %param.15) | copy-start | bytes 4915204
  9.3 74.2 %collective-permute-start = (bf16[320,1024]{1,0:T(8,128)(2,1)S(1)}, bf16[320,1024]{1,0:T(8,128)(2,1)}, u32[]{:S(2)}, u32[]{:S(2)}) collective-permute-start(bf16[320,1024]{1,0:T(8,128)(2,1)S(1)} %dynamic-slice_bitcast_fusion.2), channel_id=1, source_target_pairs={{0,16},{1,17},{2,18},{3,19},{4,20},{5,21},{6,22},{7,23},{8,24},{9,... | collective-permute-start | bytes 1966088 | tf_op jit(solution)/shard_map/ppermute | solution.py:638
  15.4 69.9 %collective-permute-start.1 = (bf16[320,1024]{1,0:T(8,128)(2,1)}, bf16[320,1024]{1,0:T(8,128)(2,1)}, u32[]{:S(2)}, u32[]{:S(2)}) collective-permute-start(bf16[320,1024]{1,0:T(8,128)(2,1)} %dynamic-slice_bitcast_fusion.1), channel_id=1, source_target_pairs={{0,16},{1,17},{2,18},{3,19},{4,20},{5,21},{6,22},{7,23},{8,24},{9,... | collective-permute-start | bytes 1966088 | tf_op jit(solution)/shard_map/ppermute | solution.py:638
  17.4 81.1 %collective-permute-start.2 = (bf16[512,640]{1,0:T(8,128)(2,1)}, bf16[512,640]{1,0:T(8,128)(2,1)}, u32[]{:S(2)}, u32[]{:S(2)}) collective-permute-start(bf16[512,640]{1,0:T(8,128)(2,1)} %dynamic-slice_bitcast_fusion), channel_id=1, source_target_pairs={{0,16},{1,17},{2,18},{3,19},{4,20},{5,21},{6,22},{7,23},{8,24},{9,... | collective-permute-start | bytes 1966088 | tf_op jit(solution)/shard_map/ppermute | solution.py:638
  36.1 9.5 copy-start.20
  41.3 2.7 copy-start.10
  41.3 3.6 copy-start.8
  298.7 75.7 %all-to-all-start = ((bf16[16,2,128,640]{3,2,1,0:T(8,128)(2,1)}), bf16[16,2,128,640]{3,2,1,0:T(8,128)(2,1)}, u32[]{:S(2)}, u32[]{:S(2)}) async-start(bf16[16,2,128,640]{3,2,1,0:T(8,128)(2,1)} %bitcast.87), calls=%async_computation | async-start | bytes 10485760 | tf_op jit(solution)/shard_map/all_to_all | solution.py:668
  303.3 720.0 %all-reduce.7.cloned.1.call-start = ((), (), s32[]{:S(2)}) async-start(), calls=%async_computation.4 | async-start | bytes 9502720 | tf_op jit(solution)/shard_map/psum | solution.py:686
  303.4 13.1 %copy-start.22 = (s32[2048]{0:T(1024)}, s32[2048]{0:T(1024)S(1)}, u32[]{:S(2)}) copy-start(s32[2048]{0:T(1024)S(1)} %broadcast_clamp_fusion.3) | copy-start | bytes 24580
  303.4 13.1 %copy-start.11 = (bf16[2048,640]{1,0:T(8,128)(2,1)S(1)}, bf16[2048,640]{1,0:T(8,128)(2,1)}, u32[]{:S(2)}) copy-start(bf16[2048,640]{1,0:T(8,128)(2,1)} %copy-done.10) | copy-start | bytes 7864324
  316.5 4.0 copy-start.28
  320.5 2.7 copy-start.15
  323.2 1.5 copy-start.12
  569.9 13.2 %copy-start.9 = (bf16[2048,640]{1,0:T(8,128)(2,1)S(1)}, bf16[2048,640]{1,0:T(8,128)(2,1)}, u32[]{:S(2)}) copy-start(bf16[2048,640]{1,0:T(8,128)(2,1)} %refs_3_.3) | copy-start | bytes 7864324
  583.1 4.3 copy-start.16
  587.4 3.2 copy-start.13
  590.6 1.7 copy-start.14
  590.6 440.6 %all-gather.8.cloned.1.call-start = ((), (), s32[]{:S(2)}) async-start(), calls=%async_computation.3 | async-start | bytes 5898240 | tf_op jit(solution)/shard_map/all_gather | solution.py:680
  591.2 449.3 %all-gather.6.cloned.1.call-start = ((), (), s32[]{:S(2)}) async-start(), calls=%async_computation.2 | async-start | bytes 5898240 | tf_op jit(solution)/shard_map/all_gather | solution.py:680
  591.7 457.8 %all-gather.4.cloned.1.call-start = ((), (), s32[]{:S(2)}) async-start(), calls=%async_computation.1 | async-start | bytes 5898240 | tf_op jit(solution)/shard_map/all_gather | solution.py:680
  597.2 0.7 copy-start.21
  615.5 204.2 %copy-start.23 = (s32[2048]{0:T(1024)S(1)}, s32[2048]{0:T(1024)}, u32[]{:S(2)}) copy-start(s32[2048]{0:T(1024)} %copy-done.22) | copy-start | bytes 24580
  830.8 5.1 copy-start.29
  835.9 3.9 copy-start.26
  839.9 2.3 copy-start.2
  839.9 2.3 copy-start.3
  839.9 2.3 copy-start.4
  839.9 2.3 copy-start.5
  839.9 2.4 copy-start.6
  839.9 2.7 copy-start.7
  1022.2 1.1 copy-start
  1023.3 2.6 copy-start.1
  1023.3 2.6 copy-start.19
  1025.9 1.8 copy-start.17
  1025.9 2.7 copy-start.18
Sparse Core Ops, SparseCore 0:
  590.7 378.8 all-reduce.6
Sparse Core Ops, SparseCore 1:
  592.9 115.0 all-gather.7
  709.8 86.2 all-gather.5
  797.9 51.5 all-gather.3

commit v3 on v2

--- a/solution.py
+++ b/solution.py
@@ -11,6 +11,11 @@
 ALL_AXES = ("ep", "dp")
 MESH = pl.DeviceIdType.MESH
 STEPS = 2
+ORDER = (0, 7, 3, 4, 5, 2, 1, 6)
+ORDER_CODE = sum(mask * 8**step for step, mask in enumerate(ORDER))
+AT_ONCE = (1, 2, 4, 6)
+RELEASED = ((1, 3), (2, 5), (4, 7))
+EARLY = (1, 2, 4)
 
 
 def contract_rows(left, right):
@@ -41,19 +46,23 @@
     def member(self, index):
         return (self.base + index // self.dp, index % self.dp)
 
-    def out_chip(self, step):
-        return (self.chip + step) % self.chips
-
-    def in_chip(self, step):
-        return (self.chip - step + self.chips) % self.chips
+    def across(self, mask):
+        total = 0
+        for bit in (1, 2, 4):
+            total += (self.chip // bit + mask // bit) % 2 * bit
+        return total
+
+    def at_step(self, step):
+        power = (1 + 7 * (step % 2)) * (1 + 63 * (step // 2 % 2)) * (1 + 4095 * (step // 4))
+        return self.across(ORDER_CODE // power % 8)
 
     def entry_barrier(self):
         barrier = pltpu.get_barrier_semaphore()
 
         @pl.loop(1, self.chips)
-        def _(step):
+        def _(mask):
             for core in range(2):
-                pl.semaphore_signal(barrier, inc=1, device_id=self.member(2 * self.out_chip(step) + core), device_id_type=MESH)
+                pl.semaphore_signal(barrier, inc=1, device_id=self.member(2 * self.across(mask) + core), device_id_type=MESH)
 
         for device in (self.sibling, self.partner):
             pl.semaphore_signal(barrier, inc=1, device_id=device, device_id_type=MESH)
@@ -66,25 +75,29 @@
 
     def copy(self, step, core):
         geo = self.geo
-        index = 2 * geo.out_chip(step) + core
+        index = 2 * geo.at_step(step) + core
         return pltpu.make_async_remote_copy(src_ref=self.send.at[index], dst_ref=self.recv.at[step, geo.core], send_sem=self.send_sem.at[step, core], recv_sem=self.recv_sem.at[step, geo.core], device_id=geo.member(index), device_id_type=MESH)
 
-    def own(self):
+    def start(self):
         geo = self.geo
-        return pltpu.make_async_copy(self.send.at[geo.me], self.recv.at[0, geo.core], self.recv_sem.at[0, geo.core])
-
-    def start(self):
-        self.own().start()
-        self.copy(0, 1 - self.geo.core).start()
-
-        @pl.loop(1, self.geo.chips)
-        def _(step):
-            for core in range(2):
-                self.copy(step, core).start()
-
-    def wait_recv(self, step):
+        pltpu.make_async_copy(self.send.at[geo.me], self.recv.at[0, geo.core], self.recv_sem.at[0, geo.core]).start()
+        self.copy(0, 1 - geo.core).start()
+        for step in AT_ONCE:
+            self.issue(step)
+
+    def issue(self, step):
+        for core in range(2):
+            self.copy(step, core).start()
+
+    def arrive(self, step):
         for core in range(2):
             pltpu.make_async_copy(self.send.at[0], self.recv.at[step, core], self.recv_sem.at[step, core]).wait()
+        for trigger, later in RELEASED:
+            if isinstance(step, int):
+                if step == trigger:
+                    self.issue(later)
+            else:
+                pl.when(step == trigger)(functools.partial(self.issue, later))
 
     def wait_sends(self):
         self.copy(0, 1 - self.geo.core).wait_send()
@@ -101,7 +114,7 @@
 
     def copy(self, step, core):
         geo = self.geo
-        return pltpu.make_async_remote_copy(src_ref=self.rows.at[step, core], dst_ref=self.back.at[geo.me], send_sem=self.send_sem.at[step, core], recv_sem=self.recv_sem.at[geo.me], device_id=geo.member(2 * geo.in_chip(step) + core), device_id_type=MESH)
+        return pltpu.make_async_remote_copy(src_ref=self.rows.at[step, core], dst_ref=self.back.at[geo.me], send_sem=self.send_sem.at[step, core], recv_sem=self.recv_sem.at[geo.me], device_id=geo.member(2 * geo.at_step(step) + core), device_id_type=MESH)
 
     def start(self, step):
         geo = self.geo
@@ -225,7 +238,7 @@
         def _(t):
             steps = pl.ds(t * STEPS, STEPS)
             for step in range(STEPS):
-                outbound[part].wait_recv(t * STEPS + step)
+                outbound[part].arrive(t * STEPS + step)
             pltpu.make_async_copy(recv.at[part, steps], recv_out.at[part, steps], save_sem.at[part, t]).start()
             rows = recv[part, steps].reshape(tile, width)
             outs[part, steps] = ffn(rows, *weights).astype(jnp.bfloat16).reshape(STEPS, 2, tile // (2 * STEPS), width)
@@ -339,7 +352,7 @@
 
     def held_block(part, step, core):
         if layer:
-            return held.at[2 * geo.in_chip(step) + core, part]
+            return held.at[2 * geo.at_step(step) + core, part]
         return held.at[part, step, core]
 
     def fetch(i, slot):
@@ -355,7 +368,8 @@
             @pl.when((i >= begin) & (i < begin + per_set))
             def _(part=part, begin=begin):
                 step = i - begin
-                outbound[part].wait_recv(step)
+                early = (step == EARLY[0]) | (step == EARLY[1]) | (step == EARLY[2])
+                pl.when(jnp.logical_not(early))(lambda: outbound[part].arrive(step))
                 for core in range(2):
                     at = pl.ds(core * (tile // 2), tile // 2)
                     pltpu.make_async_copy(recv.at[part, step, core], moved.at[slot, at], moved_sem.at[slot]).start()
@@ -375,6 +389,9 @@
     def _(i):
         slot = i % 2
         which_set = 2 - i // per_set
+        for part, ahead in ((1, 3), (0, per_set + 4)):
+            for n, step in enumerate(EARLY):
+                pl.when(i == ahead + 2 * n)(functools.partial(outbound[part].arrive, step))
         fetch(i + 1, (i + 1) % 2)
         pltpu.make_async_copy(mixed.at[pl.ds(0, tile)], x_buf.at[slot], x_sem.at[slot]).wait()
         pltpu.make_async_copy(mixed.at[pl.ds(0, tile)], g_buf.at[slot], g_sem.at[slot]).wait()
@@ -493,10 +510,9 @@
     halves, parts = take(3), take(4)
     full, sums = take(3), take(4)
     first, mine, wide, piece, other, last = [take(4) for _ in range(6)]
-    load_sem, pair_sem, wide_send, wide_recv, partner_sem, spread_send, spread_recv, cross_sem, gather_send, gather_recv, local_sem, fold_sem = refs
+    load_sem, pair_sem, wide_send, wide_recv, partner_sem, spread_send, spread_recv, cross_sem, gather_sem, local_sem, fold_sem = refs
     geo = Geometry(ep, dp)
     geo.entry_barrier()
-    plane = dp // 2
     z, core = lax.axis_index("ep"), geo.core
     four, three = range(4), range(3)
     f32, bf16 = jnp.float32, jnp.bfloat16
@@ -506,43 +522,59 @@
     for copy in to_sibling + keep:
         copy.start()
 
-    def gather(n, step):
-        to = (geo.local + step) % plane
-        return pltpu.make_async_remote_copy(src_ref=halves[n], dst_ref=full[n].at[geo.local, core], send_sem=gather_send.at[n, step], recv_sem=gather_recv.at[n, step], device_id=(z, 2 * to + core), device_id_type=MESH)
-
-    def gathered(n, step):
-        return full[n].at[(geo.local - step + plane) % plane, core]
-
-    def fold(n, step):
-        return pltpu.make_async_remote_copy(src_ref=gathered(n, step), dst_ref=gathered(n, step), send_sem=fold_sem.at[0, n, step], recv_sem=fold_sem.at[1, n, step], device_id=geo.sibling, device_id_type=MESH)
-
-    def fold_own(n):
-        return pltpu.make_async_remote_copy(src_ref=halves[n], dst_ref=full[n].at[geo.local, core], send_sem=fold_sem.at[0, n, 0], recv_sem=fold_sem.at[1, n, 0], device_id=geo.sibling, device_id_type=MESH)
+    def place(mask):
+        return geo.across(mask) % (dp // 2)
+
+    def hop(n, index, src, dst, mask):
+        return pltpu.make_async_remote_copy(src_ref=src, dst_ref=dst, send_sem=gather_sem.at[0, n, index], recv_sem=gather_sem.at[1, n, index], device_id=(z, 2 * place(mask) + core), device_id_type=MESH)
+
+    def direct(n, mask):
+        return hop(n, mask - 1, halves[n], full[n].at[geo.local, core], mask)
+
+    def relay(n, mask):
+        rows = halves[n].shape[0] // 2
+        block = full[n].at[place(3 - mask), core, pl.ds((mask - 1) * rows, rows)]
+        return hop(n, mask + 1, block, block, mask)
+
+    def fold(n, mask):
+        block = full[n].at[place(mask), core]
+        return pltpu.make_async_remote_copy(src_ref=halves[n] if mask == 0 else block, dst_ref=block, send_sem=fold_sem.at[0, n, mask], recv_sem=fold_sem.at[1, n, mask], device_id=geo.sibling, device_id_type=MESH)
 
     local = [pltpu.make_async_copy(halves[n], full[n].at[geo.local, core], local_sem.at[n]) for n in three]
 
+    def gather(n):
+        for mask in (1, 2):
+            direct(n, mask).start()
+        fold(n, 0).start()
+        local[n].start()
+
+    def forward(n):
+        for mask in (1, 2):
+            direct(n, mask).wait()
+        for mask in (1, 2):
+            relay(n, mask).start()
+            fold(n, mask).start()
+
+    gather(2)
     for n in four:
         to_sibling[n].wait()
         keep[n].wait()
         mine[n][...] = (mine[n][...].astype(f32) + first[n][...].astype(f32)).astype(bf16)
 
-    def widen(n, step):
-        to = geo.out_chip(step)
-        return pltpu.make_async_remote_copy(src_ref=mine[n].at[to], dst_ref=wide[n].at[step], send_sem=wide_send.at[n, step], recv_sem=wide_recv.at[n, step], device_id=geo.member(2 * to + core), device_id_type=MESH)
+    def widen(n, mask):
+        to = geo.across(mask)
+        return pltpu.make_async_remote_copy(src_ref=mine[n].at[to], dst_ref=wide[n].at[mask], send_sem=wide_send.at[n, mask], recv_sem=wide_recv.at[n, mask], device_id=geo.member(2 * to + core), device_id_type=MESH)
 
     for n in four:
-        for step in range(1, geo.chips):
-            widen(n, step).start()
-    for n in three:
-        local[n].start()
-        fold_own(n).start()
-        for step in range(1, plane):
-            gather(n, step).start()
+        for mask in ORDER[1:]:
+            widen(n, mask).start()
+    gather(0)
     for n in four:
+        for mask in ORDER[1:]:
+            widen(n, mask).wait()
         total = mine[n][geo.chip].astype(f32)
-        for step in range(1, geo.chips):
-            widen(n, step).wait()
-            total += wide[n][step].astype(f32)
+        for mask in ORDER[1:]:
+            total += wide[n][mask].astype(f32)
         piece[n][...] = total.astype(bf16)
 
     def swap(n):
@@ -550,38 +582,41 @@
 
     for n in four:
         swap(n).start()
+    forward(2)
     for n in four:
         swap(n).wait()
         last[n][...] = (piece[n][...].astype(f32) + other[n][...].astype(f32)).astype(bf16)
 
-    def spread(n, step):
-        return pltpu.make_async_remote_copy(src_ref=last[n], dst_ref=sums[n].at[core, geo.chip], send_sem=spread_send.at[n, step], recv_sem=spread_recv.at[n, step], device_id=geo.member(2 * geo.out_chip(step) + core), device_id_type=MESH)
+    def spread(n, mask):
+        return pltpu.make_async_remote_copy(src_ref=last[n], dst_ref=sums[n].at[core, geo.chip], send_sem=spread_send.at[n, mask], recv_sem=spread_recv.at[n, mask], device_id=geo.member(2 * geo.across(mask) + core), device_id_type=MESH)
 
     own = [pltpu.make_async_copy(last[n], sums[n].at[core, geo.chip], load_sem.at[n]) for n in four]
     for n in four:
         own[n].start()
-        for step in range(1, geo.chips):
-            spread(n, step).start()
+        for mask in ORDER[1:]:
+            spread(n, mask).start()
+    gather(1)
+    forward(0)
+
+    def cross(n):
+        return pltpu.make_async_remote_copy(src_ref=sums[n].at[core], dst_ref=sums[n].at[core], send_sem=cross_sem.at[0, n], recv_sem=cross_sem.at[1, n], device_id=geo.sibling, device_id_type=MESH)
+
+    for n in four:
+        own[n].wait()
+        for mask in ORDER[1:]:
+            spread(n, mask).wait()
+        cross(n).start()
+    forward(1)
+    for n in (2, 0, 1):
+        for mask in (1, 2):
+            relay(n, mask).wait()
+        fold(n, 3).start()
     for n in three:
         local[n].wait()
-        fold_own(n).wait()
-        for step in range(1, plane):
-            gather(n, step).wait()
-            fold(n, step).start()
-
-    def cross(n):
-        return pltpu.make_async_remote_copy(src_ref=sums[n].at[core], dst_ref=sums[n].at[core], send_sem=cross_sem.at[0, n], recv_sem=cross_sem.at[1, n], device_id=geo.sibling, device_id_type=MESH)
-
-    for n in four:
-        own[n].wait()
-        for step in range(1, geo.chips):
-            spread(n, step).wait()
-        cross(n).start()
+        for mask in range(4):
+            fold(n, mask).wait()
     for n in four:
         cross(n).wait()
-    for n in three:
-        for step in range(1, plane):
-            fold(n, step).wait()
 
 
 def final_exchange(mesh, halves, parts):
@@ -594,7 +629,7 @@
     piece = [c.shape[2:] for c in cut]
     vmem, dma = pltpu.VMEM, pltpu.SemaphoreType.DMA
     scratch = [vmem((chips,) + s, bf16) for _ in range(3) for s in piece] + [vmem(s, bf16) for _ in range(3) for s in piece]
-    scratch += [dma((4,)), dma((2, 4)), dma((4, chips)), dma((4, chips)), dma((2, 4)), dma((4, chips)), dma((4, chips)), dma((2, 4)), dma((3, plane)), dma((3, plane)), dma((3,)), dma((2, 3, plane))]
+    scratch += [dma((4,)), dma((2, 4)), dma((4, chips)), dma((4, chips)), dma((2, 4)), dma((4, chips)), dma((4, chips)), dma((2, 4)), dma((2, 3, 4)), dma((3,)), dma((2, 3, plane))]
     outs = pl.pallas_call(
         functools.partial(final_kernel, ep, dp),
         name="final_exchange",
@@ -613,6 +648,19 @@
     return jnp.take(source, index, axis=0, mode="clip")
 
 
+def slot_owners(slot_of_token, slots):
+    tokens = slot_of_token.shape[1]
+    fine = 64
+    token = jnp.arange(tokens, dtype=jnp.int32)
+    coarse = (slot_of_token[:, :, None] // fine == jnp.arange(slots // fine, dtype=jnp.int32)).astype(jnp.bfloat16)
+    value = jnp.stack([token // 256, token % 256, jnp.ones_like(token)], axis=1).astype(jnp.bfloat16)
+    within = (slot_of_token[:, :, None] % fine == jnp.arange(fine, dtype=jnp.int32)).astype(jnp.bfloat16)
+    spread = (value[None, :, :, None] * within[:, :, None, :]).reshape(slot_of_token.shape[0], tokens, 3 * fine)
+    found = jnp.einsum("lta,ltb->lab", coarse, spread, preferred_element_type=jnp.float32).astype(jnp.int32)
+    high, low, used = found[:, :, :fine], found[:, :, fine:2 * fine], found[:, :, 2 * fine:]
+    return (high * 256 + low + (1 - used) * tokens).reshape(slot_of_token.shape[0], slots)
+
+
 def solution(mesh):
     tok_spec = P(ALL_AXES, None)
     route_spec = P(None, ALL_AXES, None)
@@ -639,9 +687,7 @@
 
         side = lax.axis_index("ep") // (ep // 2)
         turned = (slot_ids.reshape(2, tokens) + side * tokens) % slots
-        flat = (turned + jnp.arange(2, dtype=jnp.int32)[:, None] * slots).reshape(-1)
-        token_ids = jnp.tile(jnp.arange(tokens, dtype=jnp.int32), 2)
-        owner = jnp.full((2 * slots,), tokens, jnp.int32).at[flat].set(token_ids, unique_indices=True).reshape(2, 2, members, block)
+        owner = slot_owners(turned, slots).reshape(2, 2, members, block)
 
         def extended(rows):
             return jnp.pad(rows, ((0, 8), (0, 0)))

time: 1070 us -> 1010 us (0.944)
  Pallas kernels: 779 us -> 702 us
  waiting for transfers between devices: 48.2 us -> 70.6 us
  local copies, waits for them, and re-layouts: 140 us -> 125 us
    pallas_call x1, Pallas kernels: 180 us -> 133 us  [final_exchange(): pl.pallas_call(functools.partial(final_kernel, ep, dp), name='final_excha...]
    pallas_call x1, Pallas kernels: 200 us -> 177 us  [forward_exchange(): pl.pallas_call(functools.partial(forward_kernel, ep, dp), name='forward_e...]
    scatter x1 -> x0, local copies, waits for them, and re-layouts: 15.5 us -> none  [body(): jnp.full((2 * slots,), tokens, jnp.int32).at[flat]]
    ppermute x3, waiting for transfers between devices: 15 us -> 29.1 us  [body(): got.append(lax.ppermute(mine, ALL_AXES, to_partner))]
  transfers between devices with their start and end apart: 8 -> 8, of which waited for: 3 -> 4; matrix products, arithmetic and copies ran while one was open for 16% -> 16% of each run, Pallas kernels for 36% -> 34%
where the time goes in v3:
time: 1010 us; the launch traced here: 998 us
  Pallas kernels  702 us (70%)
  local copies, waits for them, and re-layouts  125 us (12%)
  waiting for transfers between devices  70.6 us (7%)
  other arithmetic  48.8 us (5%)
  matrix products  21.2 us (2%)
  between operations  16.4 us (2%)
  starting transfers between devices  13.9 us (1%)
    pallas_call x2, Pallas kernels, backward_exchange(): pl.pallas_call(functools.partial(backward_kernel, ep, dp, layer), name='b...  392 us
    pallas_call x1, Pallas kernels, forward_exchange(): pl.pallas_call(functools.partial(forward_kernel, ep, dp), name='forward_e...  177 us
    pallas_call x1, Pallas kernels, final_exchange(): pl.pallas_call(functools.partial(final_kernel, ep, dp), name='final_excha...  133 us
    gather x7, local copies, waits for them, and re-layouts, take_rows(): return jnp.take(source, index, axis=0, mode='clip')  110 us
    all_to_all x1, waiting for transfers between devices, body(): lax.all_to_all(grads_two, ALL_AXES, 0, 0, axis_index_groups=groups)  40.4 us
    ppermute x3, waiting for transfers between devices, body(): got.append(lax.ppermute(mine, ALL_AXES, to_partner))  29.1 us
    another operation x3, other arithmetic, body(): expert_out = [jnp.stack(pair) for pair in zip(experts_one, experts_two)]  27.4 us
  transfers between devices with their start and end apart: 8, of which 4 were waited for; matrix products, arithmetic and copies ran while one was open for 16% of the time, Pallas kernels for 34%

profile of v3, /device:TPU:0, one launch (start us, length us, event | category | flops | bytes accessed | tf_op | source)
XLA Modules:
  0.0 997.9 jit_solution(7314738098862271781)
XLA Ops:
  8.0 1.1 dynamic-slice_bitcast_fusion.2
  9.2 4.1 collective-permute-start
  13.3 2.0 dynamic-slice_bitcast_fusion.1
  15.3 2.0 dynamic-slice_bitcast_fusion
  17.3 2.9 collective-permute-start.2
  20.3 0.1 and_select_fusion.1
  20.4 0.1 fusion.7
  20.6 0.1 pad.33.clone
  20.6 0.1 maximum_maximum_fusion
  20.7 0.1 mul.69
  20.8 0.1 bitcast_multiply_fusion
  21.0 0.6 convolution_convert_fusion.2
  21.6 0.1 fusion.21
  21.7 0.9 copy-done.8
  22.6 0.5 fusion
  23.1 1.2 copy-done.24
  24.3 0.5 copy-done.26
  24.8 3.7 add_convert_fusion.4.mixed.refs_2_
  28.5 0.1 squeeze.7
  28.6 0.1 reshape.188
  28.6 1.7 pad.14
  30.4 1.0 copy-done.10
  31.3 0.2 pad.13
  31.6 20.1 %gather_fusion.1 = bf16[4096,640]{1,0:T(8,128)(2,1)} fusion(bf16[2056,640]{1,0:T(8,128)(2,1)} %pad.14, s32[4096]{0:T(1024)S(1)} %broadcast_clamp_fusion.1), kind=kCustom, calls=%fused_computation.1 | custom fusion | bytes 10502144 | tf_op jit(solution)/shard_map/jit(_take)/gather | solution.py:648
  51.6 17.6 %gather_fusion = bf16[4096,640]{1,0:T(8,128)(2,1)} fusion(bf16[2056,640]{1,0:T(8,128)(2,1)S(1)} %pad.13, s32[4096]{0:T(1024)S(1)} %broadcast_clamp_fusion.2), kind=kCustom, calls=%fused_computation | custom fusion | bytes 10502144 | tf_op jit(solution)/shard_map/jit(_take)/gather | solution.py:648
  69.2 1.9 collective-permute-done.refs_6_
  71.1 14.0 %collective-permute-done.1.refs_7_ = bf16[320,1024]{1,0:T(8,128)(2,1)} collective-permute-done((bf16[320,1024]{1,0:T(8,128)(2,1)}, bf16[320,1024]{1,0:T(8,128)(2,1)}, u32[]{:S(2)}, u32[]{:S(2)}) %collective-permute-start.1) | collective-permute-done | bytes 655392 | tf_op jit(solution)/shard_map/ppermute | solution.py:686
  85.2 13.2 %collective-permute-done.2.refs_8_ = bf16[512,640]{1,0:T(8,128)(2,1)} collective-permute-done((bf16[512,640]{1,0:T(8,128)(2,1)}, bf16[512,640]{1,0:T(8,128)(2,1)}, u32[]{:S(2)}, u32[]{:S(2)}) %collective-permute-start.2) | collective-permute-done | bytes 655392 | tf_op jit(solution)/shard_map/ppermute | solution.py:686
  98.4 177.0 %forward_exchange.1 = (bf16[2,8,2,128,640]{4,3,2,1,0:T(8,128)(2,1)}, bf16[2,16,128,640]{3,2,1,0:T(8,128)(2,1)}, f32[2048,640]{1,0:T(8,128)}, bf16[640,1024]{1,0:...) custom-call(bf16[2,16,128,640]{3,2,1,0:T(8,128)(2,1)} %bitcast.95, ...), custom_call_target="tpu_custom_call" | custom-call | flops 24159191040 | bytes 41943040 | tf_op jit(solution)/shard_map/forward_exchange/pallas_call | solution.py:281
  275.4 6.7 all-to-all-start
  282.1 0.1 reshape.212
  282.3 12.8 %gather_fusion.2 = bf16[2048,640]{1,0:T(8,128)(2,1)} fusion(bf16[4096,640]{1,0:T(8,128)(2,1)} %bitcast.84, s32[2048]{0:T(1024)S(1)} %broadcast_clamp_fusion.4), kind=kCustom, calls=%fused_computation.2 | custom fusion | bytes 5251072 | tf_op jit(solution)/shard_map/jit(_take)/gather | solution.py:648
  295.1 3.9 add_convert_fusion.3
  299.1 2.7 add_convert_fusion.2.refs_2_
  301.8 1.5 copy-done.12
  303.3 0.2 pad.15
  303.5 17.6 %gather_fusion.3 = bf16[4096,640]{1,0:T(8,128)(2,1)} fusion(bf16[2056,640]{1,0:T(8,128)(2,1)S(1)} %pad.15, s32[4096]{0:T(1024)S(1)} %broadcast_clamp_fusion), kind=kCustom, calls=%fused_computation.3 | custom fusion | bytes 10502144 | tf_op jit(solution)/shard_map/jit(_take)/gather | solution.py:648
  321.1 40.4 %all-to-all-done.refs_0_ = bf16[16,2,128,640]{3,2,1,0:T(8,128)(2,1)} async-done(((bf16[16,2,128,640]{3,2,1,0:T(8,128)(2,1)}), bf16[16,2,128,640]{3,2,1,0:T(8,128)(2,1)}, u32[]{:S(2)}, u32[]{:S(2)}) %all-to-all-start) | async-done | bytes 5242912 | tf_op jit(solution)/shard_map/all_to_all | solution.py:714
  361.5 190.4 %backward_second.1 = (bf16[2,16,128,640]{3,2,1,0:T(8,128)(2,1)}, f32[2048,640]{1,0:T(8,128)}, bf16[2,8,2,128,640]{4,3,2,1,0:T(8,128)(2,1)}, bf16[640,1024]{1,0:T...) custom-call(bf16[16,2,128,640]{3,2,1,0:T(8,128)(2,1)} %all-to-all-do, ...), custom_call_target="tpu_custom_call" | custom-call | flops 64424509440 | bytes 62914560 | tf_op jit(solution)/shard_map/backward_second/pallas_call | solution.py:490
  551.9 13.2 %gather_fusion.4 = bf16[2048,640]{1,0:T(8,128)(2,1)} fusion(bf16[4096,640]{1,0:T(8,128)(2,1)} %bitcast.85, s32[2048]{0:T(1024)S(1)} %broadcast_clamp_fusion.3), kind=kCustom, calls=%fused_computation.4 | custom fusion | bytes 5251072 | tf_op jit(solution)/shard_map/jit(_take)/gather | solution.py:648
  565.2 4.3 fusion.2
  569.5 3.1 fusion.6
  572.7 0.5 all-gather.8.cloned.1.call-update
  573.3 0.5 all-gather.6.cloned.1.call-update
  573.8 0.5 copy-done.14
  574.3 4.9 fusion.3
  579.2 0.2 pad.16
  579.4 17.6 %gather_fusion.5 = bf16[4096,640]{1,0:T(8,128)(2,1)} fusion(bf16[2056,640]{1,0:T(8,128)(2,1)S(1)} %pad.16, s32[4096]{0:T(1024)S(1)} %broadcast_clamp_fusion.2), kind=kCustom, calls=%fused_computation.5 | custom fusion | bytes 10502144 | tf_op jit(solution)/shard_map/jit(_take)/gather | solution.py:648
  597.1 201.6 %backward_first.1 = (bf16[2,16,128,640]{3,2,1,0:T(8,128)(2,1)}, f32[2048,640]{1,0:T(8,128)}, bf16[2,8,2,128,640]{4,3,2,1,0:T(8,128)(2,1)}, bf16[640,1024]{1,0:T(...) custom-call(bf16[2,8,2,128,640]{4,3,2,1,0:T(8,128)(2,1)} %get-tuple-, ...), custom_call_target="tpu_custom_call" | custom-call | flops 64424509440 | bytes 62914560 | tf_op jit(solution)/shard_map/backward_first/pallas_call | solution.py:490
  798.8 11.4 %gather_fusion.6 = bf16[2048,640]{1,0:T(8,128)(2,1)S(1)} fusion(bf16[4096,640]{1,0:T(8,128)(2,1)} %bitcast.86, s32[2048]{0:T(1024)S(1)} %copy-done.21), kind=kCustom, calls=%fused_computation.6 | custom fusion | bytes 5251072 | tf_op jit(solution)/shard_map/jit(_take)/gather | solution.py:648
  810.2 4.2 fusion.5
  814.5 3.9 add_convert_fusion
  818.4 2.2 convolution_convert_fusion.1
  820.7 0.1 copy-done.6
  820.9 0.2 copy-done.7
  821.1 132.7 %final_exchange.1 = (bf16[4,2,320,1024]{3,2,1,0:T(8,128)(2,1)}, bf16[4,2,320,1024]{3,2,1,0:T(8,128)(2,1)}, bf16[4,2,512,640]{3,2,1,0:T(8,128)(2,1)}, bf16[2,8,40...) custom-call(bf16[320,1024]{1,0:T(8,128)(2,1)S(1)} %copy-done.5, ...), custom_call_target="tpu_custom_call" | custom-call | flops 10000000000 | bytes 31457280 | tf_op jit(solution)/shard_map/final_exchange/pallas_call | solution.py:633
  953.8 1.0 copy-done
  954.9 2.6 pad_maximum_fusion.6
  957.5 1.8 pad_maximum_fusion.5
  959.3 1.7 pad_maximum_fusion.4
  961.0 1.7 pad_maximum_fusion.3
  962.7 9.2 pad_maximum_fusion.2
  971.9 9.1 pad_maximum_fusion.1
  981.0 9.1 pad_maximum_fusion
  (75 shorter events, 0.6 us)
Async XLA Ops:
  8.0 12.2 %copy-start.22 = (s32[2,2048,1]{1,2,0:T(1,128)S(1)}, s32[2,2048,1]{1,2,0:T(1,128)}, u32[]{:S(2)}) copy-start(s32[2,2048,1]{1,2,0:T(1,128)} %param.13) | copy-start | bytes 49156
  9.2 62.0 %collective-permute-start = (bf16[320,1024]{1,0:T(8,128)(2,1)S(1)}, bf16[320,1024]{1,0:T(8,128)(2,1)}, u32[]{:S(2)}, u32[]{:S(2)}) collective-permute-start(bf16[320,1024]{1,0:T(8,128)(2,1)S(1)} %dynamic-slice_bitcast_fusion.2), channel_id=1, source_target_pairs={{0,16},{1,17},{2,18},{3,19},{4,20},{5,21},{6,22},{7,23},{8,24},{9,... | collective-permute-start | bytes 1966088 | tf_op jit(solution)/shard_map/ppermute | solution.py:686
  15.3 69.9 %collective-permute-start.1 = (bf16[320,1024]{1,0:T(8,128)(2,1)}, bf16[320,1024]{1,0:T(8,128)(2,1)}, u32[]{:S(2)}, u32[]{:S(2)}) collective-permute-start(bf16[320,1024]{1,0:T(8,128)(2,1)} %dynamic-slice_bitcast_fusion.1), channel_id=1, source_target_pairs={{0,16},{1,17},{2,18},{3,19},{4,20},{5,21},{6,22},{7,23},{8,24},{9,... | collective-permute-start | bytes 1966088 | tf_op jit(solution)/shard_map/ppermute | solution.py:686
  17.3 81.1 %collective-permute-start.2 = (bf16[512,640]{1,0:T(8,128)(2,1)}, bf16[512,640]{1,0:T(8,128)(2,1)}, u32[]{:S(2)}, u32[]{:S(2)}) collective-permute-start(bf16[512,640]{1,0:T(8,128)(2,1)} %dynamic-slice_bitcast_fusion), channel_id=1, source_target_pairs={{0,16},{1,17},{2,18},{3,19},{4,20},{5,21},{6,22},{7,23},{8,24},{9,... | collective-permute-start | bytes 1966088 | tf_op jit(solution)/shard_map/ppermute | solution.py:686
  20.8 0.9 copy-start.23
  20.8 1.7 copy-start.8
  22.6 1.7 copy-start.24
  22.6 2.2 copy-start.26
  28.6 2.7 copy-start.10
  275.4 86.2 %all-to-all-start = ((bf16[16,2,128,640]{3,2,1,0:T(8,128)(2,1)}), bf16[16,2,128,640]{3,2,1,0:T(8,128)(2,1)}, u32[]{:S(2)}, u32[]{:S(2)}) async-start(bf16[16,2,128,640]{3,2,1,0:T(8,128)(2,1)} %bitcast.87), calls=%async_computation | async-start | bytes 10485760 | tf_op jit(solution)/shard_map/all_to_all | solution.py:714
  282.0 672.8 %all-reduce.7.cloned.1.call-start = ((), (), s32[]{:S(2)}) async-start(), calls=%async_computation.4 | async-start | bytes 9502720 | tf_op jit(solution)/shard_map/psum | solution.py:732
  282.2 12.9 %copy-start.20 = (s32[2048]{0:T(1024)}, s32[2048]{0:T(1024)S(1)}, u32[]{:S(2)}) copy-start(s32[2048]{0:T(1024)S(1)} %broadcast_clamp_fusion.4) | copy-start | bytes 24580
  282.3 12.8 %copy-start.11 = (bf16[2048,640]{1,0:T(8,128)(2,1)S(1)}, bf16[2048,640]{1,0:T(8,128)(2,1)}, u32[]{:S(2)}) copy-start(bf16[2048,640]{1,0:T(8,128)(2,1)} %add_convert_fusion.4.mixed.refs_2_) | copy-start | bytes 7864324
  295.1 4.0 copy-start.27
  299.1 2.7 copy-start.15
  301.8 1.5 copy-start.12
  551.9 13.2 %copy-start.9 = (bf16[2048,640]{1,0:T(8,128)(2,1)S(1)}, bf16[2048,640]{1,0:T(8,128)(2,1)}, u32[]{:S(2)}) copy-start(bf16[2048,640]{1,0:T(8,128)(2,1)} %refs_3_.3) | copy-start | bytes 7864324
  565.2 4.3 copy-start.16
  569.4 3.2 copy-start.13
  572.6 1.7 copy-start.14
  572.6 390.1 %all-gather.8.cloned.1.call-start = ((), (), s32[]{:S(2)}) async-start(), calls=%async_computation.3 | async-start | bytes 5898240 | tf_op jit(solution)/shard_map/all_gather | solution.py:726
  573.2 398.7 %all-gather.6.cloned.1.call-start = ((), (), s32[]{:S(2)}) async-start(), calls=%async_computation.2 | async-start | bytes 5898240 | tf_op jit(solution)/shard_map/all_gather | solution.py:726
  573.8 407.2 %all-gather.4.cloned.1.call-start = ((), (), s32[]{:S(2)}) async-start(), calls=%async_computation.1 | async-start | bytes 5898240 | tf_op jit(solution)/shard_map/all_gather | solution.py:726
  597.1 201.7 %copy-start.21 = (s32[2048]{0:T(1024)S(1)}, s32[2048]{0:T(1024)}, u32[]{:S(2)}) copy-start(s32[2048]{0:T(1024)} %copy-done.20) | copy-start | bytes 24580
  810.2 4.3 copy-start.28
  814.5 3.9 copy-start.25
  818.4 2.3 copy-start.2
  818.4 2.3 copy-start.3
  818.4 2.3 copy-start.4
  818.4 2.3 copy-start.5
  818.4 2.4 copy-start.6
  818.4 2.6 copy-start.7
  953.8 1.1 copy-start
  954.9 2.6 copy-start.1
  954.9 2.6 copy-start.19
  957.5 1.8 copy-start.18
  959.3 1.7 copy-start.17
Sparse Core Ops, SparseCore 0:
  572.7 298.6 all-reduce.6
Sparse Core Ops, SparseCore 1:
  575.0 86.9 all-gather.7
  663.7 102.1 all-gather.5
  767.7 40.7 all-gather.3

commit v4 on v3

--- a/solution.py
+++ b/solution.py
@@ -16,6 +16,7 @@
 AT_ONCE = (1, 2, 4, 6)
 RELEASED = ((1, 3), (2, 5), (4, 7))
 EARLY = (1, 2, 4)
+PACK_CODE = sum(step * 8**n for n, step in enumerate((1, 2, 4, 6, 0, 3, 5, 7)))
 
 
 def contract_rows(left, right):
@@ -70,20 +71,37 @@
 
 
 class Outbound:
-    def __init__(self, geo, send, recv, send_sem, recv_sem):
-        self.geo, self.send, self.recv, self.send_sem, self.recv_sem = geo, send, recv, send_sem, recv_sem
+    def __init__(self, geo, part, send, recv, send_sem, recv_sem):
+        self.geo, self.part = geo, part
+        self.send, self.recv, self.send_sem, self.recv_sem = [ref.at[part] for ref in (send, recv, send_sem, recv_sem)]
 
     def copy(self, step, core):
         geo = self.geo
         index = 2 * geo.at_step(step) + core
         return pltpu.make_async_remote_copy(src_ref=self.send.at[index], dst_ref=self.recv.at[step, geo.core], send_sem=self.send_sem.at[step, core], recv_sem=self.recv_sem.at[step, geo.core], device_id=geo.member(index), device_id_type=MESH)
 
-    def start(self):
-        geo = self.geo
-        pltpu.make_async_copy(self.send.at[geo.me], self.recv.at[0, geo.core], self.recv_sem.at[0, geo.core]).start()
+    def own(self):
+        geo = self.geo
+        return pltpu.make_async_copy(self.send.at[geo.me], self.recv.at[0, geo.core], self.recv_sem.at[0, geo.core])
+
+    def pack(self, slots, rows):
+        geo = self.geo
+        tokens = rows.shape[0]
+        block = self.send.shape[1]
+
+        @pl.loop(0, geo.chips)
+        def _(n):
+            power = (1 + 7 * (n % 2)) * (1 + 63 * (n // 2 % 2)) * (1 + 4095 * (n // 4))
+            chip = geo.at_step(PACK_CODE // power % 8)
+            base = self.part * tokens + chip * 2 * block
+            wanted = base + lax.broadcasted_iota(jnp.int32, (2 * block, tokens), 0)
+            pick = (wanted == slots[...]).astype(jnp.float32).astype(jnp.bfloat16)
+            self.send[pl.ds(2 * chip, 2)] = dot32(pick, rows[...]).astype(jnp.bfloat16).reshape(2, block, rows.shape[1])
+            for when, step in enumerate(AT_ONCE):
+                pl.when(n == when + 1)(functools.partial(self.issue, step))
+
+        self.own().start()
         self.copy(0, 1 - geo.core).start()
-        for step in AT_ONCE:
-            self.issue(step)
 
     def issue(self, step):
         for core in range(2):
@@ -148,8 +166,8 @@
 
 
 class WeightSwap:
-    def __init__(self, geo, layer, own, foreign, sems):
-        self.geo, self.layer, self.own, self.foreign, self.sems = geo, layer, own, foreign, sems
+    def __init__(self, geo, layer, own, foreign, sems, which):
+        self.geo, self.layer, self.own, self.foreign, self.sems, self.every = geo, layer, own, foreign, sems, which
 
     def over(self, which):
         geo = self.geo
@@ -162,16 +180,16 @@
         return pltpu.make_async_remote_copy(src_ref=rows, dst_ref=rows, send_sem=self.sems.at[2, which], recv_sem=self.sems.at[3, which], device_id=geo.sibling, device_id_type=MESH)
 
     def start(self):
-        for which in range(3):
+        for which in self.every:
             self.over(which).start()
 
     def pass_on(self):
-        for which in range(3):
+        for which in self.every:
             self.over(which).wait()
             self.across(which).start()
 
     def finish(self):
-        for which in range(3):
+        for which in self.every:
             self.across(which).wait()
 
 
@@ -179,7 +197,7 @@
     return value * jax.nn.sigmoid(value)
 
 
-def forward_kernel(ep, dp, send, mixed, *refs):
+def forward_kernel(ep, dp, slots, mixed, *refs):
     refs = list(refs)
 
     def take(count):
@@ -187,29 +205,32 @@
         del refs[:count]
         return got
 
-    experts, ws, got = take(3), take(3), take(3)
+    experts, ws, got = take(3), take(3), take(2)
     recv_out, back, shared = take(3)
     keep_out, next_out = take(3), take(3)
-    recv, outs = take(2)
+    send, recv, outs = take(3)
     shared_w, own_w, foreign_w = take(3), take(3), take(3)
-    go_sem, get_sem, ret_sem, res_sem, swap_sem, pass_sem, load_sem, save_sem = refs
+    go_sem, get_sem, ret_sem, res_sem, swap_sem, down_sem, pass_sem, load_sem, save_sem = refs
     geo = Geometry(ep, dp)
     geo.entry_barrier()
-    outbound = [Outbound(geo, send.at[part], recv.at[part], go_sem.at[part], get_sem.at[part]) for part in range(2)]
+    outbound = [Outbound(geo, part, send, recv, go_sem, get_sem) for part in range(2)]
     returns = [Return(geo, outs.at[part], back.at[part], ret_sem.at[part], res_sem.at[part]) for part in range(2)]
-    swap = WeightSwap(geo, 1, experts, next_out, swap_sem)
-    outbound[0].start()
+    swap = WeightSwap(geo, 1, experts, next_out, swap_sem, range(3))
+    down = WeightSwap(geo, 0, experts, foreign_w, down_sem, (2,))
     loads = []
     passes = []
     for which in range(3):
-        mine = half_rows(foreign_w[which].shape[0], geo.core)
         loads.append(pltpu.make_async_copy(ws[which].at[0], shared_w[which], load_sem.at[0, which]))
         loads.append(pltpu.make_async_copy(experts[which].at[0, geo.local], own_w[which], load_sem.at[1, which]))
+    for which in range(2):
+        mine = half_rows(foreign_w[which].shape[0], geo.core)
         loads.append(pltpu.make_async_copy(got[which], foreign_w[which].at[mine], load_sem.at[2, which]))
         passes.append(pltpu.make_async_remote_copy(src_ref=got[which], dst_ref=foreign_w[which].at[mine], send_sem=pass_sem.at[0, which], recv_sem=pass_sem.at[1, which], device_id=geo.sibling, device_id_type=MESH))
+    down.start()
     for copy in loads + passes:
         copy.start()
-    outbound[1].start()
+    outbound[0].pack(slots, mixed)
+    outbound[1].pack(slots, mixed)
     swap.start()
 
     tile = 2 * STEPS * recv.shape[3]
@@ -228,11 +249,13 @@
         at = pl.ds(pl.multiple_of(t * tile, tile), tile)
         shared[at, :] = ffn(mixed[at, :], *shared_w)
 
-    keeps = [pltpu.make_async_copy(src, dst, load_sem.at[0, which]) for which, (src, dst) in enumerate(zip(foreign_w, keep_out))]
-    for keep in keeps:
-        keep.start()
     width = mixed.shape[1]
     for part, weights in enumerate((own_w, foreign_w)):
+        if part == 1:
+            down.finish()
+            keeps = [pltpu.make_async_copy(src, dst, load_sem.at[0, which]) for which, (src, dst) in enumerate(zip(foreign_w, keep_out))]
+            for keep in keeps:
+                keep.start()
 
         @pl.loop(0, geo.chips // STEPS)
         def _(t):
@@ -250,6 +273,8 @@
 
         for step in range(STEPS):
             returns[part].start(geo.chips - STEPS + step)
+        if part == 0:
+            down.pass_on()
     swap.pass_on()
     for part in range(2):
         outbound[part].wait_sends()
@@ -265,10 +290,11 @@
     swap.finish()
 
 
-def forward_exchange(mesh, send, mixed, experts, shared, got):
+def forward_exchange(mesh, slots, mixed, experts, shared, got):
     ep, dp = mesh.shape["ep"], mesh.shape["dp"]
-    members, block, width = send.shape[1:]
-    tokens = mixed.shape[0]
+    tokens, width = mixed.shape
+    members = ep * dp // 2
+    block = tokens // members
     bf16, f32 = jnp.bfloat16, jnp.float32
     shapes = [w.shape[2:] for w in experts]
     hidden = shapes[0][1]
@@ -282,14 +308,15 @@
         functools.partial(forward_kernel, ep, dp),
         name="forward_exchange",
         out_shape=[jax.ShapeDtypeStruct((2, chips, 2, block, width), bf16), jax.ShapeDtypeStruct((2, members, block, width), bf16), jax.ShapeDtypeStruct((tokens, width), f32)] + expert + expert,
-        in_specs=[anywhere, inside] + [anywhere] * 9,
+        in_specs=[inside, inside] + [anywhere] * 8,
         out_specs=[anywhere, anywhere, inside] + [anywhere] * 6,
-        scratch_shapes=[pltpu.VMEM((2, chips, 2, block, width), bf16) for _ in range(2)]
+        scratch_shapes=[pltpu.VMEM((2, members, block, width), bf16)]
+        + [pltpu.VMEM((2, chips, 2, block, width), bf16) for _ in range(2)]
         + [pltpu.VMEM(s, bf16) for _ in range(3) for s in shapes]
-        + [dma((2, chips, 2)), dma((2, chips, 2)), dma((2, chips, 2)), dma((2, members)), dma((4, 3)), dma((2, 3)), dma((3, 3)), dma((2, chips // STEPS))],
+        + [dma((2, chips, 2)), dma((2, chips, 2)), dma((2, chips, 2)), dma((2, members)), dma((4, 3)), dma((4, 3)), dma((2, 3)), dma((3, 3)), dma((2, chips // STEPS))],
         compiler_params=pltpu.CompilerParams(collective_id=0, has_side_effects=True, vmem_limit_bytes=60 * 2**20),
         cost_estimate=pl.CostEstimate(flops=flops, bytes_accessed=40 * 2**20, transcendentals=0),
-    )(send, mixed, *experts, *shared, *got)
+    )(slots, mixed, *experts, *shared, *got)
 
 
 class PairSum:
@@ -322,24 +349,27 @@
         del refs[:count]
         return got
 
-    held, send, mixed, grad_y = take(4)
+    slots = take(1)[0]
+    held = take(2 if layer else 1)
+    rows_in, mixed, grad_y = take(3)
     own_w, foreign_w, shared_w = take(3), take(3), take(3)
     back, shared_dx, recv = take(3)
     shared_out, own_out = take(3), take(3)
-    x_buf, g_buf, dx_rows, dx_buf = take(4)
+    source, send, x_buf, g_buf, dx_rows, dx_buf = take(6)
     weights, acc, stages, theirs, partner_in = take(3), take(3), take(3), take(3), take(3)
     go_sem, get_sem, ret_sem, res_sem, partner_sem, load_sem, x_sem, g_sem, dx_sem, pair_sem = refs
 
     geo = Geometry(ep, dp)
     geo.entry_barrier()
     tile = 2 * send.shape[2]
+    fill = pltpu.make_async_copy(rows_in, source, dx_sem.at[0])
+    fill.start()
     width = mixed.shape[1]
     per_set = mixed.shape[0] // tile
     total = 3 * per_set
-    outbound = [Outbound(geo, send.at[part], recv.at[part], go_sem.at[part], get_sem.at[part]) for part in range(2)]
+    outbound = [Outbound(geo, part, send, recv, go_sem, get_sem) for part in range(2)]
     returns = [Return(geo, dx_rows.at[part], back.at[part], ret_sem.at[part], res_sem.at[part]) for part in range(2)]
     pairs = [PairSum(geo, stages, theirs, pair_sem, expert) for expert in range(2)]
-    outbound[1].start()
     loads = []
     for which in range(3):
         loads.append(pltpu.make_async_copy(shared_w[which].at[layer], weights[which].at[2], load_sem.at[2, which]))
@@ -347,13 +377,15 @@
         loads.append(pltpu.make_async_copy(foreign_w[which], weights[which].at[1], load_sem.at[1, which]))
     for load in loads:
         load.start()
-    outbound[0].start()
+    fill.wait()
+    outbound[1].pack(slots, source)
+    outbound[0].pack(slots, source)
     moved, moved_sem, kept, kept_sem = (x_buf, x_sem, g_buf, g_sem) if layer else (g_buf, g_sem, x_buf, x_sem)
 
     def held_block(part, step, core):
         if layer:
-            return held.at[2 * geo.at_step(step) + core, part]
-        return held.at[part, step, core]
+            return held[part].at[2 * geo.at_step(step) + core]
+        return held[0].at[part, step, core]
 
     def fetch(i, slot):
         @pl.when(i < per_set)
@@ -465,11 +497,12 @@
         returns[part].wait_all()
 
 
-def backward_exchange(mesh, layer, held, send, mixed, grad_y, own, foreign, shared):
+def backward_exchange(mesh, layer, slots, held, rows, mixed, grad_y, own, foreign, shared):
     ep, dp = mesh.shape["ep"], mesh.shape["dp"]
-    members, block, width = send.shape[1:]
+    tokens, width = mixed.shape
+    members = ep * dp // 2
+    block = tokens // members
     chips = members // 2
-    tokens = mixed.shape[0]
     tile = 2 * block
     bf16, f32 = jnp.bfloat16, jnp.float32
     anywhere = pl.BlockSpec(memory_space=pl.ANY)
@@ -480,18 +513,18 @@
     by_step = like((2, chips, 2, block, width), bf16)
     outs = [like((2, members, block, width), bf16), like((tokens, width), f32), by_step] + [like(s, bf16) for s in shapes + halves]
     vmem = pltpu.VMEM
-    scratch = [vmem((2, tile, width), bf16), vmem((2, tile, width), bf16), vmem(by_step.shape, bf16), vmem((2, tile, width), f32)]
+    scratch = [vmem((tokens, width), bf16), vmem((2, members, block, width), bf16), vmem((2, tile, width), bf16), vmem((2, tile, width), bf16), vmem(by_step.shape, bf16), vmem((2, tile, width), f32)]
     scratch += [vmem((3,) + s, bf16) for s in shapes] + [vmem(s, f32) for s in shapes] + [vmem((2,) + s, bf16) for s in shapes]
     scratch += [vmem((2,) + s, bf16) for s in halves] + [vmem(s, bf16) for s in halves]
     dma = pltpu.SemaphoreType.DMA
     scratch += [dma((2, chips, 2)), dma((2, chips, 2)), dma((2, chips, 2)), dma((2, members)), dma((2, 3)), dma((3, 3)), dma((2,)), dma((2,)), dma((2,)), dma((2, 2, 3))]
-    operands = [held, send, mixed, grad_y, *own, *foreign, *shared]
+    operands = [slots, *held, rows, mixed, grad_y, *own, *foreign, *shared]
     flops = 2 * 8 * width * shapes[0][1] * (2 * members * block + tokens)
     return pl.pallas_call(
         functools.partial(backward_kernel, ep, dp, layer),
         name="backward_second" if layer else "backward_first",
         out_shape=outs,
-        in_specs=[anywhere] * len(operands),
+        in_specs=[inside] + [anywhere] * (len(operands) - 1),
         out_specs=[anywhere] * 3 + [inside] * 6,
         scratch_shapes=scratch,
         compiler_params=pltpu.CompilerParams(collective_id=1 + layer, has_side_effects=True, vmem_limit_bytes=63 * 2**20),
@@ -680,21 +713,18 @@
         core, local = lax.axis_index("dp") % 2, lax.axis_index("dp") // 2
 
         got = []
-        for w in experts:
+        for w in experts[:2]:
             rows, columns = w.shape[2] // 2, w.shape[3]
             mine = lax.dynamic_slice(w, (0, local, core * rows, 0), (1, 1, rows, columns)).reshape(rows, columns)
             got.append(lax.ppermute(mine, ALL_AXES, to_partner))
 
         side = lax.axis_index("ep") // (ep // 2)
         turned = (slot_ids.reshape(2, tokens) + side * tokens) % slots
-        owner = slot_owners(turned, slots).reshape(2, 2, members, block)
+        owner = slot_owners(turned[1:], slots).reshape(2, members, block)
 
         def extended(rows):
             return jnp.pad(rows, ((0, 8), (0, 0)))
 
-        def to_slots(layer, rows):
-            return take_rows(extended(rows), owner[layer].reshape(-1)).reshape(2, members, block, width)
-
         def from_slots(layer, back):
             return take_rows(back.reshape(slots, width), turned[layer]).astype(jnp.float32)
 
@@ -704,14 +734,16 @@
         def gated(grad, layer):
             return (gate_vals[layer] * grad.astype(jnp.float32)).astype(jnp.bfloat16)
 
-        by_member = owner[1].transpose(1, 0, 2).reshape(-1)
-        grads_two = take_rows(extended(gated(grad_out, 1)), by_member).reshape(members, 2, block, width)
+        def go_out(part, rows):
+            blocks = take_rows(rows, owner[part].reshape(-1)).reshape(members, block, width)
+            return lax.all_to_all(blocks, ALL_AXES, 0, 0, axis_index_groups=groups)
+
+        grads_two = extended(gated(grad_out, 1))
+        grads_first = go_out(1, grads_two)
         mixed_one = mix(act_in, 0)
-        sent_one = to_slots(0, mixed_one)
-        sent_one, grads_two = lax.optimization_barrier((sent_one, grads_two))
-        recv, back, shared_y, *foreign = forward_exchange(mesh, sent_one, mixed_one, experts, shared, got)
+        recv, back, shared_y, *foreign = forward_exchange(mesh, turned[0:1], mixed_one, experts, shared, got)
         back, grads_two = lax.optimization_barrier((back, grads_two))
-        grads_two = lax.all_to_all(grads_two, ALL_AXES, 0, 0, axis_index_groups=groups)
+        grads_second = go_out(0, grads_two)
         routed = from_slots(0, back)
         act_two = (mixed_one.astype(jnp.float32) + gate_vals[0] * routed + shared_y).astype(jnp.bfloat16)
         mixed_two = mix(act_two, 1)
@@ -725,13 +757,13 @@
         def gather(half):
             return lax.all_gather(half, "dp", axis=0, tiled=True).reshape((dp // 2, 2 * half.shape[0], half.shape[1]))
 
-        out = backward_exchange(mesh, 1, grads_two, to_slots(1, mixed_two), mixed_two, grad_out, experts, foreign[3:], shared)
+        out = backward_exchange(mesh, 1, turned[1:2], [grads_second, grads_first], mixed_two, mixed_two, grad_out, experts, foreign[3:], shared)
         shared_two, own_two = out[3:6], out[6:9]
         experts_two = [gather(half) for half in own_two]
         grad_one, dense_two = finish(1, act_two, grad_out, out[0], out[1])
         sums_two = [lax.psum(part, ALL_AXES) for part in (dense_two, *shared_two)]
 
-        out = backward_exchange(mesh, 0, recv, to_slots(0, gated(grad_one, 0)), mixed_one, grad_one, experts, foreign[:3], shared)
+        out = backward_exchange(mesh, 0, turned[0:1], [recv], gated(grad_one, 0), mixed_one, grad_one, experts, foreign[:3], shared)
         shared_one, own_one = out[3:6], out[6:9]
         grad_act, dense_one = finish(0, act_in, grad_one, out[0], out[1])
         experts_one, sums_one = final_exchange(mesh, own_one, [dense_one, *shared_one])

time: 1010 us -> 1020 us (level)
  Pallas kernels: 702 us -> 772 us
  local copies, waits for them, and re-layouts: 125 us -> 62.4 us
    gather x7 -> x5, local copies, waits for them, and re-layouts: 110 us -> 54.1 us  [take_rows(): return jnp.take(source, index, axis=0, mode='clip')]
    pallas_call x2, Pallas kernels: 392 us -> 431 us  [backward_exchange(): pl.pallas_call(functools.partial(backward_kernel, ep, dp, layer), name='b...]
    pallas_call x1, Pallas kernels: 177 us -> 205 us  [forward_exchange(): pl.pallas_call(functools.partial(forward_kernel, ep, dp), name='forward_e...]
    all_to_all x1 -> x2, waiting for transfers between devices: 40.4 us -> 16.1 us  [go_out(): return lax.all_to_all(blocks, ALL_AXES, 0, 0, axis_index_groups=groups)]
    ppermute x3 -> x2, waiting for transfers between devices: 29.1 us -> 51.5 us  [body(): got.append(lax.ppermute(mine, ALL_AXES, to_partner))]
  transfers between devices with their start and end apart: 8 -> 8, of which waited for: 4 -> 3; matrix products, arithmetic and copies ran while one was open for 16% -> 9% of each run, Pallas kernels for 34% -> 55%
where the time goes in v4:
time: 1020 us; the launch traced here: 1010 us
  Pallas kernels  772 us (76%)
  waiting for transfers between devices  68.6 us (7%)
  local copies, waits for them, and re-layouts  62.4 us (6%)
  other arithmetic  49.4 us (5%)
  matrix products  25.3 us (2%)
  between operations  16.4 us (2%)
  starting transfers between devices  15.3 us (2%)
    pallas_call x2, Pallas kernels, backward_exchange(): pl.pallas_call(functools.partial(backward_kernel, ep, dp, layer), name='b...  431 us
    pallas_call x1, Pallas kernels, forward_exchange(): pl.pallas_call(functools.partial(forward_kernel, ep, dp), name='forward_e...  205 us
    pallas_call x1, Pallas kernels, final_exchange(): pl.pallas_call(functools.partial(final_kernel, ep, dp), name='final_excha...  136 us
    gather x5, local copies, waits for them, and re-layouts, take_rows(): return jnp.take(source, index, axis=0, mode='clip')  54.1 us
    ppermute x2, waiting for transfers between devices, body(): got.append(lax.ppermute(mine, ALL_AXES, to_partner))  51.5 us
    another operation x3, other arithmetic, body(): expert_out = [jnp.stack(pair) for pair in zip(experts_one, experts_two)]  27.4 us
  transfers between devices with their start and end apart: 8, of which 3 were waited for; matrix products, arithmetic and copies ran while one was open for 9% of the time, Pallas kernels for 55%

profile of v4, /device:TPU:0, one launch (start us, length us, event | category | flops | bytes accessed | tf_op | source)
XLA Modules:
  0.0 1009.8 jit_solution(2483767951558249986)
XLA Ops:
  8.0 0.0 copy-start.8
  8.1 0.9 and_select_fusion.2
  9.0 0.6 fusion.32
  9.6 0.7 fusion.31
  10.4 0.1 pad.21.clone
  10.4 0.1 maximum_maximum_fusion
  10.5 0.1 broadcast_multiply_fusion
  10.6 0.4 fusion.7
  11.0 0.1 fusion.24
  11.1 0.1 reshape.332
  11.1 0.5 fusion
  11.7 0.2 pad.4
  11.9 9.3 gather_fusion.1
  21.3 6.4 all-to-all-start.1
  27.6 1.1 dynamic-slice_bitcast_fusion.1
  28.8 2.7 collective-permute-start
  31.4 2.0 dynamic-slice_bitcast_fusion
  33.4 0.3 collective-permute-start.1
  33.7 0.1 reshape.324
  33.8 6.8 add_convert_fusion.4.mixed.refs_3_
  40.6 37.5 %collective-permute-done.refs_6_ = bf16[320,1024]{1,0:T(8,128)(2,1)} collective-permute-done((bf16[320,1024]{1,0:T(8,128)(2,1)S(1)}, bf16[320,1024]{1,0:T(8,128)(2,1)}, u32[]{:S(2)}, u32[]{:S(2)}) %collective-permute-start) | collective-permute-done | bytes 655392 | tf_op jit(solution)/shard_map/ppermute | solution.py:719
  78.1 14.0 %collective-permute-done.1.refs_7_ = bf16[320,1024]{1,0:T(8,128)(2,1)} collective-permute-done((bf16[320,1024]{1,0:T(8,128)(2,1)}, bf16[320,1024]{1,0:T(8,128)(2,1)}, u32[]{:S(2)}, u32[]{:S(2)}) %collective-permute-start.1) | collective-permute-done | bytes 655392 | tf_op jit(solution)/shard_map/ppermute | solution.py:719
  92.1 205.3 %forward_exchange.1 = (bf16[2,8,2,128,640]{4,3,2,1,0:T(8,128)(2,1)}, bf16[2,16,128,640]{3,2,1,0:T(8,128)(2,1)}, f32[2048,640]{1,0:T(8,128)}, bf16[640,1024]{1,0:...) custom-call(s32[1,2048]{1,0:T(1,128)} %get-tuple-element.85.slots.re, ...), custom_call_target="tpu_custom_call" | custom-call | flops 24159191040 | bytes 41943040 | tf_op jit(solution)/shard_map/forward_exchange/pallas_call | solution.py:307
  297.4 9.3 gather_fusion
  306.7 5.8 all-to-all-start
  312.5 0.0 all-reduce.4.cloned.1.call-start
  312.6 0.0 copy-start.17
  312.6 11.1 %gather_fusion.2 = bf16[2048,640]{1,0:T(8,128)(2,1)S(1)} fusion(bf16[4096,640]{1,0:T(8,128)(2,1)} %bitcast.74, s32[2048]{0:T(1024)S(1)} %broadcast_clamp_fusion.1), kind=kCustom, calls=%fused_computation.2 | custom fusion | bytes 5251072 | tf_op jit(solution)/shard_map/jit(_take)/gather | solution.py:681
  323.7 3.9 add_convert_fusion.3
  327.7 0.0 copy-start.12
  327.7 1.5 copy-done.12
  329.2 3.7 add_convert_fusion.2.refs_3_.refs_4_
  332.9 16.1 %all-to-all-done.refs_1_ = bf16[16,128,640]{2,1,0:T(8,128)(2,1)} async-done(((bf16[16,128,640]{2,1,0:T(8,128)(2,1)}), bf16[16,128,640]{2,1,0:T(8,128)(2,1)}, u32[]{:S(2)}, u32[]{:S(2)}) %all-to-all-start) | async-done | bytes 2621472 | tf_op jit(solution)/shard_map/all_to_all | solution.py:739
  348.9 214.0 %backward_second.1 = (bf16[2,16,128,640]{3,2,1,0:T(8,128)(2,1)}, f32[2048,640]{1,0:T(8,128)}, bf16[2,8,2,128,640]{4,3,2,1,0:T(8,128)(2,1)}, bf16[640,1024]{1,0:T...) custom-call(s32[1,2048]{1,0:T(1,128)} %copy-done.20, ...), custom_call_target="tpu_custom_call" | custom-call | flops 64424509440 | bytes 62914560 | tf_op jit(solution)/shard_map/backward_second/pallas_call | solution.py:523
  563.0 12.8 %gather_fusion.3 = bf16[2048,640]{1,0:T(8,128)(2,1)} fusion(bf16[4096,640]{1,0:T(8,128)(2,1)} %bitcast.75, s32[2048]{0:T(1024)S(1)} %get-tuple-element.86), kind=kCustom, calls=%fused_computation.3 | custom fusion | bytes 5251072 | tf_op jit(solution)/shard_map/jit(_take)/gather | solution.py:681
  575.8 4.3 fusion.2
  580.1 0.0 copy-start.10
  580.1 3.1 fusion.6
  583.2 0.0 all-reduce.4.cloned.1.call-update
  583.2 0.0 all-gather.8.cloned.1.call-start
  583.3 0.5 all-gather.8.cloned.1.call-update
  583.8 0.0 all-gather.6.cloned.1.call-start
  583.9 0.5 all-gather.6.cloned.1.call-update
  584.4 0.0 all-gather.4.cloned.1.call-start
  584.5 0.5 copy-done.11
  585.0 5.3 fusion.3
  590.3 0.0 all-gather.4.cloned.1.call-update
  590.3 216.9 %backward_first.1 = (bf16[2,16,128,640]{3,2,1,0:T(8,128)(2,1)}, f32[2048,640]{1,0:T(8,128)}, bf16[2,8,2,128,640]{4,3,2,1,0:T(8,128)(2,1)}, bf16[640,1024]{1,0:T(...) custom-call(s32[1,2048]{1,0:T(1,128)} %get-tuple-element.85.slots.re, ...), custom_call_target="tpu_custom_call" | custom-call | flops 64424509440 | bytes 62914560 | tf_op jit(solution)/shard_map/backward_first/pallas_call | solution.py:523
  807.2 11.5 %gather_fusion.4 = bf16[2048,640]{1,0:T(8,128)(2,1)S(1)} fusion(bf16[4096,640]{1,0:T(8,128)(2,1)} %bitcast.76, s32[2048]{0:T(1024)S(1)} %copy-done.18), kind=kCustom, calls=%fused_computation.4 | custom fusion | bytes 5251072 | tf_op jit(solution)/shard_map/jit(_take)/gather | solution.py:681
  818.7 4.2 fusion.5
  823.0 0.0 copy-start.21
  823.0 3.7 add_convert_fusion
  826.8 2.2 convolution_convert_fusion.1
  829.1 0.1 copy-done.6
  829.2 0.2 copy-done.7
  829.4 136.0 %final_exchange.1 = (bf16[4,2,320,1024]{3,2,1,0:T(8,128)(2,1)}, bf16[4,2,320,1024]{3,2,1,0:T(8,128)(2,1)}, bf16[4,2,512,640]{3,2,1,0:T(8,128)(2,1)}, bf16[2,8,40...) custom-call(bf16[320,1024]{1,0:T(8,128)(2,1)S(1)} %copy-done.5, ...), custom_call_target="tpu_custom_call" | custom-call | flops 10000000000 | bytes 31457280 | tf_op jit(solution)/shard_map/final_exchange/pallas_call | solution.py:666
  965.5 1.0 copy-done
  966.5 2.6 pad_maximum_fusion.6
  969.2 1.8 pad_maximum_fusion.5
  970.9 1.7 pad_maximum_fusion.4
  972.6 1.7 pad_maximum_fusion.3
  974.4 9.2 pad_maximum_fusion.2
  983.6 9.1 pad_maximum_fusion.1
  992.7 9.1 pad_maximum_fusion
  (50 shorter events, 0.2 us)
Async XLA Ops:
  8.0 3.1 copy-start.8
  9.6 2.1 copy-start.20
  21.3 285.5 %all-to-all-start.1 = ((bf16[16,128,640]{2,1,0:T(8,128)(2,1)}), bf16[16,128,640]{2,1,0:T(8,128)(2,1)}, u32[]{:S(2)}, u32[]{:S(2)}) async-start(bf16[16,128,640]{2,1,0:T(8,128)(2,1)} %bitcast.77), calls=%async_computation.1 | async-start | bytes 5242880 | tf_op jit(solution)/shard_map/all_to_all | solution.py:739
  28.8 49.3 %collective-permute-start = (bf16[320,1024]{1,0:T(8,128)(2,1)S(1)}, bf16[320,1024]{1,0:T(8,128)(2,1)}, u32[]{:S(2)}, u32[]{:S(2)}) collective-permute-start(bf16[320,1024]{1,0:T(8,128)(2,1)S(1)} %dynamic-slice_bitcast_fusion.1), channel_id=1, source_target_pairs={{0,16},{1,17},{2,18},{3,19},{4,20},{5,21},{6,22},{7,23},{8,24},{9,... | collective-permute-start | bytes 1966088 | tf_op jit(solution)/shard_map/ppermute | solution.py:719
  33.4 58.7 %collective-permute-start.1 = (bf16[320,1024]{1,0:T(8,128)(2,1)}, bf16[320,1024]{1,0:T(8,128)(2,1)}, u32[]{:S(2)}, u32[]{:S(2)}) collective-permute-start(bf16[320,1024]{1,0:T(8,128)(2,1)} %dynamic-slice_bitcast_fusion), channel_id=1, source_target_pairs={{0,16},{1,17},{2,18},{3,19},{4,20},{5,21},{6,22},{7,23},{8,24},{9,... | collective-permute-start | bytes 1966088 | tf_op jit(solution)/shard_map/ppermute | solution.py:719
  306.7 5.8 copy-start.19
  306.7 42.2 %all-to-all-start = ((bf16[16,128,640]{2,1,0:T(8,128)(2,1)}), bf16[16,128,640]{2,1,0:T(8,128)(2,1)}, u32[]{:S(2)}, u32[]{:S(2)}) async-start(bf16[16,128,640]{2,1,0:T(8,128)(2,1)} %bitcast.78), calls=%async_computation | async-start | bytes 5242880 | tf_op jit(solution)/shard_map/all_to_all | solution.py:739
  312.5 654.0 %all-reduce.4.cloned.1.call-start = ((), (), s32[]{:S(2)}) async-start(), calls=%async_computation.5 | async-start | bytes 9502720 | tf_op jit(solution)/shard_map/psum | solution.py:764
  312.6 11.1 %copy-start.17 = (s32[2048]{0:T(1024)}, s32[2048]{0:T(1024)S(1)}, u32[]{:S(2)}) copy-start(s32[2048]{0:T(1024)S(1)} %broadcast_clamp_fusion.1) | copy-start | bytes 24580
  323.7 5.5 copy-start.22
  327.7 1.5 copy-start.12
  562.9 12.8 %copy-start.9 = (bf16[2048,640]{1,0:T(8,128)(2,1)S(1)}, bf16[2048,640]{1,0:T(8,128)(2,1)}, u32[]{:S(2)}) copy-start(bf16[2048,640]{1,0:T(8,128)(2,1)} %refs_5_.4) | copy-start | bytes 7864324
  575.8 4.3 copy-start.13
  580.1 3.2 copy-start.10
  583.2 1.7 copy-start.11
  583.2 391.1 %all-gather.8.cloned.1.call-start = ((), (), s32[]{:S(2)}) async-start(), calls=%async_computation.4 | async-start | bytes 5898240 | tf_op jit(solution)/shard_map/all_gather | solution.py:758
  583.8 399.8 %all-gather.6.cloned.1.call-start = ((), (), s32[]{:S(2)}) async-start(), calls=%async_computation.3 | async-start | bytes 5898240 | tf_op jit(solution)/shard_map/all_gather | solution.py:758
  584.4 408.3 %all-gather.4.cloned.1.call-start = ((), (), s32[]{:S(2)}) async-start(), calls=%async_computation.2 | async-start | bytes 5898240 | tf_op jit(solution)/shard_map/all_gather | solution.py:758
  590.3 216.9 %copy-start.18 = (s32[2048]{0:T(1024)S(1)}, s32[2048]{0:T(1024)}, u32[]{:S(2)}) copy-start(s32[2048]{0:T(1024)} %copy-done.17) | copy-start | bytes 24580
  818.7 4.3 copy-start.23
  823.0 3.8 copy-start.21
  826.7 2.3 copy-start.2
  826.7 2.3 copy-start.3
  826.7 2.3 copy-start.4
  826.7 2.3 copy-start.5
  826.8 2.4 copy-start.6
  826.8 2.6 copy-start.7
  965.5 1.1 copy-start
  966.5 2.6 copy-start.1
  966.5 2.6 copy-start.16
  969.2 1.8 copy-start.15
  970.9 1.7 copy-start.14
Sparse Core Ops, SparseCore 0:
  583.4 321.8 all-reduce.3
Sparse Core Ops, SparseCore 1:
  585.6 103.1 all-gather.7
  690.5 85.2 all-gather.5
  777.5 40.3 all-gather.3

commit v5 on v4

--- a/solution.py
+++ b/solution.py
@@ -207,7 +207,7 @@
 
     experts, ws, got = take(3), take(3), take(2)
     recv_out, back, shared = take(3)
-    keep_out, next_out = take(3), take(3)
+    keep_out, next_out = take(3), take(1)
     send, recv, outs = take(3)
     shared_w, own_w, foreign_w = take(3), take(3), take(3)
     go_sem, get_sem, ret_sem, res_sem, swap_sem, down_sem, pass_sem, load_sem, save_sem = refs
@@ -215,7 +215,7 @@
     geo.entry_barrier()
     outbound = [Outbound(geo, part, send, recv, go_sem, get_sem) for part in range(2)]
     returns = [Return(geo, outs.at[part], back.at[part], ret_sem.at[part], res_sem.at[part]) for part in range(2)]
-    swap = WeightSwap(geo, 1, experts, next_out, swap_sem, range(3))
+    swap = WeightSwap(geo, 1, experts, next_out, swap_sem, (0,))
     down = WeightSwap(geo, 0, experts, foreign_w, down_sem, (2,))
     loads = []
     passes = []
@@ -307,9 +307,9 @@
     return pl.pallas_call(
         functools.partial(forward_kernel, ep, dp),
         name="forward_exchange",
-        out_shape=[jax.ShapeDtypeStruct((2, chips, 2, block, width), bf16), jax.ShapeDtypeStruct((2, members, block, width), bf16), jax.ShapeDtypeStruct((tokens, width), f32)] + expert + expert,
+        out_shape=[jax.ShapeDtypeStruct((2, chips, 2, block, width), bf16), jax.ShapeDtypeStruct((2, members, block, width), bf16), jax.ShapeDtypeStruct((tokens, width), f32)] + expert + expert[:1],
         in_specs=[inside, inside] + [anywhere] * 8,
-        out_specs=[anywhere, anywhere, inside] + [anywhere] * 6,
+        out_specs=[anywhere, anywhere, inside] + [anywhere] * 4,
         scratch_shapes=[pltpu.VMEM((2, members, block, width), bf16)]
         + [pltpu.VMEM((2, chips, 2, block, width), bf16) for _ in range(2)]
         + [pltpu.VMEM(s, bf16) for _ in range(3) for s in shapes]
@@ -357,7 +357,7 @@
     shared_out, own_out = take(3), take(3)
     source, send, x_buf, g_buf, dx_rows, dx_buf = take(6)
     weights, acc, stages, theirs, partner_in = take(3), take(3), take(3), take(3), take(3)
-    go_sem, get_sem, ret_sem, res_sem, partner_sem, load_sem, x_sem, g_sem, dx_sem, pair_sem = refs
+    go_sem, get_sem, ret_sem, res_sem, partner_sem, load_sem, x_sem, g_sem, dx_sem, pair_sem, pass_sem = refs
 
     geo = Geometry(ep, dp)
     geo.entry_barrier()
@@ -370,11 +370,16 @@
     outbound = [Outbound(geo, part, send, recv, go_sem, get_sem) for part in range(2)]
     returns = [Return(geo, dx_rows.at[part], back.at[part], ret_sem.at[part], res_sem.at[part]) for part in range(2)]
     pairs = [PairSum(geo, stages, theirs, pair_sem, expert) for expert in range(2)]
+    begins = (2 * per_set, 0)
     loads = []
     for which in range(3):
         loads.append(pltpu.make_async_copy(shared_w[which].at[layer], weights[which].at[2], load_sem.at[2, which]))
         loads.append(pltpu.make_async_copy(own_w[which].at[layer, geo.local], weights[which].at[0], load_sem.at[0, which]))
-        loads.append(pltpu.make_async_copy(foreign_w[which], weights[which].at[1], load_sem.at[1, which]))
+        whole = foreign_w[which].shape == weights[which].shape[1:]
+        rows = weights[which].at[1] if whole else weights[which].at[1, half_rows(weights[which].shape[1], geo.core)]
+        loads.append(pltpu.make_async_copy(foreign_w[which], rows, load_sem.at[1, which]))
+        if not whole:
+            loads.append(pltpu.make_async_remote_copy(src_ref=foreign_w[which], dst_ref=rows, send_sem=pass_sem.at[0, which], recv_sem=pass_sem.at[1, which], device_id=geo.sibling, device_id_type=MESH))
     for load in loads:
         load.start()
     fill.wait()
@@ -388,27 +393,30 @@
         return held[0].at[part, step, core]
 
     def fetch(i, slot):
-        @pl.when(i < per_set)
+        @pl.when(i // per_set == 1)
         def _():
-            at = pl.ds(pl.multiple_of(i * tile, tile), tile)
+            at = pl.ds(pl.multiple_of((i - per_set) * tile, tile), tile)
             pltpu.make_async_copy(mixed.at[at], x_buf.at[slot], x_sem.at[slot]).start()
             pltpu.make_async_copy(grad_y.at[at], g_buf.at[slot], g_sem.at[slot]).start()
 
         for part in range(2):
-            begin = (2 - part) * per_set
+            begin = begins[part]
 
             @pl.when((i >= begin) & (i < begin + per_set))
             def _(part=part, begin=begin):
                 step = i - begin
-                early = (step == EARLY[0]) | (step == EARLY[1]) | (step == EARLY[2])
-                pl.when(jnp.logical_not(early))(lambda: outbound[part].arrive(step))
+                if part == 1:
+                    outbound[part].arrive(step)
+                else:
+                    early = (step == EARLY[0]) | (step == EARLY[1]) | (step == EARLY[2])
+                    pl.when(jnp.logical_not(early))(lambda: outbound[part].arrive(step))
                 for core in range(2):
                     at = pl.ds(core * (tile // 2), tile // 2)
                     pltpu.make_async_copy(recv.at[part, step, core], moved.at[slot, at], moved_sem.at[slot]).start()
                     pltpu.make_async_copy(held_block(part, step, core), kept.at[slot, at], kept_sem.at[slot]).start()
 
     def store_shared(i):
-        return pltpu.make_async_copy(dx_buf.at[i % 2], shared_dx.at[pl.ds(pl.multiple_of(i * tile, tile), tile)], dx_sem.at[i % 2])
+        return pltpu.make_async_copy(dx_buf.at[i % 2], shared_dx.at[pl.ds(pl.multiple_of((i - per_set) * tile, tile), tile)], dx_sem.at[i % 2])
 
     def partner_copies():
         return [pltpu.make_async_remote_copy(src_ref=pairs[1].mine(which), dst_ref=partner_in[which], send_sem=partner_sem.at[0, which], recv_sem=partner_sem.at[1, which], device_id=geo.partner, device_id_type=MESH) for which in range(3)]
@@ -420,10 +428,9 @@
     @pl.loop(0, total)
     def _(i):
         slot = i % 2
-        which_set = 2 - i // per_set
-        for part, ahead in ((1, 3), (0, per_set + 4)):
-            for n, step in enumerate(EARLY):
-                pl.when(i == ahead + 2 * n)(functools.partial(outbound[part].arrive, step))
+        which_set = (i // per_set + 1) % 3
+        for n, step in enumerate(EARLY):
+            pl.when(i == per_set + 1 + 2 * n)(functools.partial(outbound[0].arrive, step))
         fetch(i + 1, (i + 1) % 2)
         pltpu.make_async_copy(mixed.at[pl.ds(0, tile)], x_buf.at[slot], x_sem.at[slot]).wait()
         pltpu.make_async_copy(mixed.at[pl.ds(0, tile)], g_buf.at[slot], g_sem.at[slot]).wait()
@@ -449,19 +456,19 @@
         acc[2][...] += contract_rows(hidden, g)
         dx = contract_cols(grad_one, w_one[...]) + contract_cols(grad_three, w_three[...])
 
-        @pl.when(i < per_set)
+        @pl.when(i // per_set == 1)
         def _():
-            pl.when(i >= 2)(lambda: store_shared(i - 2).wait())
+            pl.when(i >= per_set + 2)(lambda: store_shared(i - 2).wait())
             dx_buf[slot] = dx
             store_shared(i).start()
 
-        @pl.when(i == per_set - 1)
+        @pl.when(i == 2 * per_set - 1)
         def _():
             for a, out in zip(acc, shared_out):
                 out[...] = a[...].astype(jnp.bfloat16)
 
         for part in range(2):
-            begin = (2 - part) * per_set
+            begin = begins[part]
 
             @pl.when((i >= begin) & (i < begin + per_set))
             def _(part=part, begin=begin):
@@ -476,10 +483,10 @@
                 for a, stage in zip(acc, stages):
                     stage[part] = a[...].astype(jnp.bfloat16)
 
-        pl.when(i == 2 * per_set)(pairs[1].start)
-        pl.when(i == 2 * per_set + 1)(pairs[1].finish)
-
-        @pl.when(i == 2 * per_set + 2)
+        pl.when(i == per_set)(pairs[1].start)
+        pl.when(i == per_set + 1)(pairs[1].finish)
+
+        @pl.when(i == per_set + 2)
         def _():
             for copy in partner_copies():
                 copy.start()
@@ -490,8 +497,8 @@
     for which, copy in enumerate(partner_copies()):
         copy.wait()
         own_out[which][...] = (pairs[0].mine(which)[...].astype(jnp.float32) + partner_in[which][...].astype(jnp.float32)).astype(jnp.bfloat16)
-    store_shared(per_set - 2).wait()
-    store_shared(per_set - 1).wait()
+    store_shared(2 * per_set - 2).wait()
+    store_shared(2 * per_set - 1).wait()
     for part in range(2):
         outbound[part].wait_sends()
         returns[part].wait_all()
@@ -507,7 +514,7 @@
     bf16, f32 = jnp.bfloat16, jnp.float32
     anywhere = pl.BlockSpec(memory_space=pl.ANY)
     inside = pl.BlockSpec(memory_space=pltpu.VMEM)
-    shapes = [w.shape for w in foreign]
+    shapes = [w.shape[2:] for w in own]
     halves = [(s[0] // 2, s[1]) for s in shapes]
     like = jax.ShapeDtypeStruct
     by_step = like((2, chips, 2, block, width), bf16)
@@ -517,7 +524,7 @@
     scratch += [vmem((3,) + s, bf16) for s in shapes] + [vmem(s, f32) for s in shapes] + [vmem((2,) + s, bf16) for s in shapes]
     scratch += [vmem((2,) + s, bf16) for s in halves] + [vmem(s, bf16) for s in halves]
     dma = pltpu.SemaphoreType.DMA
-    scratch += [dma((2, chips, 2)), dma((2, chips, 2)), dma((2, chips, 2)), dma((2, members)), dma((2, 3)), dma((3, 3)), dma((2,)), dma((2,)), dma((2,)), dma((2, 2, 3))]
+    scratch += [dma((2, chips, 2)), dma((2, chips, 2)), dma((2, chips, 2)), dma((2, members)), dma((2, 3)), dma((3, 3)), dma((2,)), dma((2,)), dma((2,)), dma((2, 2, 3)), dma((2, 3))]
     operands = [slots, *held, rows, mixed, grad_y, *own, *foreign, *shared]
     flops = 2 * 8 * width * shapes[0][1] * (2 * members * block + tokens)
     return pl.pallas_call(
@@ -712,11 +719,12 @@
         shared = (ws_gate, ws_up, ws_down)
         core, local = lax.axis_index("dp") % 2, lax.axis_index("dp") // 2
 
-        got = []
-        for w in experts[:2]:
+        def my_half(layer, w):
             rows, columns = w.shape[2] // 2, w.shape[3]
-            mine = lax.dynamic_slice(w, (0, local, core * rows, 0), (1, 1, rows, columns)).reshape(rows, columns)
-            got.append(lax.ppermute(mine, ALL_AXES, to_partner))
+            return lax.dynamic_slice(w, (layer, local, core * rows, 0), (1, 1, rows, columns)).reshape(rows, columns)
+
+        got = [lax.ppermute(my_half(0, w), ALL_AXES, to_partner) for w in experts[:2]]
+        halves_two = [my_half(1, w) for w in experts[1:]]
 
         side = lax.axis_index("ep") // (ep // 2)
         turned = (slot_ids.reshape(2, tokens) + side * tokens) % slots
@@ -734,16 +742,18 @@
         def gated(grad, layer):
             return (gate_vals[layer] * grad.astype(jnp.float32)).astype(jnp.bfloat16)
 
-        def go_out(part, rows):
-            blocks = take_rows(rows, owner[part].reshape(-1)).reshape(members, block, width)
+        def go_out(blocks):
             return lax.all_to_all(blocks, ALL_AXES, 0, 0, axis_index_groups=groups)
 
         grads_two = extended(gated(grad_out, 1))
-        grads_first = go_out(1, grads_two)
+        grads_two = [take_rows(grads_two, owner[part].reshape(-1)).reshape(members, block, width) for part in range(2)]
+        grads_first = go_out(grads_two[1])
         mixed_one = mix(act_in, 0)
+        mixed_one, grads_late = lax.optimization_barrier((mixed_one, grads_two[0]))
         recv, back, shared_y, *foreign = forward_exchange(mesh, turned[0:1], mixed_one, experts, shared, got)
-        back, grads_two = lax.optimization_barrier((back, grads_two))
-        grads_second = go_out(0, grads_two)
+        back, grads_late, halves_two = lax.optimization_barrier((back, grads_late, halves_two))
+        grads_second = go_out(grads_late)
+        got_two = [lax.ppermute(half, ALL_AXES, to_partner) for half in halves_two]
         routed = from_slots(0, back)
         act_two = (mixed_one.astype(jnp.float32) + gate_vals[0] * routed + shared_y).astype(jnp.bfloat16)
         mixed_two = mix(act_two, 1)
@@ -757,7 +767,7 @@
         def gather(half):
             return lax.all_gather(half, "dp", axis=0, tiled=True).reshape((dp // 2, 2 * half.shape[0], half.shape[1]))
 
-        out = backward_exchange(mesh, 1, turned[1:2], [grads_second, grads_first], mixed_two, mixed_two, grad_out, experts, foreign[3:], shared)
+        out = backward_exchange(mesh, 1, turned[1:2], [grads_second, grads_first], mixed_two, mixed_two, grad_out, experts, [foreign[3], *got_two], shared)
         shared_two, own_two = out[3:6], out[6:9]
         experts_two = [gather(half) for half in own_two]
         grad_one, dense_two = finish(1, act_two, grad_out, out[0], out[1])

time: 1020 us -> 1010 us (level)
  Pallas kernels: 772 us -> 751 us
  waiting for transfers between devices: 68.6 us -> 80.2 us
    pallas_call x1, Pallas kernels: 205 us -> 167 us  [forward_exchange(): pl.pallas_call(functools.partial(forward_kernel, ep, dp), name='forward_e...]
    ppermute x2 -> x4, waiting for transfers between devices: 51.5 us -> 73.5 us  [the longest x2 39.7 us: body(): lax.ppermute(my_half(0, w), ALL_AXES, to_partner)]
    pallas_call x2, Pallas kernels: 431 us -> 449 us  [backward_exchange(): pl.pallas_call(functools.partial(backward_kernel, ep, dp, layer), name='b...]
    all_to_all x2, waiting for transfers between devices: 16.1 us -> 5.59 us  [go_out(): return lax.all_to_all(blocks, ALL_AXES, 0, 0, axis_index_groups=groups)]
  transfers between devices with their start and end apart: 8 -> 10, of which waited for: 3 -> 5; matrix products, arithmetic and copies ran while one was open for 9% -> 9% of each run, Pallas kernels for 55% -> 53%
where the time goes in v5:
time: 1010 us; the launch traced here: 1000 us
  Pallas kernels  751 us (74%)
  waiting for transfers between devices  80.2 us (8%)
  local copies, waits for them, and re-layouts  63.5 us (6%)
  other arithmetic  49.4 us (5%)
  matrix products  25.3 us (3%)
  starting transfers between devices  16.9 us (2%)
  between operations  16.5 us (2%)
    pallas_call x2, Pallas kernels, backward_exchange(): pl.pallas_call(functools.partial(backward_kernel, ep, dp, layer), name='b...  449 us
    pallas_call x1, Pallas kernels, forward_exchange(): pl.pallas_call(functools.partial(forward_kernel, ep, dp), name='forward_e...  167 us
    pallas_call x1, Pallas kernels, final_exchange(): pl.pallas_call(functools.partial(final_kernel, ep, dp), name='final_excha...  134 us
    gather x5, local copies, waits for them, and re-layouts, take_rows(): return jnp.take(source, index, axis=0, mode='clip')  54 us
    ppermute x2, waiting for transfers between devices, body(): lax.ppermute(my_half(0, w), ALL_AXES, to_partner)  39.7 us
    ppermute x2, waiting for transfers between devices, body(): got_two = [lax.ppermute(half, ALL_AXES, to_partner) for half in halves_two]  33.8 us
    another operation x3, other arithmetic, body(): expert_out = [jnp.stack(pair) for pair in zip(experts_one, experts_two)]  27.4 us
  transfers between devices with their start and end apart: 10, of which 5 were waited for; matrix products, arithmetic and copies ran while one was open for 9% of the time, Pallas kernels for 53%

profile of v5, /device:TPU:0, one launch (start us, length us, event | category | flops | bytes accessed | tf_op | source)
XLA Modules:
  0.0 1002.8 jit_solution(10282086263972881957)
XLA Ops:
  8.1 0.9 and_select_fusion.2
  9.0 0.6 fusion.35
  9.6 0.1 pad.21.clone
  9.7 0.1 maximum_maximum_fusion
  9.8 0.1 broadcast_multiply_fusion
  9.9 0.4 fusion.7
  10.3 0.1 fusion.27
  10.3 0.7 fusion.34
  11.1 0.1 reshape.340
  11.1 0.5 fusion
  11.7 0.2 pad.4
  11.9 9.3 gather_fusion.1
  21.2 6.4 all-to-all-start.1
  27.6 2.4 dynamic-slice_bitcast_fusion.1
  30.1 2.6 collective-permute-start.1
  32.7 2.0 dynamic-slice_bitcast_fusion.3
  34.6 0.3 collective-permute-start
  35.0 0.1 reshape.332
  35.0 9.3 gather_fusion
  44.4 6.8 add_convert_fusion.4.mixed.refs_3_
  51.2 1.1 dynamic-slice_bitcast_fusion
  52.3 25.9 %collective-permute-done.1.refs_7_ = bf16[320,1024]{1,0:T(8,128)(2,1)} collective-permute-done((bf16[320,1024]{1,0:T(8,128)(2,1)}, bf16[320,1024]{1,0:T(8,128)(2,1)}, u32[]{:S(2)}, u32[]{:S(2)}) %collective-permute-start.1) | collective-permute-done | bytes 655392 | tf_op jit(solution)/shard_map/ppermute | solution.py:726
  78.2 13.9 %collective-permute-done.refs_6_ = bf16[320,1024]{1,0:T(8,128)(2,1)} collective-permute-done((bf16[320,1024]{1,0:T(8,128)(2,1)}, bf16[320,1024]{1,0:T(8,128)(2,1)}, u32[]{:S(2)}, u32[]{:S(2)}) %collective-permute-start) | collective-permute-done | bytes 655392 | tf_op jit(solution)/shard_map/ppermute | solution.py:726
  92.1 167.3 %forward_exchange.1 = (bf16[2,8,2,128,640]{4,3,2,1,0:T(8,128)(2,1)}, bf16[2,16,128,640]{3,2,1,0:T(8,128)(2,1)}, f32[2048,640]{1,0:T(8,128)}, bf16[640,1024]{1,0:...) custom-call(s32[1,2048]{1,0:T(1,128)} %get-tuple-element.91.slots.refs_0_, ...), custom_call_target="tpu_custom_call" | custom-call | flops 24159191040 | bytes 41943040 | tf_op jit(solution)/shard_map/forward_exchange/pallas_call | solution.py:307
  259.4 4.5 all-to-all-start
  263.8 0.0 all-reduce.4.cloned.1.call-start
  263.9 0.1 collective-permute-start.2
  264.0 2.9 collective-permute-start.3
  266.9 11.1 %gather_fusion.2 = bf16[2048,640]{1,0:T(8,128)(2,1)S(1)} fusion(bf16[4096,640]{1,0:T(8,128)(2,1)} %bitcast.80, s32[2048]{0:T(1024)S(1)} %broadcast_clamp_fusion.1), kind=kCustom, calls=%fused_computation.2 | custom fusion | bytes 5251072 | tf_op jit(solution)/shard_map/jit(_take)/gather | solution.py:688
  278.0 3.9 add_convert_fusion.3
  282.0 3.7 add_convert_fusion.2.refs_3_.refs_4_
  285.7 19.9 %collective-permute-done.2.refs_10_ = bf16[320,1024]{1,0:T(8,128)(2,1)} collective-permute-done((bf16[320,1024]{1,0:T(8,128)(2,1)}, bf16[320,1024]{1,0:T(8,128)(2,1)}, u32[]{:S(2)}, u32[]{:S(2)}) %collective-permute-start.2) | collective-permute-done | bytes 655392 | tf_op jit(solution)/shard_map/ppermute | solution.py:756
  305.6 13.9 %collective-permute-done.3.refs_11_ = bf16[512,640]{1,0:T(8,128)(2,1)} collective-permute-done((bf16[512,640]{1,0:T(8,128)(2,1)S(1)}, bf16[512,640]{1,0:T(8,128)(2,1)}, u32[]{:S(2)}, u32[]{:S(2)}) %collective-permute-start.3) | collective-permute-done | bytes 655392 | tf_op jit(solution)/shard_map/ppermute | solution.py:756
  319.5 5.6 all-to-all-done.refs_1_
  325.1 216.0 %backward_second.1 = (bf16[2,16,128,640]{3,2,1,0:T(8,128)(2,1)}, f32[2048,640]{1,0:T(8,128)}, bf16[2,8,2,128,640]{4,3,2,1,0:T(8,128)(2,1)}, bf16[640,1024]{1,0:T...) custom-call(s32[1,2048]{1,0:T(1,128)} %copy-done.20, ...), custom_call_target="tpu_custom_call" | custom-call | flops 64424509440 | bytes 62914560 | tf_op jit(solution)/shard_map/backward_second/pallas_call | solution.py:530
  541.1 12.8 %gather_fusion.3 = bf16[2048,640]{1,0:T(8,128)(2,1)} fusion(bf16[4096,640]{1,0:T(8,128)(2,1)} %bitcast.81, s32[2048]{0:T(1024)S(1)} %get-tuple-element.92), kind=kCustom, calls=%fused_computation.3 | custom fusion | bytes 5251072 | tf_op jit(solution)/shard_map/jit(_take)/gather | solution.py:688
  554.0 4.3 fusion.2
  558.3 3.1 fusion.6
  561.4 0.0 all-reduce.4.cloned.1.call-update
  561.4 0.0 all-gather.8.cloned.1.call-start
  561.5 0.5 all-gather.8.cloned.1.call-update
  562.0 0.0 all-gather.6.cloned.1.call-start
  562.0 0.5 all-gather.6.cloned.1.call-update
  562.6 0.0 all-gather.4.cloned.1.call-start
  562.6 0.5 copy-done.11
  563.1 5.3 fusion.3
  568.4 0.0 all-gather.4.cloned.1.call-update
  568.5 233.2 %backward_first.1 = (bf16[2,16,128,640]{3,2,1,0:T(8,128)(2,1)}, f32[2048,640]{1,0:T(8,128)}, bf16[2,8,2,128,640]{4,3,2,1,0:T(8,128)(2,1)}, bf16[640,1024]{1,0:T(...) custom-call(s32[1,2048]{1,0:T(1,128)} %get-tuple-element.91.slots.re, ...), custom_call_target="tpu_custom_call" | custom-call | flops 64424509440 | bytes 62914560 | tf_op jit(solution)/shard_map/backward_first/pallas_call | solution.py:530
  801.7 11.4 %gather_fusion.4 = bf16[2048,640]{1,0:T(8,128)(2,1)S(1)} fusion(bf16[4096,640]{1,0:T(8,128)(2,1)} %bitcast.82, s32[2048]{0:T(1024)S(1)} %copy-done.18), kind=kCustom, calls=%fused_computation.4 | custom fusion | bytes 5251072 | tf_op jit(solution)/shard_map/jit(_take)/gather | solution.py:688
  813.1 4.2 fusion.5
  817.3 3.7 add_convert_fusion
  821.1 2.2 convolution_convert_fusion.1
  823.4 0.1 copy-done.5
  823.5 0.2 copy-done.6
  823.7 0.2 copy-done.7
  824.0 134.5 %final_exchange.1 = (bf16[4,2,320,1024]{3,2,1,0:T(8,128)(2,1)}, bf16[4,2,320,1024]{3,2,1,0:T(8,128)(2,1)}, bf16[4,2,512,640]{3,2,1,0:T(8,128)(2,1)}, bf16[2,8,40...) custom-call(bf16[320,1024]{1,0:T(8,128)(2,1)S(1)} %copy-done.5, ...), custom_call_target="tpu_custom_call" | custom-call | flops 10000000000 | bytes 31457280 | tf_op jit(solution)/shard_map/final_exchange/pallas_call | solution.py:673
  958.5 1.0 copy-done
  959.5 2.6 pad_maximum_fusion.6
  962.2 1.8 pad_maximum_fusion.5
  963.9 1.7 pad_maximum_fusion.4
  965.6 1.7 pad_maximum_fusion.3
  967.4 9.2 pad_maximum_fusion.2
  976.6 9.1 pad_maximum_fusion.1
  985.7 9.1 pad_maximum_fusion
  (55 shorter events, 0.2 us)
Async XLA Ops:
  8.0 3.1 copy-start.8
  9.6 2.1 copy-start.20
  21.2 238.1 %all-to-all-start.1 = ((bf16[16,128,640]{2,1,0:T(8,128)(2,1)}), bf16[16,128,640]{2,1,0:T(8,128)(2,1)}, u32[]{:S(2)}, u32[]{:S(2)}) async-start(bf16[16,128,640]{2,1,0:T(8,128)(2,1)} %bitcast.83), calls=%async_computation.1 | async-start | bytes 5242880 | tf_op jit(solution)/shard_map/all_to_all | solution.py:746
  30.1 48.1 %collective-permute-start.1 = (bf16[320,1024]{1,0:T(8,128)(2,1)}, bf16[320,1024]{1,0:T(8,128)(2,1)}, u32[]{:S(2)}, u32[]{:S(2)}) collective-permute-start(bf16[320,1024]{1,0:T(8,128)(2,1)} %get-tuple-element.85), channel_id=1, source_target_pairs={{0,16},{1,17},{2,18},{3,19},{4,20},{5,21},{6,22},{7,23},{8,24},{9,... | collective-permute-start | bytes 1966088 | tf_op jit(solution)/shard_map/ppermute | solution.py:726
  34.6 57.4 %collective-permute-start = (bf16[320,1024]{1,0:T(8,128)(2,1)}, bf16[320,1024]{1,0:T(8,128)(2,1)}, u32[]{:S(2)}, u32[]{:S(2)}) collective-permute-start(bf16[320,1024]{1,0:T(8,128)(2,1)} %dynamic-slice_bitcast_fusion.3), channel_id=1, source_target_pairs={{0,16},{1,17},{2,18},{3,19},{4,20},{5,21},{6,22},{7,23},{8,24},{9,... | collective-permute-start | bytes 1966088 | tf_op jit(solution)/shard_map/ppermute | solution.py:726
  259.4 4.5 copy-start.19
  259.4 65.7 %all-to-all-start = ((bf16[16,128,640]{2,1,0:T(8,128)(2,1)}), bf16[16,128,640]{2,1,0:T(8,128)(2,1)}, u32[]{:S(2)}, u32[]{:S(2)}) async-start(bf16[16,128,640]{2,1,0:T(8,128)(2,1)} %bitcast.7), calls=%async_computation | async-start | bytes 5242880 | tf_op jit(solution)/shard_map/all_to_all | solution.py:746
  263.8 695.7 %all-reduce.4.cloned.1.call-start = ((), (), s32[]{:S(2)}) async-start(), calls=%async_computation.5 | async-start | bytes 9502720 | tf_op jit(solution)/shard_map/psum | solution.py:774
  263.9 14.1 %copy-start.17 = (s32[2048]{0:T(1024)}, s32[2048]{0:T(1024)S(1)}, u32[]{:S(2)}) copy-start(s32[2048]{0:T(1024)S(1)} %broadcast_clamp_fusion.1) | copy-start | bytes 24580
  263.9 41.7 %collective-permute-start.2 = (bf16[320,1024]{1,0:T(8,128)(2,1)}, bf16[320,1024]{1,0:T(8,128)(2,1)}, u32[]{:S(2)}, u32[]{:S(2)}) collective-permute-start(bf16[320,1024]{1,0:T(8,128)(2,1)} %get-tuple-element.51), channel_id=1, source_target_pairs={{0,16},{1,17},{2,18},{3,19},{4,20},{5,21},{6,22},{7,23},{8,24},{9,... | collective-permute-start | bytes 1966088 | tf_op jit(solution)/shard_map/ppermute | solution.py:756
  264.0 55.5 %collective-permute-start.3 = (bf16[512,640]{1,0:T(8,128)(2,1)S(1)}, bf16[512,640]{1,0:T(8,128)(2,1)}, u32[]{:S(2)}, u32[]{:S(2)}) collective-permute-start(bf16[512,640]{1,0:T(8,128)(2,1)S(1)} %dynamic-slice_bitcast_fusion), channel_id=1, source_target_pairs={{0,16},{1,17},{2,18},{3,19},{4,20},{5,21},{6,22},{7,23},{8,24},{9,... | collective-permute-start | bytes 1966088 | tf_op jit(solution)/shard_map/ppermute | solution.py:756
  278.0 4.0 copy-start.22
  282.0 3.7 copy-start.12
  541.1 12.8 %copy-start.9 = (bf16[2048,640]{1,0:T(8,128)(2,1)S(1)}, bf16[2048,640]{1,0:T(8,128)(2,1)}, u32[]{:S(2)}) copy-start(bf16[2048,640]{1,0:T(8,128)(2,1)} %refs_5_.4) | copy-start | bytes 7864324
  554.0 4.3 copy-start.13
  558.2 3.2 copy-start.10
  561.4 1.7 copy-start.11
  561.4 405.9 %all-gather.8.cloned.1.call-start = ((), (), s32[]{:S(2)}) async-start(), calls=%async_computation.4 | async-start | bytes 5898240 | tf_op jit(solution)/shard_map/all_gather | solution.py:768
  562.0 414.6 %all-gather.6.cloned.1.call-start = ((), (), s32[]{:S(2)}) async-start(), calls=%async_computation.3 | async-start | bytes 5898240 | tf_op jit(solution)/shard_map/all_gather | solution.py:768
  562.6 423.1 %all-gather.4.cloned.1.call-start = ((), (), s32[]{:S(2)}) async-start(), calls=%async_computation.2 | async-start | bytes 5898240 | tf_op jit(solution)/shard_map/all_gather | solution.py:768
  568.5 233.2 %copy-start.18 = (s32[2048]{0:T(1024)S(1)}, s32[2048]{0:T(1024)}, u32[]{:S(2)}) copy-start(s32[2048]{0:T(1024)} %copy-done.17) | copy-start | bytes 24580
  813.0 4.3 copy-start.23
  817.3 3.8 copy-start.21
  821.1 2.3 copy-start.2
  821.1 2.3 copy-start.3
  821.1 2.3 copy-start.4
  821.1 2.4 copy-start.5
  821.1 2.7 copy-start.6
  821.1 2.9 copy-start.7
  958.5 1.1 copy-start
  959.5 2.6 copy-start.1
  959.5 2.6 copy-start.16
  962.2 1.8 copy-start.15
  963.9 1.7 copy-start.14
Sparse Core Ops, SparseCore 0:
  561.5 325.6 all-reduce.3
Sparse Core Ops, SparseCore 1:
  563.8 107.3 all-gather.7
  672.9 75.5 all-gather.5
  750.2 58.8 all-gather.3

commit v6 on v5

--- a/solution.py
+++ b/solution.py
@@ -11,12 +11,8 @@
 ALL_AXES = ("ep", "dp")
 MESH = pl.DeviceIdType.MESH
 STEPS = 2
-ORDER = (0, 7, 3, 4, 5, 2, 1, 6)
+ORDER = (0, 1, 2, 4, 3, 6, 5, 7)
 ORDER_CODE = sum(mask * 8**step for step, mask in enumerate(ORDER))
-AT_ONCE = (1, 2, 4, 6)
-RELEASED = ((1, 3), (2, 5), (4, 7))
-EARLY = (1, 2, 4)
-PACK_CODE = sum(step * 8**n for n, step in enumerate((1, 2, 4, 6, 0, 3, 5, 7)))
 
 
 def contract_rows(left, right):
@@ -70,6 +66,12 @@
         pl.semaphore_wait(barrier, 2 * self.chips)
 
 
+def one_hot(part, chip, slots, block):
+    tokens = slots.shape[1]
+    wanted = part * tokens + chip * 2 * block + lax.broadcasted_iota(jnp.int32, (2 * block, tokens), 0)
+    return (wanted == slots[...]).astype(jnp.float32).astype(jnp.bfloat16)
+
+
 class Outbound:
     def __init__(self, geo, part, send, recv, send_sem, recv_sem):
         self.geo, self.part = geo, part
@@ -86,19 +88,14 @@
 
     def pack(self, slots, rows):
         geo = self.geo
-        tokens = rows.shape[0]
         block = self.send.shape[1]
 
         @pl.loop(0, geo.chips)
         def _(n):
-            power = (1 + 7 * (n % 2)) * (1 + 63 * (n // 2 % 2)) * (1 + 4095 * (n // 4))
-            chip = geo.at_step(PACK_CODE // power % 8)
-            base = self.part * tokens + chip * 2 * block
-            wanted = base + lax.broadcasted_iota(jnp.int32, (2 * block, tokens), 0)
-            pick = (wanted == slots[...]).astype(jnp.float32).astype(jnp.bfloat16)
+            chip = geo.at_step((n + 1) % geo.chips)
+            pick = one_hot(self.part, chip, slots, block)
             self.send[pl.ds(2 * chip, 2)] = dot32(pick, rows[...]).astype(jnp.bfloat16).reshape(2, block, rows.shape[1])
-            for when, step in enumerate(AT_ONCE):
-                pl.when(n == when + 1)(functools.partial(self.issue, step))
+            pl.when(n > 0)(functools.partial(self.issue, n))
 
         self.own().start()
         self.copy(0, 1 - geo.core).start()
@@ -110,12 +107,6 @@
     def arrive(self, step):
         for core in range(2):
             pltpu.make_async_copy(self.send.at[0], self.recv.at[step, core], self.recv_sem.at[step, core]).wait()
-        for trigger, later in RELEASED:
-            if isinstance(step, int):
-                if step == trigger:
-                    self.issue(later)
-            else:
-                pl.when(step == trigger)(functools.partial(self.issue, later))
 
     def wait_sends(self):
         self.copy(0, 1 - self.geo.core).wait_send()
@@ -147,18 +138,20 @@
             for core in range(2):
                 self.copy(step, core).start()
 
-    def wait_all(self):
-        geo = self.geo
-        self.copy(0, 1 - geo.core).wait_send()
-
-        @pl.loop(1, geo.chips)
+    def wait_sends(self):
+        self.copy(0, 1 - self.geo.core).wait_send()
+
+        @pl.loop(1, self.geo.chips)
         def _(step):
             for core in range(2):
                 self.copy(step, core).wait_send()
 
-        @pl.loop(0, 2 * geo.chips)
-        def _(index):
-            pltpu.make_async_copy(self.rows.at[0, 0], self.back.at[index], self.recv_sem.at[index]).wait()
+    def wait_back(self, index):
+        pltpu.make_async_copy(self.rows.at[0, 0], self.back.at[index], self.recv_sem.at[index]).wait()
+
+    def wait_all(self):
+        self.wait_sends()
+        pl.loop(0, 2 * self.geo.chips)(self.wait_back)
 
 
 def half_rows(rows, core):
@@ -197,7 +190,7 @@
     return value * jax.nn.sigmoid(value)
 
 
-def forward_kernel(ep, dp, slots, mixed, *refs):
+def forward_kernel(ep, dp, slots, gates, mixed, *refs):
     refs = list(refs)
 
     def take(count):
@@ -206,9 +199,9 @@
         return got
 
     experts, ws, got = take(3), take(3), take(2)
-    recv_out, back, shared = take(3)
+    recv_out, act = take(2)
     keep_out, next_out = take(3), take(1)
-    send, recv, outs = take(3)
+    send, recv, outs, back, shared, routed = take(6)
     shared_w, own_w, foreign_w = take(3), take(3), take(3)
     go_sem, get_sem, ret_sem, res_sem, swap_sem, down_sem, pass_sem, load_sem, save_sem = refs
     geo = Geometry(ep, dp)
@@ -276,9 +269,26 @@
         if part == 0:
             down.pass_on()
     swap.pass_on()
+    block = send.shape[2]
+    routed[...] = jnp.zeros(routed.shape, jnp.float32)
+    for part in range(2):
+
+        @pl.loop(0, geo.chips)
+        def _(step):
+            chip = geo.at_step(step)
+            for core in range(2):
+                returns[part].wait_back(2 * chip + core)
+            came = back[part, pl.ds(2 * chip, 2)].reshape(2 * block, width)
+            routed[...] += contract_rows(one_hot(part, chip, slots, block), came)
+
+    @pl.loop(0, mixed.shape[0] // tile)
+    def _(t):
+        at = pl.ds(pl.multiple_of(t * tile, tile), tile)
+        act[at, :] = (mixed[at, :].astype(jnp.float32) + gates[at, :] * routed[at, :] + shared[at, :]).astype(jnp.bfloat16)
+
     for part in range(2):
         outbound[part].wait_sends()
-        returns[part].wait_all()
+        returns[part].wait_sends()
 
         @pl.loop(0, geo.chips // STEPS)
         def _(t):
@@ -290,7 +300,7 @@
     swap.finish()
 
 
-def forward_exchange(mesh, slots, mixed, experts, shared, got):
+def forward_exchange(mesh, slots, gates, mixed, experts, shared, got):
     ep, dp = mesh.shape["ep"], mesh.shape["dp"]
     tokens, width = mixed.shape
     members = ep * dp // 2
@@ -307,16 +317,17 @@
     return pl.pallas_call(
         functools.partial(forward_kernel, ep, dp),
         name="forward_exchange",
-        out_shape=[jax.ShapeDtypeStruct((2, chips, 2, block, width), bf16), jax.ShapeDtypeStruct((2, members, block, width), bf16), jax.ShapeDtypeStruct((tokens, width), f32)] + expert + expert[:1],
-        in_specs=[inside, inside] + [anywhere] * 8,
-        out_specs=[anywhere, anywhere, inside] + [anywhere] * 4,
+        out_shape=[jax.ShapeDtypeStruct((2, chips, 2, block, width), bf16), jax.ShapeDtypeStruct((tokens, width), bf16)] + expert + expert[:1],
+        in_specs=[inside] * 3 + [anywhere] * 8,
+        out_specs=[anywhere, inside] + [anywhere] * 4,
         scratch_shapes=[pltpu.VMEM((2, members, block, width), bf16)]
         + [pltpu.VMEM((2, chips, 2, block, width), bf16) for _ in range(2)]
+        + [pltpu.VMEM((2, members, block, width), bf16), pltpu.VMEM((tokens, width), f32), pltpu.VMEM((tokens, width), f32)]
         + [pltpu.VMEM(s, bf16) for _ in range(3) for s in shapes]
         + [dma((2, chips, 2)), dma((2, chips, 2)), dma((2, chips, 2)), dma((2, members)), dma((4, 3)), dma((4, 3)), dma((2, 3)), dma((3, 3)), dma((2, chips // STEPS))],
         compiler_params=pltpu.CompilerParams(collective_id=0, has_side_effects=True, vmem_limit_bytes=60 * 2**20),
         cost_estimate=pl.CostEstimate(flops=flops, bytes_accessed=40 * 2**20, transcendentals=0),
-    )(slots, mixed, *experts, *shared, *got)
+    )(slots, gates, mixed, *experts, *shared, *got)
 
 
 class PairSum:
@@ -405,11 +416,7 @@
             @pl.when((i >= begin) & (i < begin + per_set))
             def _(part=part, begin=begin):
                 step = i - begin
-                if part == 1:
-                    outbound[part].arrive(step)
-                else:
-                    early = (step == EARLY[0]) | (step == EARLY[1]) | (step == EARLY[2])
-                    pl.when(jnp.logical_not(early))(lambda: outbound[part].arrive(step))
+                outbound[part].arrive(step)
                 for core in range(2):
                     at = pl.ds(core * (tile // 2), tile // 2)
                     pltpu.make_async_copy(recv.at[part, step, core], moved.at[slot, at], moved_sem.at[slot]).start()
@@ -429,8 +436,6 @@
     def _(i):
         slot = i % 2
         which_set = (i // per_set + 1) % 3
-        for n, step in enumerate(EARLY):
-            pl.when(i == per_set + 1 + 2 * n)(functools.partial(outbound[0].arrive, step))
         fetch(i + 1, (i + 1) % 2)
         pltpu.make_async_copy(mixed.at[pl.ds(0, tile)], x_buf.at[slot], x_sem.at[slot]).wait()
         pltpu.make_async_copy(mixed.at[pl.ds(0, tile)], g_buf.at[slot], g_sem.at[slot]).wait()
@@ -750,12 +755,10 @@
         grads_first = go_out(grads_two[1])
         mixed_one = mix(act_in, 0)
         mixed_one, grads_late = lax.optimization_barrier((mixed_one, grads_two[0]))
-        recv, back, shared_y, *foreign = forward_exchange(mesh, turned[0:1], mixed_one, experts, shared, got)
-        back, grads_late, halves_two = lax.optimization_barrier((back, grads_late, halves_two))
+        recv, act_two, *foreign = forward_exchange(mesh, turned[0:1], gate_vals[0], mixed_one, experts, shared, got)
+        act_two, grads_late, halves_two = lax.optimization_barrier((act_two, grads_late, halves_two))
         grads_second = go_out(grads_late)
         got_two = [lax.ppermute(half, ALL_AXES, to_partner) for half in halves_two]
-        routed = from_slots(0, back)
-        act_two = (mixed_one.astype(jnp.float32) + gate_vals[0] * routed + shared_y).astype(jnp.bfloat16)
         mixed_two = mix(act_two, 1)
 
         def finish(layer, act, grad_y, back, shared_dx):

time: 1010 us -> 949 us (0.940)
  Pallas kernels: 751 us -> 684 us
  waiting for transfers between devices: 80.2 us -> 92.7 us
    pallas_call x2, Pallas kernels: 449 us -> 386 us  [backward_exchange(): pl.pallas_call(functools.partial(backward_kernel, ep, dp, layer), name='b...]
    ppermute x2, waiting for transfers between devices: 33.8 us -> 52.6 us  [body(): got_two = [lax.ppermute(half, ALL_AXES, to_partner) for half in halves_two]]
    gather x5 -> x4, local copies, waits for them, and re-layouts: 54 us -> 42.8 us  [take_rows(): return jnp.take(source, index, axis=0, mode='clip')]
  transfers between devices with their start and end apart: 10 -> 10, of which waited for: 5 -> 4; matrix products, arithmetic and copies ran while one was open for 9% -> 9% of each run, Pallas kernels for 53% -> 53%
where the time goes in v6:
time: 949 us; the launch traced here: 939 us
  Pallas kernels  684 us (72%)
  waiting for transfers between devices  92.7 us (10%)
  local copies, waits for them, and re-layouts  53.7 us (6%)
  other arithmetic  45.5 us (5%)
  matrix products  28.5 us (3%)
  starting transfers between devices  19 us (2%)
  between operations  16.2 us (2%)
    pallas_call x2, Pallas kernels, backward_exchange(): pl.pallas_call(functools.partial(backward_kernel, ep, dp, layer), name='b...  386 us
    pallas_call x1, Pallas kernels, forward_exchange(): pl.pallas_call(functools.partial(forward_kernel, ep, dp), name='forward_e...  163 us
    pallas_call x1, Pallas kernels, final_exchange(): pl.pallas_call(functools.partial(final_kernel, ep, dp), name='final_excha...  134 us
    ppermute x2, waiting for transfers between devices, body(): got_two = [lax.ppermute(half, ALL_AXES, to_partner) for half in halves_two]  52.6 us
    gather x4, local copies, waits for them, and re-layouts, take_rows(): return jnp.take(source, index, axis=0, mode='clip')  42.8 us
    ppermute x2, waiting for transfers between devices, body(): lax.ppermute(my_half(0, w), ALL_AXES, to_partner)  39.1 us
    another operation x3, other arithmetic, body(): expert_out = [jnp.stack(pair) for pair in zip(experts_one, experts_two)]  27.4 us
  transfers between devices with their start and end apart: 10, of which 4 were waited for; matrix products, arithmetic and copies ran while one was open for 9% of the time, Pallas kernels for 53%

profile of v6, /device:TPU:0, one launch (start us, length us, event | category | flops | bytes accessed | tf_op | source)
XLA Modules:
  0.0 939.3 jit_solution(18001799547122595259)
XLA Ops:
  8.0 0.0 copy-start.8
  8.1 0.9 and_select_fusion.2
  9.0 0.6 fusion.32
  9.6 0.1 pad.21.clone
  9.7 0.1 maximum_maximum_fusion
  9.8 0.1 broadcast_multiply_fusion
  9.9 0.4 fusion.7
  10.3 0.1 fusion.24
  10.3 0.7 fusion.31
  11.1 0.1 reshape.336
  11.2 0.5 fusion
  11.7 0.2 pad.4
  11.9 9.3 gather_fusion.1
  21.3 6.4 all-to-all-start.1
  27.7 2.4 dynamic-slice_bitcast_fusion.1
  30.1 2.6 collective-permute-start.1
  32.7 1.1 dynamic-slice_bitcast_fusion.3
  33.8 0.4 collective-permute-start
  34.2 0.1 reshape.328
  34.3 9.3 gather_fusion
  43.6 6.8 add_convert_fusion.3.mixed.refs_3_
  50.4 1.3 copy.21.gates
  51.8 1.1 dynamic-slice_bitcast_fusion
  52.9 25.3 %collective-permute-done.1.refs_7_ = bf16[320,1024]{1,0:T(8,128)(2,1)} collective-permute-done((bf16[320,1024]{1,0:T(8,128)(2,1)}, bf16[320,1024]{1,0:T(8,128)(2,1)}, u32[]{:S(2)}, u32[]{:S(2)}) %collective-permute-start.1) | collective-permute-done | bytes 655392 | tf_op jit(solution)/shard_map/ppermute | solution.py:731
  78.2 13.8 %collective-permute-done.refs_6_ = bf16[320,1024]{1,0:T(8,128)(2,1)} collective-permute-done((bf16[320,1024]{1,0:T(8,128)(2,1)S(1)}, bf16[320,1024]{1,0:T(8,128)(2,1)}, u32[]{:S(2)}, u32[]{:S(2)}) %collective-permute-start) | collective-permute-done | bytes 655392 | tf_op jit(solution)/shard_map/ppermute | solution.py:731
  92.0 163.3 %forward_exchange.1 = (bf16[2,8,2,128,640]{4,3,2,1,0:T(8,128)(2,1)}, bf16[2048,640]{1,0:T(8,128)(2,1)}, bf16[640,1024]{1,0:T(8,128)(2,1)}, bf16[640,1024]{1,0:T(...) custom-call(s32[1,2048]{1,0:T(1,128)} %get-tuple-element.90.slots.refs_0_, f32[2048,1]{1,0:T(8,128)} %copy.21.gates, ...), custom_call_target="tpu_custom_call" | custom-call | flops 24159191040 | bytes 41943040 | tf_op jit(solution)/shard_map/forward_exchange/pallas_call | solution.py:317
  255.3 6.5 all-to-all-start
  261.8 0.0 all-reduce.4.cloned.1.call-start
  261.9 1.6 collective-permute-start.2
  263.5 1.4 collective-permute-start.3
  264.9 6.5 add_convert_fusion.2.refs_3_.refs_4_
  271.4 39.3 %collective-permute-done.2.refs_10_ = bf16[320,1024]{1,0:T(8,128)(2,1)S(1)} collective-permute-done((bf16[320,1024]{1,0:T(8,128)(2,1)S(1)}, bf16[320,1024]{1,0:T(8,128)(2,1)S(1)}, u32[]{:S(2)}, u32[]{:S(2)}) %collective-permute-start.2) | collective-permute-done | bytes 655392 | tf_op jit(solution)/shard_map/ppermute | solution.py:761
  310.7 0.8 copy-done.21
  311.6 13.2 %collective-permute-done.3.refs_11_ = bf16[512,640]{1,0:T(8,128)(2,1)} collective-permute-done((bf16[512,640]{1,0:T(8,128)(2,1)S(1)}, bf16[512,640]{1,0:T(8,128)(2,1)}, u32[]{:S(2)}, u32[]{:S(2)}) %collective-permute-start.3) | collective-permute-done | bytes 655392 | tf_op jit(solution)/shard_map/ppermute | solution.py:761
  324.8 183.9 %backward_second.1 = (bf16[2,16,128,640]{3,2,1,0:T(8,128)(2,1)}, f32[2048,640]{1,0:T(8,128)}, bf16[2,8,2,128,640]{4,3,2,1,0:T(8,128)(2,1)}, bf16[640,1024]{1,0:T...) custom-call(s32[1,2048]{1,0:T(1,128)} %copy-done.17, ...), custom_call_target="tpu_custom_call" | custom-call | flops 64424509440 | bytes 62914560 | tf_op jit(solution)/shard_map/backward_second/pallas_call | solution.py:535
  508.7 12.8 %gather_fusion.2 = bf16[2048,640]{1,0:T(8,128)(2,1)} fusion(bf16[4096,640]{1,0:T(8,128)(2,1)} %bitcast.79, s32[2048]{0:T(1024)S(1)} %get-tuple-element.91), kind=kCustom, calls=%fused_computation.2 | custom fusion | bytes 5251072 | tf_op jit(solution)/shard_map/jit(_take)/gather | solution.py:693
  521.6 4.3 fusion.2
  525.9 3.1 fusion.6
  529.0 0.0 all-reduce.4.cloned.1.call-update
  529.0 0.0 all-gather.8.cloned.1.call-start
  529.1 0.5 all-gather.8.cloned.1.call-update
  529.6 0.0 all-gather.6.cloned.1.call-start
  529.7 0.5 all-gather.6.cloned.1.call-update
  530.2 0.0 all-gather.4.cloned.1.call-start
  530.3 0.5 copy-done.11
  530.8 5.7 fusion.3
  536.5 0.0 all-gather.4.cloned.1.call-update
  536.5 202.2 %backward_first.1 = (bf16[2,16,128,640]{3,2,1,0:T(8,128)(2,1)}, f32[2048,640]{1,0:T(8,128)}, bf16[2,8,2,128,640]{4,3,2,1,0:T(8,128)(2,1)}, bf16[640,1024]{1,0:T(...) custom-call(s32[1,2048]{1,0:T(1,128)} %get-tuple-element.90.slots.re, ...), custom_call_target="tpu_custom_call" | custom-call | flops 64424509440 | bytes 62914560 | tf_op jit(solution)/shard_map/backward_first/pallas_call | solution.py:535
  738.7 11.3 %gather_fusion.3 = bf16[2048,640]{1,0:T(8,128)(2,1)S(1)} fusion(bf16[4096,640]{1,0:T(8,128)(2,1)} %bitcast.80, s32[2048]{0:T(1024)S(1)} %broadcast_clamp_fusion), kind=kCustom, calls=%fused_computation.3 | custom fusion | bytes 5251072 | tf_op jit(solution)/shard_map/jit(_take)/gather | solution.py:693
  750.0 4.3 fusion.5
  754.3 3.7 add_convert_fusion
  758.1 2.2 convolution_convert_fusion.1
  760.4 0.1 copy-done.5
  760.4 0.2 copy-done.6
  760.6 0.3 copy-done.7
  760.9 134.3 %final_exchange.1 = (bf16[4,2,320,1024]{3,2,1,0:T(8,128)(2,1)}, bf16[4,2,320,1024]{3,2,1,0:T(8,128)(2,1)}, bf16[4,2,512,640]{3,2,1,0:T(8,128)(2,1)}, bf16[2,8,40...) custom-call(bf16[320,1024]{1,0:T(8,128)(2,1)S(1)} %copy-done.5, ...), custom_call_target="tpu_custom_call" | custom-call | flops 10000000000 | bytes 31457280 | tf_op jit(solution)/shard_map/final_exchange/pallas_call | solution.py:678
  895.2 1.0 copy-done
  896.3 2.6 pad_maximum_fusion.6
  898.9 1.8 pad_maximum_fusion.5
  900.7 1.7 pad_maximum_fusion.4
  902.4 1.7 pad_maximum_fusion.3
  904.1 9.2 pad_maximum_fusion.2
  913.4 9.1 pad_maximum_fusion.1
  922.5 9.1 pad_maximum_fusion
  (52 shorter events, 0.2 us)
Async XLA Ops:
  8.0 3.2 copy-start.8
  9.6 2.1 copy-start.17
  21.3 234.0 %all-to-all-start.1 = ((bf16[16,128,640]{2,1,0:T(8,128)(2,1)}), bf16[16,128,640]{2,1,0:T(8,128)(2,1)}, u32[]{:S(2)}, u32[]{:S(2)}) async-start(bf16[16,128,640]{2,1,0:T(8,128)(2,1)} %bitcast.81), calls=%async_computation.1 | async-start | bytes 5242880 | tf_op jit(solution)/shard_map/all_to_all | solution.py:751
  30.1 48.1 %collective-permute-start.1 = (bf16[320,1024]{1,0:T(8,128)(2,1)}, bf16[320,1024]{1,0:T(8,128)(2,1)}, u32[]{:S(2)}, u32[]{:S(2)}) collective-permute-start(bf16[320,1024]{1,0:T(8,128)(2,1)} %get-tuple-element.83), channel_id=1, source_target_pairs={{0,16},{1,17},{2,18},{3,19},{4,20},{5,21},{6,22},{7,23},{8,24},{9,... | collective-permute-start | bytes 1966088 | tf_op jit(solution)/shard_map/ppermute | solution.py:731
  33.8 58.2 %collective-permute-start = (bf16[320,1024]{1,0:T(8,128)(2,1)S(1)}, bf16[320,1024]{1,0:T(8,128)(2,1)}, u32[]{:S(2)}, u32[]{:S(2)}) collective-permute-start(bf16[320,1024]{1,0:T(8,128)(2,1)S(1)} %dynamic-slice_bitcast_fusion.3), channel_id=1, source_target_pairs={{0,16},{1,17},{2,18},{3,19},{4,20},{5,21},{6,22},{7,23},{8,24},{9,... | collective-permute-start | bytes 1966088 | tf_op jit(solution)/shard_map/ppermute | solution.py:731
  255.3 6.6 copy-start.15
  255.3 9.6 %copy-start.19 = (bf16[2,640,640]{2,1,0:T(8,128)(2,1)S(1)}, bf16[2,640,640]{2,1,0:T(8,128)(2,1)}, u32[]{:S(2)}) copy-start(bf16[2,640,640]{2,1,0:T(8,128)(2,1)} %param.15) | copy-start | bytes 4915204
  255.3 69.5 %all-to-all-start = ((bf16[16,128,640]{2,1,0:T(8,128)(2,1)}), bf16[16,128,640]{2,1,0:T(8,128)(2,1)}, u32[]{:S(2)}, u32[]{:S(2)}) async-start(bf16[16,128,640]{2,1,0:T(8,128)(2,1)} %bitcast.8), calls=%async_computation | async-start | bytes 5242880 | tf_op jit(solution)/shard_map/all_to_all | solution.py:751
  261.8 634.4 %all-reduce.4.cloned.1.call-start = ((), (), s32[]{:S(2)}) async-start(), calls=%async_computation.5 | async-start | bytes 9502720 | tf_op jit(solution)/shard_map/psum | solution.py:777
  261.9 48.8 %collective-permute-start.2 = (bf16[320,1024]{1,0:T(8,128)(2,1)S(1)}, bf16[320,1024]{1,0:T(8,128)(2,1)S(1)}, u32[]{:S(2)}, u32[]{:S(2)}) collective-permute-start(bf16[320,1024]{1,0:T(8,128)(2,1)S(1)} %copy-done.15), channel_id=1, source_target_pairs={{0,16},{1,17},{2,18},{3,19},{4,20},{5,21},{6,22},{7,23},{8,24},{9,... | collective-permute-start | bytes 1966088 | tf_op jit(solution)/shard_map/ppermute | solution.py:761
  263.5 61.3 %collective-permute-start.3 = (bf16[512,640]{1,0:T(8,128)(2,1)S(1)}, bf16[512,640]{1,0:T(8,128)(2,1)}, u32[]{:S(2)}, u32[]{:S(2)}) collective-permute-start(bf16[512,640]{1,0:T(8,128)(2,1)S(1)} %dynamic-slice_bitcast_fusion), channel_id=1, source_target_pairs={{0,16},{1,17},{2,18},{3,19},{4,20},{5,21},{6,22},{7,23},{8,24},{9,... | collective-permute-start | bytes 1966088 | tf_op jit(solution)/shard_map/ppermute | solution.py:761
  310.7 0.8 copy-start.21
  508.7 12.8 %copy-start.9 = (bf16[2048,640]{1,0:T(8,128)(2,1)S(1)}, bf16[2048,640]{1,0:T(8,128)(2,1)}, u32[]{:S(2)}) copy-start(bf16[2048,640]{1,0:T(8,128)(2,1)} %refs_5_.4) | copy-start | bytes 7864324
  521.6 4.3 copy-start.22
  525.8 3.2 copy-start.10
  529.0 1.2 copy-start.16
  529.0 1.8 copy-start.11
  529.0 375.1 %all-gather.8.cloned.1.call-start = ((), (), s32[]{:S(2)}) async-start(), calls=%async_computation.4 | async-start | bytes 5898240 | tf_op jit(solution)/shard_map/all_gather | solution.py:771
  529.6 383.8 %all-gather.6.cloned.1.call-start = ((), (), s32[]{:S(2)}) async-start(), calls=%async_computation.3 | async-start | bytes 5898240 | tf_op jit(solution)/shard_map/all_gather | solution.py:771
  530.2 392.3 %all-gather.4.cloned.1.call-start = ((), (), s32[]{:S(2)}) async-start(), calls=%async_computation.2 | async-start | bytes 5898240 | tf_op jit(solution)/shard_map/all_gather | solution.py:771
  750.0 4.3 copy-start.20
  754.3 3.8 copy-start.18
  758.0 2.3 copy-start.2
  758.0 2.3 copy-start.3
  758.0 2.3 copy-start.4
  758.0 2.4 copy-start.5
  758.1 2.6 copy-start.6
  758.1 2.8 copy-start.7
  895.2 1.1 copy-start
  896.3 2.6 copy-start.1
  896.3 2.6 copy-start.14
  898.9 1.8 copy-start.13
  900.7 1.7 copy-start.12
Sparse Core Ops, SparseCore 0:
  529.2 297.8 all-reduce.3
Sparse Core Ops, SparseCore 1:
  531.4 107.1 all-gather.7
  640.3 78.7 all-gather.5
  720.8 43.8 all-gather.3

commit v7 on v6

--- a/solution.py
+++ b/solution.py
@@ -198,7 +198,7 @@
         del refs[:count]
         return got
 
-    experts, ws, got = take(3), take(3), take(2)
+    experts, ws, got = take(3), take(3), take(1)
     recv_out, act = take(2)
     keep_out, next_out = take(3), take(1)
     send, recv, outs, back, shared, routed = take(6)
@@ -209,13 +209,13 @@
     outbound = [Outbound(geo, part, send, recv, go_sem, get_sem) for part in range(2)]
     returns = [Return(geo, outs.at[part], back.at[part], ret_sem.at[part], res_sem.at[part]) for part in range(2)]
     swap = WeightSwap(geo, 1, experts, next_out, swap_sem, (0,))
-    down = WeightSwap(geo, 0, experts, foreign_w, down_sem, (2,))
+    down = WeightSwap(geo, 0, experts, foreign_w, down_sem, (1, 2))
     loads = []
     passes = []
     for which in range(3):
         loads.append(pltpu.make_async_copy(ws[which].at[0], shared_w[which], load_sem.at[0, which]))
         loads.append(pltpu.make_async_copy(experts[which].at[0, geo.local], own_w[which], load_sem.at[1, which]))
-    for which in range(2):
+    for which in range(1):
         mine = half_rows(foreign_w[which].shape[0], geo.core)
         loads.append(pltpu.make_async_copy(got[which], foreign_w[which].at[mine], load_sem.at[2, which]))
         passes.append(pltpu.make_async_remote_copy(src_ref=got[which], dst_ref=foreign_w[which].at[mine], send_sem=pass_sem.at[0, which], recv_sem=pass_sem.at[1, which], device_id=geo.sibling, device_id_type=MESH))
@@ -318,7 +318,7 @@
         functools.partial(forward_kernel, ep, dp),
         name="forward_exchange",
         out_shape=[jax.ShapeDtypeStruct((2, chips, 2, block, width), bf16), jax.ShapeDtypeStruct((tokens, width), bf16)] + expert + expert[:1],
-        in_specs=[inside] * 3 + [anywhere] * 8,
+        in_specs=[inside] * 3 + [anywhere] * 7,
         out_specs=[anywhere, inside] + [anywhere] * 4,
         scratch_shapes=[pltpu.VMEM((2, members, block, width), bf16)]
         + [pltpu.VMEM((2, chips, 2, block, width), bf16) for _ in range(2)]
@@ -364,11 +364,11 @@
     held = take(2 if layer else 1)
     rows_in, mixed, grad_y = take(3)
     own_w, foreign_w, shared_w = take(3), take(3), take(3)
-    back, shared_dx, recv = take(3)
+    back, grad_mixed, recv = take(3)
     shared_out, own_out = take(3), take(3)
-    source, send, x_buf, g_buf, dx_rows, dx_buf = take(6)
+    source, send, x_buf, g_buf, dx_rows, total, came = take(7)
     weights, acc, stages, theirs, partner_in = take(3), take(3), take(3), take(3), take(3)
-    go_sem, get_sem, ret_sem, res_sem, partner_sem, load_sem, x_sem, g_sem, dx_sem, pair_sem, pass_sem = refs
+    go_sem, get_sem, ret_sem, res_sem, partner_sem, load_sem, x_sem, g_sem, dx_sem, pair_sem, pass_sem, came_sem, keep_sem = refs
 
     geo = Geometry(ep, dp)
     geo.entry_barrier()
@@ -377,7 +377,7 @@
     fill.start()
     width = mixed.shape[1]
     per_set = mixed.shape[0] // tile
-    total = 3 * per_set
+    tiles = 3 * per_set
     outbound = [Outbound(geo, part, send, recv, go_sem, get_sem) for part in range(2)]
     returns = [Return(geo, dx_rows.at[part], back.at[part], ret_sem.at[part], res_sem.at[part]) for part in range(2)]
     pairs = [PairSum(geo, stages, theirs, pair_sem, expert) for expert in range(2)]
@@ -422,8 +422,7 @@
                     pltpu.make_async_copy(recv.at[part, step, core], moved.at[slot, at], moved_sem.at[slot]).start()
                     pltpu.make_async_copy(held_block(part, step, core), kept.at[slot, at], kept_sem.at[slot]).start()
 
-    def store_shared(i):
-        return pltpu.make_async_copy(dx_buf.at[i % 2], shared_dx.at[pl.ds(pl.multiple_of((i - per_set) * tile, tile), tile)], dx_sem.at[i % 2])
+    keeps = [pltpu.make_async_copy(stage.at[0], out, keep_sem.at[n]) for n, (stage, out) in enumerate(zip(stages, shared_out))]
 
     def partner_copies():
         return [pltpu.make_async_remote_copy(src_ref=pairs[1].mine(which), dst_ref=partner_in[which], send_sem=partner_sem.at[0, which], recv_sem=partner_sem.at[1, which], device_id=geo.partner, device_id_type=MESH) for which in range(3)]
@@ -432,7 +431,7 @@
     for load in loads:
         load.wait()
 
-    @pl.loop(0, total)
+    @pl.loop(0, tiles)
     def _(i):
         slot = i % 2
         which_set = (i // per_set + 1) % 3
@@ -463,14 +462,22 @@
 
         @pl.when(i // per_set == 1)
         def _():
-            pl.when(i >= per_set + 2)(lambda: store_shared(i - 2).wait())
-            dx_buf[slot] = dx
-            store_shared(i).start()
+            total[pl.ds(pl.multiple_of((i - per_set) * tile, tile), tile), :] = dx
 
         @pl.when(i == 2 * per_set - 1)
         def _():
-            for a, out in zip(acc, shared_out):
-                out[...] = a[...].astype(jnp.bfloat16)
+            for a, stage in zip(acc, stages):
+                stage[0] = a[...].astype(jnp.bfloat16)
+
+        @pl.when(i == 2 * per_set)
+        def _():
+            for keep in keeps:
+                keep.start()
+
+        @pl.when(i == tiles - 1)
+        def _():
+            for keep in keeps:
+                keep.wait()
 
         for part in range(2):
             begin = begins[part]
@@ -499,14 +506,45 @@
     returns[0].start(per_set - 1)
     pairs[0].start()
     pairs[0].finish()
+
+    block = tile // 2
+
+    def bring(part, step):
+        chip = geo.at_step(step)
+        for core in range(2):
+            returns[part].wait_back(2 * chip + core)
+            pltpu.make_async_copy(back.at[part, 2 * chip + core], came.at[step % 2, pl.ds(core * block, block)], came_sem.at[step % 2]).start()
+
+    for part in (1, 0):
+        bring(part, 0)
+
+        @pl.loop(0, geo.chips)
+        def _(step):
+            pl.when(step + 1 < geo.chips)(lambda: bring(part, step + 1))
+            pltpu.make_async_copy(mixed.at[pl.ds(0, tile)], came.at[step % 2], came_sem.at[step % 2]).wait()
+            total[...] += contract_rows(one_hot(part, geo.at_step(step), slots, block), came[step % 2])
+
+    def grad_tile(t):
+        return pltpu.make_async_copy(grad_y.at[pl.ds(pl.multiple_of(t * tile, tile), tile)], g_buf.at[t % 2], g_sem.at[t % 2])
+
+    grad_tile(0).start()
+
+    @pl.loop(0, per_set)
+    def _(t):
+        pl.when(t + 1 < per_set)(lambda: grad_tile(t + 1).start())
+        grad_tile(t).wait()
+        at = pl.ds(pl.multiple_of(t * tile, tile), tile)
+        source[at, :] = (g_buf[t % 2].astype(jnp.float32) + total[at, :]).astype(jnp.bfloat16)
+
     for which, copy in enumerate(partner_copies()):
         copy.wait()
         own_out[which][...] = (pairs[0].mine(which)[...].astype(jnp.float32) + partner_in[which][...].astype(jnp.float32)).astype(jnp.bfloat16)
-    store_shared(2 * per_set - 2).wait()
-    store_shared(2 * per_set - 1).wait()
+    store = pltpu.make_async_copy(source, grad_mixed, dx_sem.at[0])
+    store.start()
     for part in range(2):
         outbound[part].wait_sends()
-        returns[part].wait_all()
+        returns[part].wait_sends()
+    store.wait()
 
 
 def backward_exchange(mesh, layer, slots, held, rows, mixed, grad_y, own, foreign, shared):
@@ -523,13 +561,13 @@
     halves = [(s[0] // 2, s[1]) for s in shapes]
     like = jax.ShapeDtypeStruct
     by_step = like((2, chips, 2, block, width), bf16)
-    outs = [like((2, members, block, width), bf16), like((tokens, width), f32), by_step] + [like(s, bf16) for s in shapes + halves]
+    outs = [like((2, members, block, width), bf16), like((tokens, width), bf16), by_step] + [like(s, bf16) for s in shapes + halves]
     vmem = pltpu.VMEM
-    scratch = [vmem((tokens, width), bf16), vmem((2, members, block, width), bf16), vmem((2, tile, width), bf16), vmem((2, tile, width), bf16), vmem(by_step.shape, bf16), vmem((2, tile, width), f32)]
+    scratch = [vmem((tokens, width), bf16), vmem((2, members, block, width), bf16), vmem((2, tile, width), bf16), vmem((2, tile, width), bf16), vmem(by_step.shape, bf16), vmem((tokens, width), f32), vmem((2, tile, width), bf16)]
     scratch += [vmem((3,) + s, bf16) for s in shapes] + [vmem(s, f32) for s in shapes] + [vmem((2,) + s, bf16) for s in shapes]
     scratch += [vmem((2,) + s, bf16) for s in halves] + [vmem(s, bf16) for s in halves]
     dma = pltpu.SemaphoreType.DMA
-    scratch += [dma((2, chips, 2)), dma((2, chips, 2)), dma((2, chips, 2)), dma((2, members)), dma((2, 3)), dma((3, 3)), dma((2,)), dma((2,)), dma((2,)), dma((2, 2, 3)), dma((2, 3))]
+    scratch += [dma((2, chips, 2)), dma((2, chips, 2)), dma((2, chips, 2)), dma((2, members)), dma((2, 3)), dma((3, 3)), dma((2,)), dma((2,)), dma((2,)), dma((2, 2, 3)), dma((2, 3)), dma((2,)), dma((3,))]
     operands = [slots, *held, rows, mixed, grad_y, *own, *foreign, *shared]
     flops = 2 * 8 * width * shapes[0][1] * (2 * members * block + tokens)
     return pl.pallas_call(
@@ -537,7 +575,7 @@
         name="backward_second" if layer else "backward_first",
         out_shape=outs,
         in_specs=[inside] + [anywhere] * (len(operands) - 1),
-        out_specs=[anywhere] * 3 + [inside] * 6,
+        out_specs=[anywhere] * 6 + [inside] * 3,
         scratch_shapes=scratch,
         compiler_params=pltpu.CompilerParams(collective_id=1 + layer, has_side_effects=True, vmem_limit_bytes=63 * 2**20),
         cost_estimate=pl.CostEstimate(flops=flops, bytes_accessed=60 * 2**20, transcendentals=0),
@@ -728,7 +766,7 @@
             rows, columns = w.shape[2] // 2, w.shape[3]
             return lax.dynamic_slice(w, (layer, local, core * rows, 0), (1, 1, rows, columns)).reshape(rows, columns)
 
-        got = [lax.ppermute(my_half(0, w), ALL_AXES, to_partner) for w in experts[:2]]
+        got = [lax.ppermute(my_half(0, w), ALL_AXES, to_partner) for w in experts[:1]]
         halves_two = [my_half(1, w) for w in experts[1:]]
 
         side = lax.axis_index("ep") // (ep // 2)
@@ -738,9 +776,6 @@
         def extended(rows):
             return jnp.pad(rows, ((0, 8), (0, 0)))
 
-        def from_slots(layer, back):
-            return take_rows(back.reshape(slots, width), turned[layer]).astype(jnp.float32)
-
         def mix(act, layer):
             return (act.astype(jnp.float32) + dot32(act, w_dense[layer])).astype(jnp.bfloat16)
 
@@ -751,19 +786,15 @@
             return lax.all_to_all(blocks, ALL_AXES, 0, 0, axis_index_groups=groups)
 
         grads_two = extended(gated(grad_out, 1))
-        grads_two = [take_rows(grads_two, owner[part].reshape(-1)).reshape(members, block, width) for part in range(2)]
-        grads_first = go_out(grads_two[1])
+        grads_first = go_out(take_rows(grads_two, owner[1].reshape(-1)).reshape(members, block, width))
         mixed_one = mix(act_in, 0)
-        mixed_one, grads_late = lax.optimization_barrier((mixed_one, grads_two[0]))
         recv, act_two, *foreign = forward_exchange(mesh, turned[0:1], gate_vals[0], mixed_one, experts, shared, got)
-        act_two, grads_late, halves_two = lax.optimization_barrier((act_two, grads_late, halves_two))
-        grads_second = go_out(grads_late)
+        act_two, grads_two, halves_two = lax.optimization_barrier((act_two, grads_two, halves_two))
+        grads_second = go_out(take_rows(grads_two, owner[0].reshape(-1)).reshape(members, block, width))
         got_two = [lax.ppermute(half, ALL_AXES, to_partner) for half in halves_two]
         mixed_two = mix(act_two, 1)
 
-        def finish(layer, act, grad_y, back, shared_dx):
-            routed = from_slots(layer, back)
-            grad_mixed = (grad_y.astype(jnp.float32) + routed + shared_dx).astype(jnp.bfloat16)
+        def finish(layer, act, grad_mixed):
             g_dense = contract_rows(act, grad_mixed).astype(jnp.bfloat16)
             return (grad_mixed.astype(jnp.float32) + contract_cols(grad_mixed, w_dense[layer])).astype(jnp.bfloat16), g_dense
 
@@ -773,12 +804,12 @@
         out = backward_exchange(mesh, 1, turned[1:2], [grads_second, grads_first], mixed_two, mixed_two, grad_out, experts, [foreign[3], *got_two], shared)
         shared_two, own_two = out[3:6], out[6:9]
         experts_two = [gather(half) for half in own_two]
-        grad_one, dense_two = finish(1, act_two, grad_out, out[0], out[1])
+        grad_one, dense_two = finish(1, act_two, out[1])
         sums_two = [lax.psum(part, ALL_AXES) for part in (dense_two, *shared_two)]
 
         out = backward_exchange(mesh, 0, turned[0:1], [recv], gated(grad_one, 0), mixed_one, grad_one, experts, foreign[:3], shared)
         shared_one, own_one = out[3:6], out[6:9]
-        grad_act, dense_one = finish(0, act_in, grad_one, out[0], out[1])
+        grad_act, dense_one = finish(0, act_in, out[1])
         experts_one, sums_one = final_exchange(mesh, own_one, [dense_one, *shared_one])
 
         expert_out = [jnp.stack(pair) for pair in zip(experts_one, experts_two)]

time: 949 us -> 968 us (1.020)
  Pallas kernels: 684 us -> 731 us
  local copies, waits for them, and re-layouts: 53.7 us -> 29.5 us
    gather x4 -> x2, local copies, waits for them, and re-layouts: 42.8 us -> 18.7 us  [take_rows(): return jnp.take(source, index, axis=0, mode='clip')]
    pallas_call x2, Pallas kernels: 386 us -> 405 us  [backward_exchange(): pl.pallas_call(functools.partial(backward_kernel, ep, dp, layer), name='b...]
    pallas_call x1, Pallas kernels: 163 us -> 182 us  [forward_exchange(): pl.pallas_call(functools.partial(forward_kernel, ep, dp), name='forward_e...]
    ppermute x2 -> x1, waiting for transfers between devices: 39.1 us -> 34.5 us  [body(): lax.ppermute(my_half(0, w), ALL_AXES, to_partner)]
  transfers between devices with their start and end apart: 10 -> 9, of which waited for: 4 -> 3; matrix products, arithmetic and copies ran while one was open for 9% -> 8% of each run, Pallas kernels for 53% -> 56%
where the time goes in v7:
time: 968 us; the launch traced here: 957 us
  Pallas kernels  731 us (76%)
  waiting for transfers between devices  87.5 us (9%)
  other arithmetic  37 us (4%)
  matrix products  36 us (4%)
  local copies, waits for them, and re-layouts  29.5 us (3%)
  starting transfers between devices  19.4 us (2%)
  between operations  16.3 us (2%)
    pallas_call x2, Pallas kernels, backward_exchange(): pl.pallas_call(functools.partial(backward_kernel, ep, dp, layer), name='b...  405 us
    pallas_call x1, Pallas kernels, forward_exchange(): pl.pallas_call(functools.partial(forward_kernel, ep, dp), name='forward_e...  182 us
    pallas_call x1, Pallas kernels, final_exchange(): pl.pallas_call(functools.partial(final_kernel, ep, dp), name='final_excha...  144 us
    ppermute x2, waiting for transfers between devices, body(): got_two = [lax.ppermute(half, ALL_AXES, to_partner) for half in halves_two]  51.9 us
    ppermute x1, waiting for transfers between devices, body(): lax.ppermute(my_half(0, w), ALL_AXES, to_partner)  34.5 us
    another operation x3, other arithmetic, body(): expert_out = [jnp.stack(pair) for pair in zip(experts_one, experts_two)]  27.4 us
  transfers between devices with their start and end apart: 9, of which 3 were waited for; matrix products, arithmetic and copies ran while one was open for 8% of the time, Pallas kernels for 56%

profile of v7, /device:TPU:0, one launch (start us, length us, event | category | flops | bytes accessed | tf_op | source)
XLA Modules:
  0.0 956.9 jit_solution(8120046743709086657)
XLA Ops:
  8.0 0.0 copy-start.8
  8.1 0.9 and_select_fusion.2
  9.0 0.6 fusion.29
  9.6 0.7 fusion.28
  10.4 0.1 pad.21.clone
  10.5 0.1 maximum_maximum_fusion
  10.5 0.1 broadcast_multiply_fusion
  10.6 0.4 fusion.1
  11.0 0.1 fusion.21
  11.1 0.1 reshape.322
  11.2 0.5 multiply_convert_fusion.1
  11.7 0.0 copy-done.13
  11.7 0.2 pad.4
  11.9 9.3 gather_fusion.1
  21.3 6.4 all-to-all-start.1
  27.7 2.0 dynamic-slice_bitcast_fusion.2
  29.6 2.6 collective-permute-start
  32.2 0.1 reshape.314
  32.3 1.1 dynamic-slice_bitcast_fusion.1
  33.4 1.3 copy.21.gates
  34.8 2.0 dynamic-slice_bitcast_fusion
  36.8 6.8 add_convert_fusion.3.mixed.refs_3_
  43.6 34.5 %collective-permute-done.refs_6_ = bf16[320,1024]{1,0:T(8,128)(2,1)} collective-permute-done((bf16[320,1024]{1,0:T(8,128)(2,1)}, bf16[320,1024]{1,0:T(8,128)(2,1)}, u32[]{:S(2)}, u32[]{:S(2)}) %collective-permute-start) | collective-permute-done | bytes 655392 | tf_op jit(solution)/shard_map/ppermute | solution.py:769
  78.1 182.0 %forward_exchange.1 = (bf16[2,8,2,128,640]{4,3,2,1,0:T(8,128)(2,1)}, bf16[2048,640]{1,0:T(8,128)(2,1)}, bf16[640,1024]{1,0:T(8,128)(2,1)}, bf16[640,1024]{1,0:T(...) custom-call(s32[1,2048]{1,0:T(1,128)} %get-tuple-element.80.slots.refs_0_, f32[2048,1]{1,0:T(8,128)} %copy.21.gates, ...), custom_call_target="tpu_custom_call" | custom-call | flops 24159191040 | bytes 41943040 | tf_op jit(solution)/shard_map/forward_exchange/pallas_call | solution.py:317
  260.1 9.3 gather_fusion
  269.4 0.0 all-to-all-done.1.refs_2_
  269.4 7.3 all-to-all-start
  276.7 0.0 all-reduce.4.cloned.1.call-start
  276.8 0.1 collective-permute-start.1
  276.9 2.9 collective-permute-start.2
  279.8 6.5 add_convert_fusion.2.refs_3_.refs_4_
  286.3 38.9 %collective-permute-done.1.refs_10_ = bf16[320,1024]{1,0:T(8,128)(2,1)S(1)} collective-permute-done((bf16[320,1024]{1,0:T(8,128)(2,1)S(1)}, bf16[320,1024]{1,0:T(8,128)(2,1)S(1)}, u32[]{:S(2)}, u32[]{:S(2)}) %collective-permute-start.1) | collective-permute-done | bytes 655392 | tf_op jit(solution)/shard_map/ppermute | solution.py:794
  325.2 0.8 copy-done.17
  326.0 13.0 %collective-permute-done.2.refs_11_ = bf16[512,640]{1,0:T(8,128)(2,1)} collective-permute-done((bf16[512,640]{1,0:T(8,128)(2,1)S(1)}, bf16[512,640]{1,0:T(8,128)(2,1)}, u32[]{:S(2)}, u32[]{:S(2)}) %collective-permute-start.2) | collective-permute-done | bytes 655392 | tf_op jit(solution)/shard_map/ppermute | solution.py:794
  339.1 0.0 all-to-all-done.refs_1_
  339.1 198.2 %backward_second.1 = (bf16[2,16,128,640]{3,2,1,0:T(8,128)(2,1)}, bf16[2048,640]{1,0:T(8,128)(2,1)}, bf16[2,8,2,128,640]{4,3,2,1,0:T(8,128)(2,1)}, bf16[640,1024]...) custom-call(s32[1,2048]{1,0:T(1,128)} %copy-done.13, ...), custom_call_target="tpu_custom_call" | custom-call | flops 64424509440 | bytes 62914560 | tf_op jit(solution)/shard_map/backward_second/pallas_call | solution.py:573
  537.2 5.7 fusion
  542.9 0.0 all-reduce.4.cloned.1.call-update
  542.9 0.0 all-gather.8.cloned.1.call-start
  543.0 0.5 all-gather.8.cloned.1.call-update
  543.5 0.0 all-gather.6.cloned.1.call-start
  543.6 0.5 all-gather.6.cloned.1.call-update
  544.1 0.0 all-gather.4.cloned.1.call-start
  544.1 0.2 copy-done.16
  544.3 7.4 multiply_convert_fusion
  551.7 0.0 all-gather.4.cloned.1.call-update
  551.7 207.1 %backward_first.1 = (bf16[2,16,128,640]{3,2,1,0:T(8,128)(2,1)}, bf16[2048,640]{1,0:T(8,128)(2,1)}, bf16[2,8,2,128,640]{4,3,2,1,0:T(8,128)(2,1)}, bf16[640,1024]{...) custom-call(s32[1,2048]{1,0:T(1,128)} %get-tuple-element.80.slots.re, ...), custom_call_target="tpu_custom_call" | custom-call | flops 64424509440 | bytes 62914560 | tf_op jit(solution)/shard_map/backward_first/pallas_call | solution.py:573
  758.9 0.0 copy-start.14
  758.9 0.0 copy-start.18
  758.9 7.0 add_convert_fusion
  766.0 2.2 convolution_convert_fusion.1
  768.3 0.1 copy-done.5
  768.4 0.2 copy-done.6
  768.6 0.2 copy-done.7
  768.7 143.8 %final_exchange.1 = (bf16[4,2,320,1024]{3,2,1,0:T(8,128)(2,1)}, bf16[4,2,320,1024]{3,2,1,0:T(8,128)(2,1)}, bf16[4,2,512,640]{3,2,1,0:T(8,128)(2,1)}, bf16[2,8,40...) custom-call(bf16[320,1024]{1,0:T(8,128)(2,1)S(1)} %copy-done.5, ...), custom_call_target="tpu_custom_call" | custom-call | flops 10000000000 | bytes 31457280 | tf_op jit(solution)/shard_map/final_exchange/pallas_call | solution.py:716
  912.6 0.0 copy-start
  912.6 1.0 copy-done
  913.7 2.6 pad_maximum_fusion.6
  916.3 1.8 pad_maximum_fusion.5
  918.1 1.7 pad_maximum_fusion.4
  919.8 1.7 pad_maximum_fusion.3
  921.5 9.2 pad_maximum_fusion.2
  930.7 9.1 pad_maximum_fusion.1
  939.8 9.1 pad_maximum_fusion
  (37 shorter events, 0.2 us)
Async XLA Ops:
  8.0 3.2 copy-start.8
  9.6 2.1 copy-start.13
  21.3 248.1 %all-to-all-start.1 = ((bf16[16,128,640]{2,1,0:T(8,128)(2,1)}), bf16[16,128,640]{2,1,0:T(8,128)(2,1)}, u32[]{:S(2)}, u32[]{:S(2)}) async-start(bf16[16,128,640]{2,1,0:T(8,128)(2,1)} %bitcast.76), calls=%async_computation.1 | async-start | bytes 5242880 | tf_op jit(solution)/shard_map/all_to_all | solution.py:786
  29.6 48.4 %collective-permute-start = (bf16[320,1024]{1,0:T(8,128)(2,1)}, bf16[320,1024]{1,0:T(8,128)(2,1)}, u32[]{:S(2)}, u32[]{:S(2)}) collective-permute-start(bf16[320,1024]{1,0:T(8,128)(2,1)} %dynamic-slice_bitcast_fusion.2), channel_id=1, source_target_pairs={{0,16},{1,17},{2,18},{3,19},{4,20},{5,21},{6,22},{7,23},{8,24},{9,... | collective-permute-start | bytes 1966088 | tf_op jit(solution)/shard_map/ppermute | solution.py:769
  269.4 7.5 copy-start.12
  269.4 10.4 %copy-start.15 = (bf16[2,640,640]{2,1,0:T(8,128)(2,1)S(1)}, bf16[2,640,640]{2,1,0:T(8,128)(2,1)}, u32[]{:S(2)}) copy-start(bf16[2,640,640]{2,1,0:T(8,128)(2,1)} %param.15) | copy-start | bytes 4915204
  269.4 69.7 %all-to-all-start = ((bf16[16,128,640]{2,1,0:T(8,128)(2,1)}), bf16[16,128,640]{2,1,0:T(8,128)(2,1)}, u32[]{:S(2)}, u32[]{:S(2)}) async-start(bf16[16,128,640]{2,1,0:T(8,128)(2,1)} %bitcast.77), calls=%async_computation | async-start | bytes 5242880 | tf_op jit(solution)/shard_map/all_to_all | solution.py:786
  276.7 636.9 %all-reduce.4.cloned.1.call-start = ((), (), s32[]{:S(2)}) async-start(), calls=%async_computation.5 | async-start | bytes 9502720 | tf_op jit(solution)/shard_map/psum | solution.py:808
  276.8 48.4 %collective-permute-start.1 = (bf16[320,1024]{1,0:T(8,128)(2,1)S(1)}, bf16[320,1024]{1,0:T(8,128)(2,1)S(1)}, u32[]{:S(2)}, u32[]{:S(2)}) collective-permute-start(bf16[320,1024]{1,0:T(8,128)(2,1)S(1)} %dynamic-slice_bitcast_fusion.1), channel_id=1, source_target_pairs={{0,16},{1,17},{2,18},{3,19},{4,20},{5,21},{6,22},{7,23},{8,24},{9,... | collective-permute-start | bytes 1966088 | tf_op jit(solution)/shard_map/ppermute | solution.py:794
  276.9 62.2 %collective-permute-start.2 = (bf16[512,640]{1,0:T(8,128)(2,1)S(1)}, bf16[512,640]{1,0:T(8,128)(2,1)}, u32[]{:S(2)}, u32[]{:S(2)}) collective-permute-start(bf16[512,640]{1,0:T(8,128)(2,1)S(1)} %copy-done.12), channel_id=1, source_target_pairs={{0,16},{1,17},{2,18},{3,19},{4,20},{5,21},{6,22},{7,23},{8,24},{9,... | collective-permute-start | bytes 1966088 | tf_op jit(solution)/shard_map/ppermute | solution.py:794
  325.2 0.8 copy-start.17
  542.9 1.4 copy-start.16
  542.9 378.6 %all-gather.8.cloned.1.call-start = ((), (), s32[]{:S(2)}) async-start(), calls=%async_computation.4 | async-start | bytes 5898240 | tf_op jit(solution)/shard_map/all_gather | solution.py:802
  543.5 387.2 %all-gather.6.cloned.1.call-start = ((), (), s32[]{:S(2)}) async-start(), calls=%async_computation.3 | async-start | bytes 5898240 | tf_op jit(solution)/shard_map/all_gather | solution.py:802
  544.1 395.7 %all-gather.4.cloned.1.call-start = ((), (), s32[]{:S(2)}) async-start(), calls=%async_computation.2 | async-start | bytes 5898240 | tf_op jit(solution)/shard_map/all_gather | solution.py:802
  758.9 7.0 copy-start.14
  758.9 7.0 copy-start.18
  765.9 2.3 copy-start.2
  765.9 2.3 copy-start.3
  766.0 2.3 copy-start.4
  766.0 2.4 copy-start.5
  766.0 2.6 copy-start.6
  766.0 2.8 copy-start.7
  912.6 1.1 copy-start
  913.7 2.6 copy-start.1
  913.7 2.6 copy-start.11
  916.3 1.8 copy-start.10
  918.1 1.7 copy-start.9
Sparse Core Ops, SparseCore 0:
  543.0 328.3 all-reduce.3
Sparse Core Ops, SparseCore 1:
  545.3 110.2 all-gather.7
  657.4 81.5 all-gather.5
  740.6 52.5 all-gather.3

commit v8 on v7

--- a/solution.py
+++ b/solution.py
@@ -786,11 +786,12 @@
             return lax.all_to_all(blocks, ALL_AXES, 0, 0, axis_index_groups=groups)
 
         grads_two = extended(gated(grad_out, 1))
-        grads_first = go_out(take_rows(grads_two, owner[1].reshape(-1)).reshape(members, block, width))
-        mixed_one = mix(act_in, 0)
+        grads_two = [take_rows(grads_two, owner[part].reshape(-1)).reshape(members, block, width) for part in range(2)]
+        grads_first = go_out(grads_two[1])
+        mixed_one, grads_late = lax.optimization_barrier((mix(act_in, 0), grads_two[0]))
         recv, act_two, *foreign = forward_exchange(mesh, turned[0:1], gate_vals[0], mixed_one, experts, shared, got)
-        act_two, grads_two, halves_two = lax.optimization_barrier((act_two, grads_two, halves_two))
-        grads_second = go_out(take_rows(grads_two, owner[0].reshape(-1)).reshape(members, block, width))
+        act_two, grads_late, halves_two = lax.optimization_barrier((act_two, grads_late, halves_two))
+        grads_second = go_out(grads_late)
         got_two = [lax.ppermute(half, ALL_AXES, to_partner) for half in halves_two]
         mixed_two = mix(act_two, 1)
 

time: 968 us -> 956 us (0.988)
    pallas_call x2, Pallas kernels: 405 us -> 395 us  [backward_exchange(): pl.pallas_call(functools.partial(backward_kernel, ep, dp, layer), name='b...]
  transfers between devices with their start and end apart: 9 -> 9, of which waited for: 3 -> 3; matrix products, arithmetic and copies ran while one was open for 8% -> 7% of each run, Pallas kernels for 56% -> 57%
where the time goes in v8:
time: 956 us; the launch traced here: 946 us
  Pallas kernels  729 us (76%)
  waiting for transfers between devices  79.4 us (8%)
  other arithmetic  37 us (4%)
  matrix products  35.9 us (4%)
  local copies, waits for them, and re-layouts  27.8 us (3%)
  starting transfers between devices  19.7 us (2%)
  between operations  16.4 us (2%)
    pallas_call x2, Pallas kernels, backward_exchange(): pl.pallas_call(functools.partial(backward_kernel, ep, dp, layer), name='b...  395 us
    pallas_call x1, Pallas kernels, forward_exchange(): pl.pallas_call(functools.partial(forward_kernel, ep, dp), name='forward_e...  182 us
    pallas_call x1, Pallas kernels, final_exchange(): pl.pallas_call(functools.partial(final_kernel, ep, dp), name='final_excha...  152 us
    ppermute x2, waiting for transfers between devices, body(): got_two = [lax.ppermute(half, ALL_AXES, to_partner) for half in halves_two]  51.7 us
    another operation x3, other arithmetic, body(): expert_out = [jnp.stack(pair) for pair in zip(experts_one, experts_two)]  27.4 us
    ppermute x1, waiting for transfers between devices, body(): lax.ppermute(my_half(0, w), ALL_AXES, to_partner)  26.6 us
  transfers between devices with their start and end apart: 9, of which 3 were waited for; matrix products, arithmetic and copies ran while one was open for 7% of the time, Pallas kernels for 57%

profile of v8, /device:TPU:0, one launch (start us, length us, event | category | flops | bytes accessed | tf_op | source)
XLA Modules:
  0.0 945.6 jit_solution(2383564410285330631)
XLA Ops:
  8.0 0.0 copy-start.8
  8.1 0.9 and_select_fusion.2
  9.0 0.6 fusion.29
  9.6 0.1 pad.21.clone
  9.7 0.1 maximum_maximum_fusion
  9.8 0.1 broadcast_multiply_fusion
  9.9 0.4 fusion.1
  10.3 0.1 fusion.21
  10.3 0.7 fusion.28
  11.1 0.1 reshape.322
  11.2 0.5 multiply_convert_fusion.1
  11.7 0.0 copy-done.12
  11.7 0.2 pad.4
  11.9 9.3 gather_fusion.1
  21.3 6.4 all-to-all-start.1
  27.7 1.1 dynamic-slice_bitcast_fusion.2
  28.8 2.7 collective-permute-start
  31.4 0.1 reshape.314
  31.5 9.3 gather_fusion
  40.9 6.8 add_convert_fusion.3.mixed.refs_3_
  47.7 1.3 copy.21.gates
  49.0 1.1 dynamic-slice_bitcast_fusion.1
  50.1 1.2 dynamic-slice_bitcast_fusion
  51.3 26.6 %collective-permute-done.refs_6_ = bf16[320,1024]{1,0:T(8,128)(2,1)} collective-permute-done((bf16[320,1024]{1,0:T(8,128)(2,1)S(1)}, bf16[320,1024]{1,0:T(8,128)(2,1)}, u32[]{:S(2)}, u32[]{:S(2)}) %collective-permute-start) | collective-permute-done | bytes 655392 | tf_op jit(solution)/shard_map/ppermute | solution.py:769
  77.9 182.0 %forward_exchange.1 = (bf16[2,8,2,128,640]{4,3,2,1,0:T(8,128)(2,1)}, bf16[2048,640]{1,0:T(8,128)(2,1)}, bf16[640,1024]{1,0:T(8,128)(2,1)}, bf16[640,1024]{1,0:T(...) custom-call(s32[1,2048]{1,0:T(1,128)} %get-tuple-element.84.slots.refs_0_, f32[2048,1]{1,0:T(8,128)} %copy.21.gates, ...), custom_call_target="tpu_custom_call" | custom-call | flops 24159191040 | bytes 41943040 | tf_op jit(solution)/shard_map/forward_exchange/pallas_call | solution.py:317
  259.9 0.0 copy-start.14
  260.0 0.0 all-to-all-done.1.refs_2_
  260.0 7.5 all-to-all-start
  267.5 0.0 all-reduce.4.cloned.1.call-start
  267.5 0.1 collective-permute-start.1
  267.6 2.9 collective-permute-start.2
  270.5 6.5 add_convert_fusion.2.refs_3_.refs_4_
  277.0 38.6 %collective-permute-done.1.refs_10_ = bf16[320,1024]{1,0:T(8,128)(2,1)S(1)} collective-permute-done((bf16[320,1024]{1,0:T(8,128)(2,1)S(1)}, bf16[320,1024]{1,0:T(8,128)(2,1)S(1)}, u32[]{:S(2)}, u32[]{:S(2)}) %collective-permute-start.1) | collective-permute-done | bytes 655392 | tf_op jit(solution)/shard_map/ppermute | solution.py:795
  315.7 0.8 copy-done.16
  316.5 13.0 %collective-permute-done.2.refs_11_ = bf16[512,640]{1,0:T(8,128)(2,1)} collective-permute-done((bf16[512,640]{1,0:T(8,128)(2,1)S(1)}, bf16[512,640]{1,0:T(8,128)(2,1)}, u32[]{:S(2)}, u32[]{:S(2)}) %collective-permute-start.2) | collective-permute-done | bytes 655392 | tf_op jit(solution)/shard_map/ppermute | solution.py:795
  329.5 0.0 all-to-all-done.refs_1_
  329.5 189.7 %backward_second.1 = (bf16[2,16,128,640]{3,2,1,0:T(8,128)(2,1)}, bf16[2048,640]{1,0:T(8,128)(2,1)}, bf16[2,8,2,128,640]{4,3,2,1,0:T(8,128)(2,1)}, bf16[640,1024]...) custom-call(s32[1,2048]{1,0:T(1,128)} %copy-done.12, ...), custom_call_target="tpu_custom_call" | custom-call | flops 64424509440 | bytes 62914560 | tf_op jit(solution)/shard_map/backward_second/pallas_call | solution.py:573
  519.3 5.7 fusion
  524.9 0.0 all-reduce.4.cloned.1.call-update
  525.0 0.0 all-gather.8.cloned.1.call-start
  525.0 0.5 all-gather.8.cloned.1.call-update
  525.5 0.0 all-gather.6.cloned.1.call-start
  525.6 0.5 all-gather.6.cloned.1.call-update
  526.1 0.0 all-gather.4.cloned.1.call-start
  526.2 0.2 copy-done.15
  526.4 7.4 multiply_convert_fusion
  533.7 0.0 all-gather.4.cloned.1.call-update
  533.8 205.5 %backward_first.1 = (bf16[2,16,128,640]{3,2,1,0:T(8,128)(2,1)}, bf16[2048,640]{1,0:T(8,128)(2,1)}, bf16[2,8,2,128,640]{4,3,2,1,0:T(8,128)(2,1)}, bf16[640,1024]{...) custom-call(s32[1,2048]{1,0:T(1,128)} %get-tuple-element.84.slots.re, ...), custom_call_target="tpu_custom_call" | custom-call | flops 64424509440 | bytes 62914560 | tf_op jit(solution)/shard_map/backward_first/pallas_call | solution.py:573
  739.3 0.0 copy-start.13
  739.3 6.9 add_convert_fusion
  746.3 0.0 copy-done.17
  746.4 2.2 convolution_convert_fusion.1
  748.6 0.2 copy-done.6
  748.8 0.2 copy-done.7
  749.0 152.2 %final_exchange.1 = (bf16[4,2,320,1024]{3,2,1,0:T(8,128)(2,1)}, bf16[4,2,320,1024]{3,2,1,0:T(8,128)(2,1)}, bf16[4,2,512,640]{3,2,1,0:T(8,128)(2,1)}, bf16[2,8,40...) custom-call(bf16[320,1024]{1,0:T(8,128)(2,1)S(1)} %copy-done.5, ...), custom_call_target="tpu_custom_call" | custom-call | flops 10000000000 | bytes 31457280 | tf_op jit(solution)/shard_map/final_exchange/pallas_call | solution.py:716
  901.2 0.0 copy-start
  901.3 1.0 copy-done
  902.3 2.6 pad_maximum_fusion.6
  905.0 1.8 pad_maximum_fusion.5
  906.7 1.7 pad_maximum_fusion.4
  908.4 1.7 pad_maximum_fusion.3
  910.2 9.2 pad_maximum_fusion.2
  919.4 9.1 pad_maximum_fusion.1
  928.5 9.1 pad_maximum_fusion
  (35 shorter events, 0.2 us)
Async XLA Ops:
  8.0 3.2 copy-start.8
  9.6 2.1 copy-start.12
  21.3 238.7 %all-to-all-start.1 = ((bf16[16,128,640]{2,1,0:T(8,128)(2,1)}), bf16[16,128,640]{2,1,0:T(8,128)(2,1)}, u32[]{:S(2)}, u32[]{:S(2)}) async-start(bf16[16,128,640]{2,1,0:T(8,128)(2,1)} %bitcast.76), calls=%async_computation.1 | async-start | bytes 5242880 | tf_op jit(solution)/shard_map/all_to_all | solution.py:786
  28.8 49.2 %collective-permute-start = (bf16[320,1024]{1,0:T(8,128)(2,1)S(1)}, bf16[320,1024]{1,0:T(8,128)(2,1)}, u32[]{:S(2)}, u32[]{:S(2)}) collective-permute-start(bf16[320,1024]{1,0:T(8,128)(2,1)S(1)} %dynamic-slice_bitcast_fusion.2), channel_id=1, source_target_pairs={{0,16},{1,17},{2,18},{3,19},{4,20},{5,21},{6,22},{7,23},{8,24},{9,... | collective-permute-start | bytes 1966088 | tf_op jit(solution)/shard_map/ppermute | solution.py:769
  259.9 10.6 %copy-start.14 = (bf16[2,640,640]{2,1,0:T(8,128)(2,1)S(1)}, bf16[2,640,640]{2,1,0:T(8,128)(2,1)}, u32[]{:S(2)}) copy-start(bf16[2,640,640]{2,1,0:T(8,128)(2,1)} %param.15) | copy-start | bytes 4915204
  260.0 69.6 %all-to-all-start = ((bf16[16,128,640]{2,1,0:T(8,128)(2,1)}), bf16[16,128,640]{2,1,0:T(8,128)(2,1)}, u32[]{:S(2)}, u32[]{:S(2)}) async-start(bf16[16,128,640]{2,1,0:T(8,128)(2,1)} %bitcast.8), calls=%async_computation | async-start | bytes 5242880 | tf_op jit(solution)/shard_map/all_to_all | solution.py:786
  267.5 634.8 %all-reduce.4.cloned.1.call-start = ((), (), s32[]{:S(2)}) async-start(), calls=%async_computation.5 | async-start | bytes 9502720 | tf_op jit(solution)/shard_map/psum | solution.py:809
  267.5 48.1 %collective-permute-start.1 = (bf16[320,1024]{1,0:T(8,128)(2,1)S(1)}, bf16[320,1024]{1,0:T(8,128)(2,1)S(1)}, u32[]{:S(2)}, u32[]{:S(2)}) collective-permute-start(bf16[320,1024]{1,0:T(8,128)(2,1)S(1)} %dynamic-slice_bitcast_fusion.1), channel_id=1, source_target_pairs={{0,16},{1,17},{2,18},{3,19},{4,20},{5,21},{6,22},{7,23},{8,24},{9,... | collective-permute-start | bytes 1966088 | tf_op jit(solution)/shard_map/ppermute | solution.py:795
  267.6 61.9 %collective-permute-start.2 = (bf16[512,640]{1,0:T(8,128)(2,1)S(1)}, bf16[512,640]{1,0:T(8,128)(2,1)}, u32[]{:S(2)}, u32[]{:S(2)}) collective-permute-start(bf16[512,640]{1,0:T(8,128)(2,1)S(1)} %dynamic-slice_bitcast_fusion), channel_id=1, source_target_pairs={{0,16},{1,17},{2,18},{3,19},{4,20},{5,21},{6,22},{7,23},{8,24},{9,... | collective-permute-start | bytes 1966088 | tf_op jit(solution)/shard_map/ppermute | solution.py:795
  315.7 0.8 copy-start.16
  524.9 1.4 copy-start.15
  525.0 385.2 %all-gather.8.cloned.1.call-start = ((), (), s32[]{:S(2)}) async-start(), calls=%async_computation.4 | async-start | bytes 5898240 | tf_op jit(solution)/shard_map/all_gather | solution.py:803
  525.5 393.9 %all-gather.6.cloned.1.call-start = ((), (), s32[]{:S(2)}) async-start(), calls=%async_computation.3 | async-start | bytes 5898240 | tf_op jit(solution)/shard_map/all_gather | solution.py:803
  526.1 402.4 %all-gather.4.cloned.1.call-start = ((), (), s32[]{:S(2)}) async-start(), calls=%async_computation.2 | async-start | bytes 5898240 | tf_op jit(solution)/shard_map/all_gather | solution.py:803
  739.3 7.0 copy-start.13
  739.3 7.0 copy-start.17
  746.3 2.3 copy-start.2
  746.3 2.3 copy-start.3
  746.3 2.3 copy-start.4
  746.3 2.3 copy-start.5
  746.3 2.5 copy-start.6
  746.3 2.7 copy-start.7
  901.2 1.1 copy-start
  902.3 2.6 copy-start.1
  902.3 2.6 copy-start.11
  904.9 1.8 copy-start.10
  906.7 1.7 copy-start.9
Sparse Core Ops, SparseCore 0:
  525.1 356.1 all-reduce.3
Sparse Core Ops, SparseCore 1:
  527.3 108.3 all-gather.7
  637.5 94.0 all-gather.5
  733.3 73.6 all-gather.3
